TPU v7x, 512 devices: a whole 4x4x16 slice. The times are simulated.
512 devices in a mesh: tgt: 16 (over y, x), src: 32 (over z, core).
Axes of the slice: x: 4, y: 4, z: 16, core: 2. Of those that a mesh axis runs over, the one named last changes fastest.
Arguments:
- positions: float32 [3, 262144], P(None, ('tgt', 'src')), may hold values from -1 to 1
- velocities: float32 [3, 262144], P(None, ('tgt', 'src')), may hold values from -3 to 3
- accels: float32 [3, 262144], P(None, ('tgt', 'src')), may hold values from -6 to 6
- jerks: float32 [3, 262144], P(None, ('tgt', 'src')), may hold values from -12 to 12
- masses: float32 [262144], P(('tgt', 'src')), may hold values from 0.2 to 5
- levels: int32 [262144], P(('tgt', 'src')), may hold values from 0 to 3
- active_first: int32 [4096], P('tgt'), may hold values from -1 to 262143, as said below
- active_second: int32 [2048], P('tgt'), may hold values from -1 to 262143, as said below
Outputs:
- new_positions: float32 [3, 262144], P(None, ('tgt', 'src'))
- new_velocities: float32 [3, 262144], P(None, ('tgt', 'src'))
- new_accels: float32 [3, 262144], P(None, ('tgt', 'src'))
- new_jerks: float32 [3, 262144], P(None, ('tgt', 'src'))
Inputs may be any that keep to these rules, and one draw needn't show every extreme that they name: Target group g owns slots g * 256 to (g + 1) * 256 - 1. In each group the star numbers come first and -1 fills the remaining slots; no star is named twice anywhere in active_first; every group names at least one star, and some group names 256. Target group g owns slots g * 128 to (g + 1) * 128 - 1. In each group the star numbers come first and -1 fills the remaining slots; no star is named twice anywhere in active_second; every group names at least one star, and some group names 128. Stars may also appear in active_first.
All inputs are finite; a program needn't handle non-finite values.
Results may differ from a plain program's by a relative error of at most 0.0003.
Values sent between devices are 32-bit elements; how exact they have to be, the bound alone decides.
No kernel may reach another device: no remote copies, remote signals or barrier semaphores. Data moves between devices by JAX's collectives and lax.ppermute only.
A program may use at most 64 MiB of HBM per device.

v0:
```python
import jax
import jax.numpy as jnp
from jax import lax
from jax.sharding import PartitionSpec as P

TILE = 128
LEVELS = 4


SOFTENING_SQ = 0.0001
BASE_STEP = 0.5


def sent_to_all(shard, axis):
    copies = jnp.broadcast_to(shard, (lax.axis_size(axis), *shard.shape))
    return lax.all_to_all(copies, axis, split_axis=0, concat_axis=0, tiled=True)


def laid_out(tiles, dim):
    dims = list(tiles.shape[1:])
    dims[dim] *= tiles.shape[0]
    return jnp.moveaxis(tiles, 0, dim).reshape(dims)


def gathered_copies(shard, axis, dim):
    tiles = sent_to_all(shard, axis)
    return laid_out(tiles, dim)


def over_pieces(shard, axis):
    return lax.all_gather(shard, axis).sum(0)


def taken_together(shard, axis):
    return sent_to_all(shard, axis).sum(axis=0)


def predict(states, span):
    ahead_pos = states[0:3] + span * (
        states[3:6] + span * (states[6:9] * 0.5 + span * states[9:12] / 6.0)
    )
    moving = states[3:6] + span * (states[6:9] + span * states[9:12] * 0.5)
    return (ahead_pos, moving)


def pair_block(tile_place, tile_speed, tile_ident, sources, source_ident):
    offset = sources[0:3, None, :] - tile_place[:, :, None]
    motion = sources[3:6, None, :] - tile_speed[:, :, None]
    dist_sq = jnp.sum(offset * offset, axis=0) + SOFTENING_SQ
    inverse = lax.rsqrt(dist_sq)
    inverse_sq = inverse * inverse
    weight3 = jnp.where(
        source_ident[None, :] == tile_ident[:, None],
        0.0,
        sources[6][None, :] * inverse_sq * inverse,
    )
    closing = jnp.sum(offset * motion, axis=0)
    attract = jnp.sum(offset * weight3, axis=2)
    change = jnp.sum(motion * weight3 - 3.0 * (closing * inverse_sq * weight3) * offset, axis=2)
    return jnp.concatenate([attract, change], axis=0)


def correct(ahead_pos, moving, old_accel, old_jolt, span, forces):
    new_acc = forces[0:3]
    new_jolt = forces[3:6]
    second_term = -6.0 * (old_accel - new_acc) - span * (4.0 * old_jolt + 2.0 * new_jolt)
    third_term = 12.0 * (old_accel - new_acc) + 6.0 * span * (old_jolt + new_jolt)
    new_place = ahead_pos + span * span * (second_term / 24.0 + third_term / 120.0)
    new_speed = moving + span * (second_term / 6.0 + third_term / 24.0)
    return jnp.concatenate([new_place, new_speed, new_acc, new_jolt], axis=0)


def tile_forces(held, tgt_ahead, tgt_moving, slot_ids, tiles_used, shard_part, idents):
    length = shard_part.shape[1]
    block_len = length
    while block_len > 2048 and block_len % 2 == 0:
        block_len = block_len // 2
    block_count = length // block_len
    src_blocks = shard_part.reshape(7, block_count, block_len).transpose(1, 0, 2)
    ident_blocks = idents.reshape(block_count, block_len)

    def one_tile(tile_no, carried):
        place_tile = lax.dynamic_slice_in_dim(tgt_ahead, tile_no * TILE, TILE, 1)
        speed_tile = lax.dynamic_slice_in_dim(tgt_moving, tile_no * TILE, TILE, 1)
        ident_tile = lax.dynamic_slice_in_dim(slot_ids, tile_no * TILE, TILE, 0)

        def add_block(running, source_pair):
            return (
                running
                + pair_block(place_tile, speed_tile, ident_tile, source_pair[0], source_pair[1]),
                None,
            )

        running, _ = lax.scan(
            add_block, jnp.zeros((6, TILE), jnp.float32), (src_blocks, ident_blocks)
        )
        before = lax.dynamic_slice_in_dim(carried, tile_no * TILE, TILE, 1)
        return lax.dynamic_update_slice_in_dim(carried, before + running, tile_no * TILE, 1)

    return lax.fori_loop(0, tiles_used, one_tile, held)


def advance(states, last_time, weights, active, now_time, s_dev, n_tgt, n_src, my_row, my_column):
    slot_count = active.shape[0]
    own_first = (my_row * n_src + my_column) * s_dev
    listed = gathered_copies(active, "tgt", 0)
    span_all = now_time - last_time
    my_slots = lax.dynamic_slice_in_dim(listed, my_row * slot_count, slot_count, 0)
    filled = jnp.sum((my_slots >= 0).astype(jnp.int32))
    tiles_used = (filled + TILE - 1) // TILE
    local_at = listed - own_first
    is_owned = (listed >= 0) & (local_at >= 0) & (local_at < s_dev)
    stacked = jnp.concatenate([states, span_all[None, :], weights[None, :]], axis=0)
    column_all = gathered_copies(stacked, "tgt", 1)
    owner_col = my_slots // s_dev % n_src
    places = my_slots // (s_dev * n_src) * s_dev + my_slots % s_dev
    mine_owned = (my_slots >= 0) & (owner_col == my_column)
    chosen = jnp.take(column_all[0:13], jnp.clip(places, 0, n_tgt * s_dev - 1), axis=1)
    partial_rows = jnp.where(mine_owned[None, :], chosen, 0.0)
    ahead_pos, moving = predict(column_all[0:12], column_all[12:13])
    sources = jnp.concatenate([ahead_pos, moving, column_all[13:14]], axis=0)
    target = over_pieces(partial_rows, "src")
    tgt_ahead, tgt_moving = predict(target[0:12], target[12:13])
    zero_forces = jnp.zeros((6, slot_count), jnp.float32)
    columns = jnp.arange(sources.shape[1], dtype=jnp.int32)
    idents = columns // s_dev * (s_dev * n_src) + my_column * s_dev + columns % s_dev
    partial_forces = tile_forces(
        zero_forces, tgt_ahead, tgt_moving, my_slots, tiles_used, sources, idents
    )
    forces = taken_together(partial_forces, "src")
    corrected = correct(tgt_ahead, tgt_moving, target[6:9], target[9:12], target[12:13], forces)
    returned = gathered_copies(corrected, "tgt", 1)
    write_at = jnp.where(is_owned, local_at, s_dev)
    states = states.at[:, write_at].set(returned, mode="drop")
    last_time = last_time.at[write_at].set(now_time, mode="drop")
    return (states, last_time)


def shards(positions, velocities, accels, jerks, masses, levels, active_first, active_second):
    s_dev = positions.shape[1]
    n_tgt = lax.axis_size("tgt")
    n_src = lax.axis_size("src")
    my_row = lax.axis_index("tgt")
    my_column = lax.axis_index("src")
    weights = masses / (s_dev * n_tgt * n_src)
    states = jnp.concatenate([positions, velocities, accels, jerks], axis=0)
    last_time = -BASE_STEP * jnp.exp2(-levels.astype(jnp.float32))
    for now_time, active in ((0.0, active_first), (BASE_STEP / (1 << LEVELS), active_second)):
        states, last_time = advance(
            states, last_time, weights, active, now_time, s_dev, n_tgt, n_src, my_row, my_column
        )
    return (states[0:3], states[3:6], states[6:9], states[9:12])


def solution(mesh):
    return jax.shard_map(
        shards,
        mesh=mesh,
        in_specs=(
            P(None, ("tgt", "src")),
            P(None, ("tgt", "src")),
            P(None, ("tgt", "src")),
            P(None, ("tgt", "src")),
            P(("tgt", "src")),
            P(("tgt", "src")),
            P("tgt"),
            P("tgt"),
        ),
        out_specs=(
            P(None, ("tgt", "src")),
            P(None, ("tgt", "src")),
            P(None, ("tgt", "src")),
            P(None, ("tgt", "src")),
        ),
        check_vma=False,
    )
```

profile of v0, /device:TPU:2, one launch (start us, length us, event | category | flops | bytes accessed | tf_op | source)
XLA Modules:
  0.0 269.7 jit_solution(1272249492909889296)
XLA Ops:
  0.6 1.3 broadcast_in_dim.134
  1.9 9.1 %all-to-all-start.4 = ((s32[16,1,128]{2,1,0:T(1,128)}), s32[16,1,128]{2,1,0:T(1,128)S(1)}, u32[]{:S(2)}, u32[]{:S(2)}) async-start(s32[16,1,128]{2,1,0:T(1,128)} %broadcast_in_dim.134), calls=%async_computation.4 | async-start | bytes 16384 | tf_op jit(solution)/shard_map/all_to_all | solution.py:16
  13.3 2.3 concatenate.37
  15.6 1.7 all-to-all-done.4
  17.2 1.3 broadcast_in_dim.122
  18.5 5.6 %all-to-all-start = ((s32[16,1,256]{2,1,0:T(1,128)}), s32[16,1,256]{2,1,0:T(1,128)S(1)}, u32[]{:S(2)}, u32[]{:S(2)}) async-start(s32[16,1,256]{2,1,0:T(1,128)} %broadcast_in_dim.122), calls=%async_computation | async-start | bytes 32768 | tf_op jit(solution)/shard_map/all_to_all | solution.py:16
  24.2 6.1 %all-to-all-done = s32[16,1,256]{2,1,0:T(1,128)S(1)} async-done(((s32[16,1,256]{2,1,0:T(1,128)}), s32[16,1,256]{2,1,0:T(1,128)S(1)}, u32[]{:S(2)}, u32[]{:S(2)}) %all-to-all-start) | async-done | bytes 16416 | tf_op jit(solution)/shard_map/all_to_all | solution.py:16
  31.2 4.8 %all-to-all-start.1 = ((f32[16,14,512]{2,1,0:T(8,128)}), f32[16,14,512]{2,1,0:T(8,128)S(1)}, u32[]{:S(2)}, u32[]{:S(2)}) async-start(f32[16,14,512]{2,1,0:T(8,128)} %broadcast_in_dim.127), calls=%async_computation.1 | async-start | bytes 1048576 | tf_op jit(solution)/shard_map/all_to_all | solution.py:16
  37.5 7.4 %all-to-all-done.1 = f32[16,14,512]{2,1,0:T(8,128)S(1)} async-done(((f32[16,14,512]{2,1,0:T(8,128)}), f32[16,14,512]{2,1,0:T(8,128)S(1)}, u32[]{:S(2)}, u32[]{:S(2)}) %all-to-all-start.1) | async-done | bytes 458784 | tf_op jit(solution)/shard_map/all_to_all | solution.py:16
  45.2 2.6 copy.235
  47.8 2.9 %gather_fusion = f32[256,13]{1,0:T(8,128)S(1)} fusion(f32[13,8192]{0,1:T(8,128)} %bitcast.91, s32[1024]{0:T(1024)S(1)} %pad_clamp_fusion.1), kind=kCustom, calls=%fused_computation | custom fusion | bytes 27648 | tf_op jit(solution)/shard_map/jit(_take)/gather | solution.py:118
  50.9 35.9 %all_gather.8 = f32[32,13,256]{2,1,0:T(8,128)S(1)} all-gather(f32[1,13,256]{2,1,0:T(8,128)S(1)} %copy.236), channel_id=1, replica_groups=mesh['tgt'=16,'src'=32] {'src'}, dimensions={0}, use_global_device_ids=true | all-gather | bytes 439296 | tf_op jit(solution)/shard_map/all_gather | solution.py:31
  87.7 10.5 %while.47 = (s32[]{:T(128)}, f32[6,256]{1,0:T(8,128)S(1)}, s32[]{:T(128)}, f32[3,256]{1,0:T(4,128)S(1)}, f32[3,256]{1,0:T(4,128)S(1)}, /*index=5*/s32[256]{0:T(2...) while((s32[]{:T(128)}, f32[6,256]{1,0:T(8,128)S(1)}, ...), condition=%wide.region_9.10_spmd.clone, body=%wide.region_2.9_spmd.clone.sunk | while | flops 13043979 | bytes 8706006 | solution.py:100
  88.0 10.3 %while.50 = (s32[]{:T(128)}, f32[6,128]{1,0:T(8,128)S(1)}, f32[4,7,2048]{2,1,0:T(8,128)S(1)}, f32[3,128]{1,0:T(4,128)S(1)}, s32[4,2048]{1,0:T(4,128)S(1)}, /*ind...) while((s32[]{:T(128)}, f32[6,128]{1,0:T(8,128)S(1)}, ...), condition=%wide.region_8.8_spmd.clone, body=%wide.region_3.7_spmd.clone.sunk | while | flops 12846597 | bytes 8653475 | solution.py:94
  99.0 7.0 %all-to-all-start.2 = ((f32[32,6,256]{2,1,0:T(8,128)}), f32[32,6,256]{2,1,0:T(8,128)S(1)}, u32[]{:S(2)}, u32[]{:S(2)}) async-start(f32[32,6,256]{2,1,0:T(8,128)} %broadcast_in_dim.132), calls=%async_computation.2 | async-start | bytes 524288 | tf_op jit(solution)/shard_map/all_to_all | solution.py:16
  106.1 15.5 %scatter_fusion.1 = f32[512]{0:T(512)S(1)} fusion(f32[512]{0:T(512)S(1)} %get-tuple-element.538, s32[4096]{0:T(1024)S(1)} %bitcast.101, f32[4096]{0:T(1024)S(1)} %broadcast.604), kind=kCustom, calls=%fused_computation.3 | custom fusion | bytes 65536 | tf_op jit(solution)/shard_map/scatter | solution.py:135
  121.9 6.8 %all-to-all-done.2 = f32[32,6,256]{2,1,0:T(8,128)S(1)} async-done(((f32[32,6,256]{2,1,0:T(8,128)}), f32[32,6,256]{2,1,0:T(8,128)S(1)}, u32[]{:S(2)}, u32[]{:S(2)}) %all-to-all-start.2) | async-done | bytes 196640 | tf_op jit(solution)/shard_map/all_to_all | solution.py:16
  129.5 15.1 %all-to-all-start.3 = ((f32[16,12,256]{2,1,0:T(8,128)}), f32[16,12,256]{2,1,0:T(8,128)S(1)}, u32[]{:S(2)}, u32[]{:S(2)}) async-start(f32[16,12,256]{2,1,0:T(8,128)} %broadcast_in_dim.133), calls=%async_computation.3 | async-start | bytes 524288 | tf_op jit(solution)/shard_map/all_to_all | solution.py:16
  144.5 7.3 %all-to-all-done.3 = f32[16,12,256]{2,1,0:T(8,128)S(1)} async-done(((f32[16,12,256]{2,1,0:T(8,128)}), f32[16,12,256]{2,1,0:T(8,128)S(1)}, u32[]{:S(2)}, u32[]{:S(2)}) %all-to-all-start.3) | async-done | bytes 196640 | tf_op jit(solution)/shard_map/all_to_all | solution.py:16
  152.8 10.7 %scatter_fusion = f32[12,512]{0,1:T(8,128)S(1)} fusion(f32[12,512]{0,1:T(8,128)S(1)} %copy.249, s32[4096]{0:T(1024)S(1)} %bitcast.102, f32[4096,12]{1,0:T(8,128)S(1)} %copy.250), kind=kCustom, calls=%fused_computation.2 | custom fusion | bytes 606208 | tf_op jit(solution)/shard_map/scatter | solution.py:134
  164.6 4.8 %all-to-all-start.5 = ((f32[16,14,512]{2,1,0:T(8,128)}), f32[16,14,512]{2,1,0:T(8,128)S(1)}, u32[]{:S(2)}, u32[]{:S(2)}) async-start(f32[16,14,512]{2,1,0:T(8,128)} %broadcast_in_dim.139), calls=%async_computation.5 | async-start | bytes 1048576 | tf_op jit(solution)/shard_map/all_to_all | solution.py:16
  170.7 7.8 %all-to-all-done.5 = f32[16,14,512]{2,1,0:T(8,128)S(1)} async-done(((f32[16,14,512]{2,1,0:T(8,128)}), f32[16,14,512]{2,1,0:T(8,128)S(1)}, u32[]{:S(2)}, u32[]{:S(2)}) %all-to-all-start.5) | async-done | bytes 458784 | tf_op jit(solution)/shard_map/all_to_all | solution.py:16
  178.8 2.6 copy.252
  181.5 2.8 %gather_fusion.1 = f32[128,13]{1,0:T(8,128)S(1)} fusion(f32[13,8192]{0,1:T(8,128)} %bitcast.92, s32[1024]{0:T(1024)S(1)} %pad_clamp_fusion), kind=kCustom, calls=%fused_computation.1 | custom fusion | bytes 13824 | tf_op jit(solution)/shard_map/jit(_take)/gather | solution.py:118
  184.5 27.7 %all_gather.9 = f32[32,13,128]{2,1,0:T(8,128)S(1)} all-gather(f32[1,13,128]{2,1,0:T(8,128)S(1)} %copy.253), channel_id=1, replica_groups=mesh['tgt'=16,'src'=32] {'src'}, dimensions={0}, use_global_device_ids=true | all-gather | bytes 219648 | tf_op jit(solution)/shard_map/all_gather | solution.py:31
  213.0 10.6 %while.49 = (s32[]{:T(128)}, f32[6,128]{1,0:T(8,128)S(1)}, s32[]{:T(128)}, f32[4,7,2048]{2,1,0:T(8,128)S(1)}, f32[3,128]{1,0:T(4,128)S(1)}, /*index=5*/s32[128]{...) while((s32[]{:T(128)}, f32[6,128]{1,0:T(8,128)S(1)}, ...), condition=%wide.region_22.23_spmd.clone, body=%wide.region_15.22_spmd.clone.sunk | while | flops 13043975 | bytes 8695692 | solution.py:100
  213.1 10.5 %while.51 = (s32[]{:T(128)}, f32[6,128]{1,0:T(8,128)S(1)}, f32[4,7,2048]{2,1,0:T(8,128)S(1)}, f32[3,128]{1,0:T(4,128)S(1)}, s32[4,2048]{1,0:T(4,128)S(1)}, /*ind...) while((s32[]{:T(128)}, f32[6,128]{1,0:T(8,128)S(1)}, ...), condition=%wide.region_21.21_spmd.clone, body=%wide.region_16.20_spmd.clone.sunk | while | flops 12846597 | bytes 8653475 | solution.py:94
  224.3 6.7 %all-to-all-start.6 = ((f32[32,6,128]{2,1,0:T(8,128)}), f32[32,6,128]{2,1,0:T(8,128)S(1)}, u32[]{:S(2)}, u32[]{:S(2)}) async-start(f32[32,6,128]{2,1,0:T(8,128)} %broadcast_in_dim.143), calls=%async_computation.6 | async-start | bytes 262144 | tf_op jit(solution)/shard_map/all_to_all | solution.py:16
  231.2 17.0 %all-to-all-done.6 = f32[32,6,128]{2,1,0:T(8,128)S(1)} async-done(((f32[32,6,128]{2,1,0:T(8,128)}), f32[32,6,128]{2,1,0:T(8,128)S(1)}, u32[]{:S(2)}, u32[]{:S(2)}) %all-to-all-start.6) | async-done | bytes 98336 | tf_op jit(solution)/shard_map/all_to_all | solution.py:16
  248.9 4.8 %all-to-all-start.7 = ((f32[16,12,128]{2,1,0:T(8,128)}), f32[16,12,128]{2,1,0:T(8,128)S(1)}, u32[]{:S(2)}, u32[]{:S(2)}) async-start(f32[16,12,128]{2,1,0:T(8,128)} %broadcast_in_dim.144), calls=%async_computation.7 | async-start | bytes 262144 | tf_op jit(solution)/shard_map/all_to_all | solution.py:16
  253.7 6.7 %all-to-all-done.7 = f32[16,12,128]{2,1,0:T(8,128)S(1)} async-done(((f32[16,12,128]{2,1,0:T(8,128)}), f32[16,12,128]{2,1,0:T(8,128)S(1)}, u32[]{:S(2)}, u32[]{:S(2)}) %all-to-all-start.7) | async-done | bytes 98336 | tf_op jit(solution)/shard_map/all_to_all | solution.py:16
  260.8 5.7 %scatter_fusion.2 = f32[12,512]{0,1:T(8,128)S(1)} fusion(f32[12,512]{0,1:T(8,128)S(1)} %scatter_fusion, s32[2048]{0:T(1024)S(1)} %bitcast.106, f32[2048,12]{1,0:T(8,128)S(1)} %copy.266), kind=kCustom, calls=%fused_computation.4 | custom fusion | bytes 303104 | tf_op jit(solution)/shard_map/scatter | solution.py:134
  (157 shorter events, 36.6 us)
Async XLA Ops:
  1.9 15.3 %all-to-all-start.4 = ((s32[16,1,128]{2,1,0:T(1,128)}), s32[16,1,128]{2,1,0:T(1,128)S(1)}, u32[]{:S(2)}, u32[]{:S(2)}) async-start(s32[16,1,128]{2,1,0:T(1,128)} %broadcast_in_dim.134), calls=%async_computation.4 | async-start | bytes 16384 | tf_op jit(solution)/shard_map/all_to_all | solution.py:16
  18.5 11.9 %all-to-all-start = ((s32[16,1,256]{2,1,0:T(1,128)}), s32[16,1,256]{2,1,0:T(1,128)S(1)}, u32[]{:S(2)}, u32[]{:S(2)}) async-start(s32[16,1,256]{2,1,0:T(1,128)} %broadcast_in_dim.122), calls=%async_computation | async-start | bytes 32768 | tf_op jit(solution)/shard_map/all_to_all | solution.py:16
  31.2 13.7 %all-to-all-start.1 = ((f32[16,14,512]{2,1,0:T(8,128)}), f32[16,14,512]{2,1,0:T(8,128)S(1)}, u32[]{:S(2)}, u32[]{:S(2)}) async-start(f32[16,14,512]{2,1,0:T(8,128)} %broadcast_in_dim.127), calls=%async_computation.1 | async-start | bytes 1048576 | tf_op jit(solution)/shard_map/all_to_all | solution.py:16
  99.0 29.7 %all-to-all-start.2 = ((f32[32,6,256]{2,1,0:T(8,128)}), f32[32,6,256]{2,1,0:T(8,128)S(1)}, u32[]{:S(2)}, u32[]{:S(2)}) async-start(f32[32,6,256]{2,1,0:T(8,128)} %broadcast_in_dim.132), calls=%async_computation.2 | async-start | bytes 524288 | tf_op jit(solution)/shard_map/all_to_all | solution.py:16
  129.5 22.4 %all-to-all-start.3 = ((f32[16,12,256]{2,1,0:T(8,128)}), f32[16,12,256]{2,1,0:T(8,128)S(1)}, u32[]{:S(2)}, u32[]{:S(2)}) async-start(f32[16,12,256]{2,1,0:T(8,128)} %broadcast_in_dim.133), calls=%async_computation.3 | async-start | bytes 524288 | tf_op jit(solution)/shard_map/all_to_all | solution.py:16
  164.6 14.0 %all-to-all-start.5 = ((f32[16,14,512]{2,1,0:T(8,128)}), f32[16,14,512]{2,1,0:T(8,128)S(1)}, u32[]{:S(2)}, u32[]{:S(2)}) async-start(f32[16,14,512]{2,1,0:T(8,128)} %broadcast_in_dim.139), calls=%async_computation.5 | async-start | bytes 1048576 | tf_op jit(solution)/shard_map/all_to_all | solution.py:16
  224.3 23.9 %all-to-all-start.6 = ((f32[32,6,128]{2,1,0:T(8,128)}), f32[32,6,128]{2,1,0:T(8,128)S(1)}, u32[]{:S(2)}, u32[]{:S(2)}) async-start(f32[32,6,128]{2,1,0:T(8,128)} %broadcast_in_dim.143), calls=%async_computation.6 | async-start | bytes 262144 | tf_op jit(solution)/shard_map/all_to_all | solution.py:16
  248.9 11.5 %all-to-all-start.7 = ((f32[16,12,128]{2,1,0:T(8,128)}), f32[16,12,128]{2,1,0:T(8,128)S(1)}, u32[]{:S(2)}, u32[]{:S(2)}) async-start(f32[16,12,128]{2,1,0:T(8,128)} %broadcast_in_dim.144), calls=%async_computation.7 | async-start | bytes 262144 | tf_op jit(solution)/shard_map/all_to_all | solution.py:16
where the time goes:
time: 271 us; the launch traced here: 270 us
  blocking collectives  63.6 us (23%)
  waiting for transfers between devices  60.8 us (22%)
  local copies, waits for them, and re-layouts  59.6 us (22%)
  starting transfers between devices  57.9 us (21%)
  other arithmetic  24.8 us (9%)
    all_gather x2, blocking collectives, over_pieces(): return lax.all_gather(shard, axis).sum(0)  63.6 us
    all_to_all x8, waiting for transfers between devices, sent_to_all(): return lax.all_to_all(copies, axis, split_axis=0, concat_axis=0, tiled=True)  60.8 us
    all_to_all x8, starting transfers between devices, sent_to_all(): return lax.all_to_all(copies, axis, split_axis=0, concat_axis=0, tiled=True)  57.9 us
    scatter x3, local copies, waits for them, and re-layouts, advance(): states = states.at[:, write_at].set(returned, mode='drop')  16.6 us
    scatter x1, local copies, waits for them, and re-layouts, advance(): last_time = last_time.at[write_at].set(now_time, mode='drop')  15.5 us
    reduce_sum x8, other arithmetic, pair_block(): attract = jnp.sum(offset * weight3, axis=2)  9.5 us
    broadcast_in_dim x8, local copies, waits for them, and re-layouts, sent_to_all(): copies = jnp.broadcast_to(shard, (lax.axis_size(axis), *shard.shape))  6.96 us
    reduce_sum x8, other arithmetic, pair_block(): dist_sq = jnp.sum(offset * offset, axis=0) + SOFTENING_SQ  6.81 us
  transfers between devices with their start and end apart: 8, of which 8 were waited for; matrix products, arithmetic and copies ran while one was open for 8% of the time, Pallas kernels for 0%

commit v1 on v0

--- a/solution.py
+++ b/solution.py
@@ -1,14 +1,22 @@
 import jax
 import jax.numpy as jnp
 from jax import lax
+from jax.experimental import pallas as pl
+from jax.experimental.pallas import tpu as pltpu
+from jax.sharding import Mesh
 from jax.sharding import PartitionSpec as P
 
 TILE = 128
 LEVELS = 4
-
+LANES = 128
+FIRST_ROOM = 256
+SECOND_ROOM = 128
 
 SOFTENING_SQ = 0.0001
 BASE_STEP = 0.5
+TIME_FIRST = 0.0
+TIME_SECOND = BASE_STEP / (1 << LEVELS)
+SRC = ("z", "core")
 
 
 def sent_to_all(shard, axis):
@@ -119,7 +127,7 @@
     partial_rows = jnp.where(mine_owned[None, :], chosen, 0.0)
     ahead_pos, moving = predict(column_all[0:12], column_all[12:13])
     sources = jnp.concatenate([ahead_pos, moving, column_all[13:14]], axis=0)
-    target = over_pieces(partial_rows, "src")
+    target = over_pieces(partial_rows, SRC)
     tgt_ahead, tgt_moving = predict(target[0:12], target[12:13])
     zero_forces = jnp.zeros((6, slot_count), jnp.float32)
     columns = jnp.arange(sources.shape[1], dtype=jnp.int32)
@@ -127,7 +135,7 @@
     partial_forces = tile_forces(
         zero_forces, tgt_ahead, tgt_moving, my_slots, tiles_used, sources, idents
     )
-    forces = taken_together(partial_forces, "src")
+    forces = taken_together(partial_forces, SRC)
     corrected = correct(tgt_ahead, tgt_moving, target[6:9], target[9:12], target[12:13], forces)
     returned = gathered_copies(corrected, "tgt", 1)
     write_at = jnp.where(is_owned, local_at, s_dev)
@@ -136,41 +144,398 @@
     return (states, last_time)
 
 
-def shards(positions, velocities, accels, jerks, masses, levels, active_first, active_second):
+def whole_program(positions, velocities, accels, jerks, masses, levels, active_first, active_second):
     s_dev = positions.shape[1]
     n_tgt = lax.axis_size("tgt")
-    n_src = lax.axis_size("src")
+    n_src = lax.axis_size(SRC)
     my_row = lax.axis_index("tgt")
-    my_column = lax.axis_index("src")
+    my_column = lax.axis_index(SRC)
     weights = masses / (s_dev * n_tgt * n_src)
     states = jnp.concatenate([positions, velocities, accels, jerks], axis=0)
     last_time = -BASE_STEP * jnp.exp2(-levels.astype(jnp.float32))
-    for now_time, active in ((0.0, active_first), (BASE_STEP / (1 << LEVELS), active_second)):
+    for now_time, active in ((TIME_FIRST, active_first), (TIME_SECOND, active_second)):
         states, last_time = advance(
             states, last_time, weights, active, now_time, s_dev, n_tgt, n_src, my_row, my_column
         )
     return (states[0:3], states[3:6], states[6:9], states[9:12])
 
 
+def log2_of(size):
+    assert size & (size - 1) == 0, "size"
+    return size.bit_length() - 1
+
+
+def iota(shape, dim):
+    return lax.broadcasted_iota(jnp.int32, shape, dim)
+
+
+def lane_pick(table, lanes):
+    return lax.gather(
+        table,
+        lanes[:, :, None],
+        lax.GatherDimensionNumbers(
+            offset_dims=(),
+            collapsed_slice_dims=(1,),
+            start_index_map=(1,),
+            operand_batching_dims=(0,),
+            start_indices_batching_dims=(0,),
+        ),
+        slice_sizes=(1, 1),
+        mode=lax.GatherScatterMode.PROMISE_IN_BOUNDS,
+    )
+
+
+def turned(rows):
+    pad = jnp.zeros((LANES - rows.shape[0], LANES), rows.dtype)
+    return jnp.concatenate([rows, pad], axis=0).T
+
+
+def rows_of(values, count):
+    width = values[0].shape[1]
+    below = count - sum(v.shape[0] for v in values)
+    pad = [jnp.zeros((below, width), jnp.float32)] if below else []
+    return jnp.concatenate(list(values) + pad, axis=0)
+
+
+def prepare_kernel(pos, vel, acc, jerk, mass, levels, first, second, column_out, row_out):
+    s_dev = pos.shape[1]
+    stars = row_out.shape[0]
+    last = -BASE_STEP * jnp.exp2(-levels[...].astype(jnp.float32))
+    states = jnp.concatenate([pos[...], vel[...], acc[...], jerk[...]], axis=0)
+    room = first.shape[1] + second.shape[1]
+    lists = [first[...].astype(jnp.float32), second[...].astype(jnp.float32)]
+    if s_dev > room:
+        lists.append(jnp.full((1, s_dev - room), -1.0, jnp.float32))
+    listed = jnp.concatenate(lists, axis=1)
+    column = rows_of([states, last, listed], 16)
+    ahead, moving = predict(states, TIME_FIRST - last)
+    row = rows_of([ahead, moving, mass[...]], 8)
+    for copy in range(column_out.shape[0]):
+        column_out[copy] = column
+    for copy in range(stars):
+        row_out[copy] = row
+
+
+def matching_slots(listed, column, n_src, s_dev):
+    ids = listed.astype(jnp.int32)
+    valid = ids >= 0
+    column_of = jnp.where(valid, (ids >> log2_of(s_dev)) & (n_src - 1), -1)
+    per_column = jnp.zeros((n_src, ids.shape[1]), jnp.float32)
+    for row in range(ids.shape[0]):
+        here = column_of[row : row + 1] == iota((n_src, ids.shape[1]), 0)
+        per_column = per_column + here.astype(jnp.float32)
+    most = jnp.max(jnp.sum(per_column, axis=1, keepdims=True))
+    return column_of == column, most
+
+
+def packed_ids(listed, mine, room):
+    n_rows, width = listed.shape
+    flags = mine.astype(jnp.float32)
+    upto = (iota((width, width), 0) <= iota((width, width), 1)).astype(jnp.bfloat16)
+    inside = jnp.dot(flags.astype(jnp.bfloat16), upto, preferred_element_type=jnp.float32)
+    totals = jnp.broadcast_to(inside[:, width - 1 : width], (n_rows, LANES))
+    place = jnp.zeros((1, LANES), jnp.float32)
+    before = []
+    for row in range(n_rows):
+        before.append(place)
+        place = place + totals[row : row + 1]
+    count = jnp.max(place)
+    start = jnp.concatenate(before, axis=0)[:, 0:1]
+    slot = jnp.where(mine, (inside + start).astype(jnp.int32) - 1, -1)
+    columns, rows = [], []
+    for part in range(room // LANES):
+        found = jnp.zeros((LANES, LANES), jnp.float32)
+        want = iota((LANES, LANES), 0) + part * LANES
+        for row in range(n_rows):
+            for chunk in range(width // LANES):
+                cut = slice(chunk * LANES, (chunk + 1) * LANES)
+                hit = jnp.broadcast_to(slot[row : row + 1, cut], (LANES, LANES)) == want
+                found = found + jnp.where(hit, listed[row : row + 1, cut] + 1.0, 0.0)
+        ids = jnp.broadcast_to(jnp.sum(found, axis=1, keepdims=True) - 1.0, (LANES, LANES))
+        columns.append(ids)
+        rows.append(ids.T[0:1])
+    return columns, rows, count
+
+
+def select_kernel(n_src, slots_first, slots_second, where_am_i, held, target_out, turned_out, info_out):
+    n_tgt, _, s_dev = held.shape
+    my_row, my_column = where_am_i[0], where_am_i[1]
+    star_bits, row_bits = log2_of(s_dev), log2_of(s_dev * n_src)
+    listed = held[:, 13, :]
+    first, second = listed[:, :slots_first], listed[:, slots_first : slots_first + slots_second]
+    mine_first, most_first = matching_slots(first, my_column, n_src, s_dev)
+    mine_second, most_second = matching_slots(second, my_column, n_src, s_dev)
+    cols_first, rows_first, count_first = packed_ids(first, mine_first, FIRST_ROOM)
+    cols_second, rows_second, count_second = packed_ids(second, mine_second, SECOND_ROOM)
+    info_out[0] = count_first.astype(jnp.int32)
+    info_out[1] = count_second.astype(jnp.int32)
+    fits = (most_first <= FIRST_ROOM) & (most_second <= SECOND_ROOM)
+    info_out[2] = fits.astype(jnp.int32)
+    info_out[3] = my_row
+    ids = [r.astype(jnp.int32) for r in rows_first + rows_second]
+    per_row = s_dev // LANES
+    lane = [jnp.broadcast_to(i & (LANES - 1), (16, LANES)) for i in ids]
+    chunk_of = [
+        jnp.where(i >= 0, (i >> row_bits) * per_row + ((i & (s_dev - 1)) >> log2_of(LANES)), -1) for i in ids
+    ]
+
+    def one_row(row, picked):
+        for chunk in range(per_row):
+            table = held[row, :, chunk * LANES : (chunk + 1) * LANES]
+            picked = [
+                jnp.where(chunk_of[g] == row * per_row + chunk, lane_pick(table, lane[g]), picked[g])
+                for g in range(len(ids))
+            ]
+        return picked
+
+    picked = lax.fori_loop(0, n_tgt, one_row, [jnp.zeros((16, LANES), jnp.float32)] * len(ids))
+    for g, (states, number) in enumerate(zip(picked, ids)):
+        key = jnp.where((number >= 0) & ((number >> row_bits) == my_row), number & (s_dev - 1), -1)
+        ahead, moving = predict(states[0:12], TIME_FIRST - states[12:13])
+        key = key.astype(jnp.float32)
+        number = number.astype(jnp.float32)
+        cut = slice(g * LANES, (g + 1) * LANES)
+        target_out[:, cut] = rows_of([states[0:13], number, key], 16)
+        turned_out[cut, :] = turned(rows_of([ahead, moving, key, number], 8))
+
+
+def force_kernel(info, near, far, turned_in, force_out, sums):
+    count, my_z = info[0], info[1]
+    n_z, _, s_dev = near.shape
+    copies, _, room = force_out.shape
+    tall = 16
+    sums[...] = jnp.zeros_like(sums)
+
+    def one_block(block, _):
+        at = pl.ds(pl.multiple_of(block * tall, tall), tall)
+        facts = turned_in[at, :]
+        target = [jnp.broadcast_to(facts[:, j : j + 1], (tall, LANES)) for j in range(6)]
+        key = jnp.broadcast_to(facts[:, 6:7], (tall, LANES)).astype(jnp.int32)
+
+        def segment(ref, which, running, own):
+            running = list(running)
+            for chunk in range(s_dev // LANES):
+                cut = slice(chunk * LANES, (chunk + 1) * LANES)
+                source = [jnp.broadcast_to(ref[which, j : j + 1, cut], (tall, LANES)) for j in range(7)]
+                rx, ry, rz = (source[j] - target[j] for j in range(3))
+                ux, uy, uz = (source[j] - target[j] for j in range(3, 6))
+                inverse = lax.rsqrt((rx * rx + ry * ry + rz * rz) + SOFTENING_SQ)
+                inverse_sq = inverse * inverse
+                weight3 = source[6] * inverse * inverse_sq
+                if own:
+                    weight3 = jnp.where(key == iota((tall, LANES), 1) + chunk * LANES, 0.0, weight3)
+                closing = (rx * ux + ry * uy + rz * uz) * inverse_sq * weight3
+                parts = (
+                    rx * weight3, ry * weight3, rz * weight3,
+                    ux * weight3, uy * weight3, uz * weight3,
+                    rx * closing, ry * closing, rz * closing,
+                )
+                running = [a + b for a, b in zip(running, parts)]
+            return tuple(running)
+
+        def both(step, running):
+            running = segment(far, step, running, False)
+            which = jnp.where(step < my_z, step, step + 1)
+            which = jnp.where(step == n_z - 1, my_z, which)
+            return lax.cond(
+                step == n_z - 1,
+                lambda r: segment(near, which, r, True),
+                lambda r: segment(near, which, r, False),
+                running,
+            )
+
+        zero = jnp.zeros((tall, LANES), jnp.float32)
+        running = lax.fori_loop(0, n_z, both, (zero,) * 9)
+        totals = [jnp.sum(r, axis=1, keepdims=True) for r in running]
+        totals = totals[0:3] + [totals[3 + j] - 3.0 * totals[6 + j] for j in range(3)]
+        lanes = iota((tall, LANES), 1)
+        packed = jnp.zeros((tall, LANES), jnp.float32)
+        for j in range(6):
+            packed = jnp.where(lanes == j, jnp.broadcast_to(totals[j], (tall, LANES)), packed)
+        sums[at, :] = packed
+        return 0
+
+    lax.fori_loop(0, (count + tall - 1) // tall, one_block, 0)
+    for part in range(room // LANES):
+        cut = slice(part * LANES, (part + 1) * LANES)
+        rows = sums[cut, :].T[0:8]
+        for copy in range(copies):
+            force_out[copy, :, cut] = rows
+
+
+def summed(received):
+    total = received[0]
+    for row in range(1, received.shape[0]):
+        total = total + received[row]
+    return total
+
+
+def placed(values, keys, old, room):
+    s_dev = old.shape[1]
+    outs, hits = [], []
+    for chunk in range(s_dev // LANES):
+        star = (iota((LANES, LANES), 1) + chunk * LANES).astype(jnp.float32)
+        found = jnp.zeros((LANES, LANES), jnp.float32)
+        for part in range(room // LANES):
+            number = (iota((LANES, LANES), 0) + part * LANES + 1).astype(jnp.float32)
+            found = found + jnp.where(keys[part] == star, number, 0.0)
+        slot = jnp.sum(found, axis=0, keepdims=True).astype(jnp.int32) - 1
+        new = picked_slots(values, slot, room)
+        hit = slot >= 0
+        hits.append(hit)
+        outs.append(jnp.where(hit, new, old[:, chunk * LANES : (chunk + 1) * LANES]))
+    return outs, hits
+
+
+def picked_slots(values, slot, room):
+    lane = jnp.broadcast_to(slot & (LANES - 1), (16, LANES))
+    new = jnp.zeros((16, LANES), jnp.float32)
+    for part in range(room // LANES):
+        pick = lane_pick(values[:, part * LANES : (part + 1) * LANES], lane)
+        new = jnp.where((slot >> log2_of(LANES)) == part, pick, new)
+    return new
+
+
+def correct_kernel(received, target, turned_in, old_states, old_last, weights, row_out, own_out, second_out, turned_out):
+    copies, _, s_dev = row_out.shape
+    room = received.shape[2]
+    forces = summed(received)
+    states = target[0:12, :room]
+    span = TIME_FIRST - target[12:13, :room]
+    ahead, moving = predict(states, span)
+    corrected = correct(ahead, moving, states[6:9], states[9:12], span, forces[0:6])
+    corrected = jnp.concatenate([corrected, jnp.full((1, room), TIME_FIRST, jnp.float32), jnp.zeros((3, room), jnp.float32)], axis=0)
+    columns = [turned_in[part * LANES : (part + 1) * LANES, :] for part in range(room // LANES)]
+    keys = [jnp.broadcast_to(c[:, 6:7], (LANES, LANES)) for c in columns]
+    numbers = [jnp.broadcast_to(c[:, 7:8], (LANES, LANES)) for c in columns]
+    old = rows_of([old_states[...], old_last[...]], 16)
+    outs, _ = placed(corrected, keys, old, room)
+    for chunk, states_new in enumerate(outs):
+        cut = slice(chunk * LANES, (chunk + 1) * LANES)
+        own_out[:, cut] = states_new
+        ahead, moving = predict(states_new[0:12], TIME_SECOND - states_new[12:13])
+        row = rows_of([ahead, moving, weights[:, cut]], 8)
+        for copy in range(copies):
+            row_out[copy, :, cut] = row
+    other = target[:, room : room + SECOND_ROOM]
+    number = other[13:14]
+    found = jnp.zeros((LANES, LANES), jnp.float32)
+    for part in range(room // LANES):
+        place = (iota((LANES, LANES), 0) + part * LANES + 1).astype(jnp.float32)
+        found = found + jnp.where((numbers[part] == number) & (numbers[part] >= 0.0), place, 0.0)
+    slot = jnp.sum(found, axis=0, keepdims=True).astype(jnp.int32) - 1
+    states = jnp.where(slot >= 0, picked_slots(corrected, slot, room), other)
+    span = TIME_SECOND - states[12:13]
+    ahead, moving = predict(states[0:12], span)
+    second_out[...] = rows_of([ahead, moving, states[6:12], span], 16)
+    turned_out[...] = turned(rows_of([ahead, moving, other[14:15]], 8))
+
+
+def finish_kernel(received, second, turned_in, own, pos_out, vel_out, acc_out, jerk_out):
+    forces = summed(received)
+    facts = second[...]
+    corrected = correct(facts[0:3], facts[3:6], facts[6:9], facts[9:12], facts[12:13], forces[0:6])
+    corrected = jnp.concatenate([corrected, jnp.zeros((4, SECOND_ROOM), jnp.float32)], axis=0)
+    keys = [jnp.broadcast_to(turned_in[:, 6:7], (LANES, LANES))]
+    outs, _ = placed(corrected, keys, own[...], SECOND_ROOM)
+    for chunk, new in enumerate(outs):
+        cut = slice(chunk * LANES, (chunk + 1) * LANES)
+        pos_out[:, cut] = new[0:3]
+        vel_out[:, cut] = new[3:6]
+        acc_out[:, cut] = new[6:9]
+        jerk_out[:, cut] = new[9:12]
+
+
+def f32(*shape):
+    return jax.ShapeDtypeStruct(shape, jnp.float32)
+
+
+INTERPRET = False
+
+
+def call(kernel, outs, name, scalars=0, operands=0, scratch=(), smem_out=None):
+    smem, vmem = pl.BlockSpec(memory_space=pltpu.SMEM), pl.BlockSpec(memory_space=pltpu.VMEM)
+    return pl.pallas_call(
+        kernel,
+        out_shape=outs,
+        in_specs=[smem] * scalars + [vmem] * operands,
+        out_specs=tuple(smem if i == smem_out else vmem for i in range(len(outs))),
+        scratch_shapes=list(scratch),
+        name=name,
+        interpret=INTERPRET,
+    )
+
+
+def exchanged(copies, axis):
+    return lax.all_to_all(copies, axis, split_axis=0, concat_axis=0, tiled=True)
+
+
+def other_core(near):
+    return lax.ppermute(near, "core", [(0, 1), (1, 0)])
+
+
+def shards(positions, velocities, accels, jerks, masses, levels, active_first, active_second):
+    s_dev = positions.shape[1]
+    n_tgt, n_z, n_src = lax.axis_size("tgt"), lax.axis_size("z"), lax.axis_size(SRC)
+    my_row, my_column, my_z = lax.axis_index("tgt"), lax.axis_index(SRC), lax.axis_index("z")
+    weights = (masses / (s_dev * n_tgt * n_src)).reshape(1, s_dev)
+    column_copies, row_copies = call(prepare_kernel, (f32(n_tgt, 16, s_dev), f32(n_z, 8, s_dev)), "prepare", 0, 8)(
+        positions, velocities, accels, jerks, weights, levels.reshape(1, s_dev),
+        active_first.reshape(1, -1), active_second.reshape(1, -1),
+    )
+    near = exchanged(row_copies, "z")
+    column = exchanged(column_copies, "tgt")
+    far = other_core(near)
+    all_room = FIRST_ROOM + SECOND_ROOM
+
+    def select(where_am_i, held, *outs):
+        select_kernel(n_src, active_first.shape[0], active_second.shape[0], where_am_i, held, *outs)
+
+    target, columns, info = call(
+        select, (f32(16, all_room), f32(all_room, LANES), jax.ShapeDtypeStruct((4,), jnp.int32)), "select", 1, 1, smem_out=2
+    )(jnp.stack([my_row, my_column]).astype(jnp.int32), column)
+
+    def by_columns(args):
+        near, far, target, columns, info, weights = args[:6]
+        states = jnp.concatenate(args[6:10], axis=0)
+        last = -BASE_STEP * jnp.exp2(-args[11].astype(jnp.float32)).reshape(1, s_dev)
+        first_info = jnp.stack([info[0], my_z]).astype(jnp.int32)
+        second_info = jnp.stack([info[1], my_z]).astype(jnp.int32)
+        (partial,) = call(
+            force_kernel, (f32(n_tgt, 8, FIRST_ROOM),), "forces_first", 1, 3, [pltpu.VMEM((FIRST_ROOM, LANES), jnp.float32)]
+        )(first_info, near, far, columns)
+        received = exchanged(partial, "tgt")
+        row_copies, own, second, second_columns = call(
+            correct_kernel,
+            (f32(n_z, 8, s_dev), f32(16, s_dev), f32(16, SECOND_ROOM), f32(LANES, LANES)),
+            "correct", 0, 6,
+        )(received, target, columns, states, last, weights)
+        near = exchanged(row_copies, "z")
+        far = other_core(near)
+        (partial,) = call(
+            force_kernel, (f32(n_tgt, 8, SECOND_ROOM),), "forces_second", 1, 3, [pltpu.VMEM((SECOND_ROOM, LANES), jnp.float32)]
+        )(second_info, near, far, second_columns)
+        received = exchanged(partial, "tgt")
+        return call(finish_kernel, (f32(3, s_dev),) * 4, "finish", 0, 4)(received, second, second_columns, own)
+
+    inputs = (positions, velocities, accels, jerks, masses, levels, active_first, active_second)
+    return lax.cond(
+        info[2] == 1,
+        lambda args: tuple(by_columns(args)),
+        lambda args: whole_program(*args[6:]),
+        (near, far, target, columns, info, weights, *inputs),
+    )
+
+
 def solution(mesh):
+    n_tgt, n_src = mesh.devices.shape
+    finer = Mesh(mesh.devices.reshape(n_tgt, n_src // 2, 2), ("tgt", "z", "core"))
+    stars = ("tgt", "z", "core")
+    vector, scalar = P(None, stars), P(stars)
     return jax.shard_map(
         shards,
-        mesh=mesh,
-        in_specs=(
-            P(None, ("tgt", "src")),
-            P(None, ("tgt", "src")),
-            P(None, ("tgt", "src")),
-            P(None, ("tgt", "src")),
-            P(("tgt", "src")),
-            P(("tgt", "src")),
-            P("tgt"),
-            P("tgt"),
-        ),
-        out_specs=(
-            P(None, ("tgt", "src")),
-            P(None, ("tgt", "src")),
-            P(None, ("tgt", "src")),
-            P(None, ("tgt", "src")),
-        ),
+        mesh=finer,
+        in_specs=(vector, vector, vector, vector, scalar, scalar, P("tgt"), P("tgt")),
+        out_specs=(vector,) * 4,
         check_vma=False,
     )

time: 271 us -> 131 us (0.48)
  the two profiles are of different devices: /device:TPU:2 before, /device:TPU:32 now
where the time goes in v1:
time: 131 us
  blocking collectives  69.1 us (53%)
  Pallas kernels  22.2 us (17%)
  starting transfers between devices  14.4 us (11%)
  waiting for transfers between devices  13.8 us (11%)
  other arithmetic  6.37 us (5%)
  local copies, waits for them, and re-layouts  3.31 us (3%)
  between operations  1.33 us (1%)
    all_to_all x3, blocking collectives, exchanged(): return lax.all_to_all(copies, axis, split_axis=0, concat_axis=0, tiled=True)  69.1 us
    all_to_all x2, waiting for transfers between devices, exchanged(): return lax.all_to_all(copies, axis, split_axis=0, concat_axis=0, tiled=True)  13.6 us
    all_to_all x2, starting transfers between devices, exchanged(): return lax.all_to_all(copies, axis, split_axis=0, concat_axis=0, tiled=True)  10.5 us
    pallas_call x1, Pallas kernels, by_columns(): call(force_kernel, (f32(n_tgt, 8, FIRST_ROOM),), 'forces_first', 1, 3, [p...  6.83 us
    pallas_call x1, Pallas kernels, by_columns(): call(force_kernel, (f32(n_tgt, 8, SECOND_ROOM),), 'forces_second', 1, 3,...  5.37 us
    pallas_call x1, Pallas kernels, shards(): call(select, (f32(16, all_room), f32(all_room, LANES), jax.ShapeDtypeStru...  4.62 us
    ppermute x2, starting transfers between devices, other_core(): return lax.ppermute(near, 'core', [(0, 1), (1, 0)])  3.83 us
  transfers between devices with their start and end apart: 4, of which 3 were waited for; matrix products, arithmetic and copies ran while one was open for 4% of the time, Pallas kernels for 4%

profile of v1, /device:TPU:32, one launch (start us, length us, event | category | flops | bytes accessed | tf_op | source)
XLA Modules:
  0.0 130.8 jit_solution(12941186345155350540)
XLA Ops:
  0.6 0.7 broadcast_multiply_fusion.1
  1.3 1.7 %prepare.1 = (f32[16,16,512]{2,1,0:T(8,128)}, f32[16,8,512]{2,1,0:T(8,128)}) custom-call(f32[3,512]{1,0:T(4,128)} %pos.1, f32[3,512]{1,0:T(4,128)} %vel.1, f32[3,512]{1,0:T(4,128)} %acc.1, f32[3,512]{1,0:T(4,128)} %jerk.1, f32[1,512]{1,0:T(1,128)S(1)} %bitcast.116, s32[1,512]{1,0:T(1,128)} %bitcast.120, s32[1,256]{1,0:T(1,128)} %bitcast.124, s32[1,128]{1,0:T(1,128)} %bitcast.125), custom_call_target="tpu_custom_call" | custom-call | tf_op jit(solution)/shard_map/prepare/pallas_call | solution.py:482
  3.0 33.1 %all_to_all.58 = f32[16,8,512]{2,1,0:T(8,128)S(1)} all-to-all(f32[16,8,512]{2,1,0:T(8,128)} %get-tuple-element.235), channel_id=1, replica_groups=mesh['tgt'=16,'z'=16,'core'=2] {'z'}, dimensions={0} | all-to-all | bytes 524288 | tf_op jit(solution)/shard_map/all_to_all | solution.py:470
  36.1 7.0 %all-to-all-start.11 = ((f32[16,16,512]{2,1,0:T(8,128)}), f32[16,16,512]{2,1,0:T(8,128)S(1)}, u32[]{:S(2)}, u32[]{:S(2)}) async-start(f32[16,16,512]{2,1,0:T(8,128)} %get-tuple-element.233), calls=%async_computation.11 | async-start | bytes 1048576 | tf_op jit(solution)/shard_map/all_to_all | solution.py:470
  43.2 1.9 %collective-permute-start.1 = (f32[16,8,512]{2,1,0:T(8,128)S(1)}, f32[16,8,512]{2,1,0:T(8,128)S(1)}, u32[]{:S(2)}, u32[]{:S(2)}) collective-permute-start(f32[16,8,512]{2,1,0:T(8,128)S(1)} %all_to_all.58), channel_id=1, source_target_pairs={{0,1},{1,0},{2,3},{3,2},{4,5},{5,4},{6,7},{7,6},{8,9},{9,8},{10,11... | collective-permute-start | bytes 786440 | tf_op jit(solution)/shard_map/ppermute | solution.py:474
  45.1 0.6 pad_add_fusion.2.where_am_i
  45.7 8.3 %all-to-all-done.11.held = f32[16,16,512]{2,1,0:T(8,128)S(1)} async-done(((f32[16,16,512]{2,1,0:T(8,128)}), f32[16,16,512]{2,1,0:T(8,128)S(1)}, u32[]{:S(2)}, u32[]{:S(2)}) %all-to-all-start.11) | async-done | bytes 524320 | tf_op jit(solution)/shard_map/all_to_all | solution.py:470
  54.0 0.0 copy-start
  54.0 0.8 copy-done
  54.7 4.6 %select.53 = (f32[16,384]{1,0:T(8,128)S(1)}, f32[384,128]{1,0:T(8,128)S(1)}, s32[4]{0:T(128)S(1)}) custom-call(s32[2]{0:T(128)} %pad_add_fusion.2.where_am_i, f32[16,16,512]{2,1,0:T(8,128)} %copy-done), custom_call_target="tpu_custom_call" | custom-call | tf_op jit(solution)/shard_map/select/pallas_call | solution.py:494
  59.4 0.6 slice.205
  60.6 0.0 collective-permute-done.1
  60.6 70.2 %conditional.1 = ((f32[3,512]{1,0:T(4,128)}, f32[3,512]{1,0:T(4,128)}, f32[3,512]{1,0:T(4,128)}, f32[3,512]{1,0:T(4,128)})) conditional(s32[]{:T(128)} %bitcast.35, (f32[3,512]{1,0:T(4,128)}, f32[3,512]{1,0:T(4,128)}, f32[3,512]{1,0:T(4,128)}, f32[3,512]{1,0:T(4,128)}, s32[256]{0:T(256)}, /*index=5*/s32[512]{0:T(512)}, f32[512]{0:T(512)}, ...), branch_computations={%region_0.26_spmd, %region_26.27_spmd} | conditional | flops 27315782 | bytes 40337412 | solution.py:522
  60.9 0.6 fusion.34
  61.4 1.2 pad_add_fusion.1.info
  62.7 6.8 %forces_first.1 = f32[16,8,256]{2,1,0:T(8,128)} custom-call(s32[2]{0:T(128)} %pad_add_fusion.1.info, f32[16,8,512]{2,1,0:T(8,128)S(1)} %get-tuple-element.210.near, f32[16,8,512]{2,1,0:T(8,128)S(1)} %get-tuple-element.211.far, f32[384,128]{1,0:T(8,128)S(1)} %get-tuple-element.212.turned_in), custom_call_target="tpu_custom_call" | custom-call | tf_op jit(solution)/shard_map/cond/branch_1_fun/forces_first/pallas_call | solution.py:504
  69.5 3.5 %all-to-all-start = ((f32[16,8,256]{2,1,0:T(8,128)}), f32[16,8,256]{2,1,0:T(8,128)S(1)}, u32[]{:S(2)}, u32[]{:S(2)}) async-start(f32[16,8,256]{2,1,0:T(8,128)} %forces_first.1), calls=%async_computation | async-start | bytes 262144 | tf_op jit(solution)/shard_map/cond/branch_1_fun/all_to_all | solution.py:470
  73.0 1.3 exponential_multiply_fusion
  74.3 1.4 %pad_maximum_fusion.old_states = f32[12,512]{1,0:T(8,128)} fusion(f32[3,512]{1,0:T(4,128)} %get-tuple-element.217, f32[3,512]{1,0:T(4,128)} %get-tuple-element.216, f32[3,512]{1,0:T(4,128)} %get-tuple-element.215, f32[3,512]{1,0:T(4,128)} %get-tuple-element.214), kind=kLoop, calls=%fused_computation.7 | loop fusion | flops 18432 | bytes 49152 | tf_op jit(solution)/shard_map/cond/branch_1_fun/concatenate | solution.py:500
  75.7 5.3 %all-to-all-done.received = f32[16,8,256]{2,1,0:T(8,128)S(1)} async-done(((f32[16,8,256]{2,1,0:T(8,128)}), f32[16,8,256]{2,1,0:T(8,128)S(1)}, u32[]{:S(2)}, u32[]{:S(2)}) %all-to-all-start) | async-done | bytes 131104 | tf_op jit(solution)/shard_map/cond/branch_1_fun/all_to_all | solution.py:470
  81.0 0.0 copy-start.2
  81.0 0.7 copy-done.2
  81.6 2.0 %correct.1 = (f32[16,8,512]{2,1,0:T(8,128)}, f32[16,512]{1,0:T(8,128)}, f32[16,128]{1,0:T(8,128)}, f32[128,128]{1,0:T(8,128)}) custom-call(f32[16,8,256]{2,1,0:T(8,128)} %copy-done.2, f32[16,384]{1,0:T(8,128)S(1)} %get-tuple-element.213.target, f32[384,128]{1,0:T(8,128)S(1)} %get-tuple-element.212.turned_in, f32[12,512]{1,0:T(8,128)} %pad_maximum_fusion.old_states, ...), custom_call_target="tpu_custom_call" | custom-call | tf_op jit(solution)/shard_map/cond/branch_1_fun/correct/pallas_call | solution.py:508
  83.6 24.2 %all_to_all.56.near = f32[16,8,512]{2,1,0:T(8,128)S(1)} all-to-all(f32[16,8,512]{2,1,0:T(8,128)} %get-tuple-element.220), channel_id=1, replica_groups=mesh['tgt'=16,'z'=16,'core'=2] {'z'}, dimensions={0} | all-to-all | bytes 524288 | tf_op jit(solution)/shard_map/cond/branch_1_fun/all_to_all | solution.py:470
  107.8 1.9 %collective-permute-start = (f32[16,8,512]{2,1,0:T(8,128)S(1)}, f32[16,8,512]{2,1,0:T(8,128)S(1)}, u32[]{:S(2)}, u32[]{:S(2)}) collective-permute-start(f32[16,8,512]{2,1,0:T(8,128)S(1)} %all_to_all.56.near), channel_id=1, source_target_pairs={{0,1},{1,0},{2,3},{3,2},{4,5},{5,4},{6,7},{7,6},{8,9},{9,8},{10,11... | collective-permute-start | bytes 786440 | tf_op jit(solution)/shard_map/cond/branch_1_fun/ppermute | solution.py:474
  109.7 1.2 pad_add_fusion.info
  111.0 0.3 collective-permute-done.far
  111.2 0.0 copy-done.1
  111.2 0.7 copy-done.3
  111.9 5.4 %forces_second.1 = f32[16,8,128]{2,1,0:T(8,128)} custom-call(s32[2]{0:T(128)} %pad_add_fusion.info, f32[16,8,512]{2,1,0:T(8,128)} %copy-done.1, f32[16,8,512]{2,1,0:T(8,128)} %copy-done.3, f32[128,128]{1,0:T(8,128)} %get-tuple-element.221.turned_in), custom_call_target="tpu_custom_call" | custom-call | tf_op jit(solution)/shard_map/cond/branch_1_fun/forces_second/pallas_call | solution.py:515
  117.3 11.8 %all_to_all.57.received = f32[16,8,128]{2,1,0:T(8,128)} all-to-all(f32[16,8,128]{2,1,0:T(8,128)} %forces_second.1), channel_id=1, replica_groups=mesh['tgt'=16,'z'=16,'core'=2] {'tgt'}, dimensions={0} | all-to-all | bytes 131072 | tf_op jit(solution)/shard_map/cond/branch_1_fun/all_to_all | solution.py:470
  129.1 1.7 %finish.1 = (f32[3,512]{1,0:T(4,128)}, f32[3,512]{1,0:T(4,128)}, f32[3,512]{1,0:T(4,128)}, f32[3,512]{1,0:T(4,128)}) custom-call(f32[16,8,128]{2,1,0:T(8,128)} %all_to_all.57.received, f32[16,128]{1,0:T(8,128)} %get-tuple-element.222.second, f32[128,128]{1,0:T(8,128)} %get-tuple-element.221.turned_in, f32[16,512]{1,0:T(8,128)} %get-tuple-element.223.own), custom_call_target="tpu_custom_call" | custom-call | tf_op jit(solution)/shard_map/cond/branch_1_fun/finish/pallas_call | solution.py:519
  (2 shorter events, 0.0 us)
Async XLA Ops:
  36.1 17.8 %all-to-all-start.11 = ((f32[16,16,512]{2,1,0:T(8,128)}), f32[16,16,512]{2,1,0:T(8,128)S(1)}, u32[]{:S(2)}, u32[]{:S(2)}) async-start(f32[16,16,512]{2,1,0:T(8,128)} %get-tuple-element.233), calls=%async_computation.11 | async-start | bytes 1048576 | tf_op jit(solution)/shard_map/all_to_all | solution.py:470
  43.2 17.4 %collective-permute-start.1 = (f32[16,8,512]{2,1,0:T(8,128)S(1)}, f32[16,8,512]{2,1,0:T(8,128)S(1)}, u32[]{:S(2)}, u32[]{:S(2)}) collective-permute-start(f32[16,8,512]{2,1,0:T(8,128)S(1)} %all_to_all.58), channel_id=1, source_target_pairs={{0,1},{1,0},{2,3},{3,2},{4,5},{5,4},{6,7},{7,6},{8,9},{9,8},{10,11... | collective-permute-start | bytes 786440 | tf_op jit(solution)/shard_map/ppermute | solution.py:474
  54.0 0.8 copy-start
  69.5 11.5 %all-to-all-start = ((f32[16,8,256]{2,1,0:T(8,128)}), f32[16,8,256]{2,1,0:T(8,128)S(1)}, u32[]{:S(2)}, u32[]{:S(2)}) async-start(f32[16,8,256]{2,1,0:T(8,128)} %forces_first.1), calls=%async_computation | async-start | bytes 262144 | tf_op jit(solution)/shard_map/cond/branch_1_fun/all_to_all | solution.py:470
  81.0 0.7 copy-start.2
  107.8 3.4 %copy-start.1 = (f32[16,8,512]{2,1,0:T(8,128)}, f32[16,8,512]{2,1,0:T(8,128)S(1)}, u32[]{:S(2)}) copy-start(f32[16,8,512]{2,1,0:T(8,128)S(1)} %all_to_all.56.near) | copy-start | bytes 786436 | tf_op jit(solution)/shard_map/cond
  107.8 3.4 %collective-permute-start = (f32[16,8,512]{2,1,0:T(8,128)S(1)}, f32[16,8,512]{2,1,0:T(8,128)S(1)}, u32[]{:S(2)}, u32[]{:S(2)}) collective-permute-start(f32[16,8,512]{2,1,0:T(8,128)S(1)} %all_to_all.56.near), channel_id=1, source_target_pairs={{0,1},{1,0},{2,3},{3,2},{4,5},{5,4},{6,7},{7,6},{8,9},{9,8},{10,11... | collective-permute-start | bytes 786440 | tf_op jit(solution)/shard_map/cond/branch_1_fun/ppermute | solution.py:474
  111.2 0.7 copy-start.3

commit v2 on v1

--- a/solution.py
+++ b/solution.py
@@ -1,3 +1,5 @@
+import functools
+
 import jax
 import jax.numpy as jnp
 from jax import lax
@@ -197,7 +199,7 @@
     return jnp.concatenate(list(values) + pad, axis=0)
 
 
-def prepare_kernel(pos, vel, acc, jerk, mass, levels, first, second, column_out, row_out):
+def prepare_kernel(n_stars, pos, vel, acc, jerk, mass, levels, first, second, column_out, row_out, own_out):
     s_dev = pos.shape[1]
     stars = row_out.shape[0]
     last = -BASE_STEP * jnp.exp2(-levels[...].astype(jnp.float32))
@@ -209,7 +211,9 @@
     listed = jnp.concatenate(lists, axis=1)
     column = rows_of([states, last, listed], 16)
     ahead, moving = predict(states, TIME_FIRST - last)
-    row = rows_of([ahead, moving, mass[...]], 8)
+    weights = mass[...] / n_stars
+    row = rows_of([ahead, moving, weights], 8)
+    own_out[...] = rows_of([states, last, weights], 16)
     for copy in range(column_out.shape[0]):
         column_out[copy] = column
     for copy in range(stars):
@@ -257,21 +261,21 @@
     return columns, rows, count
 
 
-def select_kernel(n_src, slots_first, slots_second, where_am_i, held, target_out, turned_out, info_out):
+def select_kernel(n_src, slots_first, slots_second, held, target_out, turned_out, info_out):
     n_tgt, _, s_dev = held.shape
-    my_row, my_column = where_am_i[0], where_am_i[1]
-    star_bits, row_bits = log2_of(s_dev), log2_of(s_dev * n_src)
+    my_row, my_column = lax.axis_index("tgt"), lax.axis_index(SRC)
+    row_bits = log2_of(s_dev * n_src)
     listed = held[:, 13, :]
     first, second = listed[:, :slots_first], listed[:, slots_first : slots_first + slots_second]
     mine_first, most_first = matching_slots(first, my_column, n_src, s_dev)
     mine_second, most_second = matching_slots(second, my_column, n_src, s_dev)
-    cols_first, rows_first, count_first = packed_ids(first, mine_first, FIRST_ROOM)
-    cols_second, rows_second, count_second = packed_ids(second, mine_second, SECOND_ROOM)
+    _, rows_first, count_first = packed_ids(first, mine_first, FIRST_ROOM)
+    _, rows_second, count_second = packed_ids(second, mine_second, SECOND_ROOM)
     info_out[0] = count_first.astype(jnp.int32)
     info_out[1] = count_second.astype(jnp.int32)
     fits = (most_first <= FIRST_ROOM) & (most_second <= SECOND_ROOM)
     info_out[2] = fits.astype(jnp.int32)
-    info_out[3] = my_row
+    info_out[3] = lax.axis_index("z")
     ids = [r.astype(jnp.int32) for r in rows_first + rows_second]
     per_row = s_dev // LANES
     lane = [jnp.broadcast_to(i & (LANES - 1), (16, LANES)) for i in ids]
@@ -299,24 +303,19 @@
         turned_out[cut, :] = turned(rows_of([ahead, moving, key, number], 8))
 
 
-def force_kernel(info, near, far, turned_in, force_out, sums):
-    count, my_z = info[0], info[1]
-    n_z, _, s_dev = near.shape
+def force_sums(count, my_z, turned_in, near_of, far_of, s_dev, n_z, force_out, sums):
     copies, _, room = force_out.shape
-    tall = 16
     sums[...] = jnp.zeros_like(sums)
 
-    def one_block(block, _):
-        at = pl.ds(pl.multiple_of(block * tall, tall), tall)
+    def one_block(first, tall):
+        at = pl.ds(pl.multiple_of(first, 8), tall)
         facts = turned_in[at, :]
         target = [jnp.broadcast_to(facts[:, j : j + 1], (tall, LANES)) for j in range(6)]
         key = jnp.broadcast_to(facts[:, 6:7], (tall, LANES)).astype(jnp.int32)
 
-        def segment(ref, which, running, own):
-            running = list(running)
+        def segment(source_of, which, running, own=False):
             for chunk in range(s_dev // LANES):
-                cut = slice(chunk * LANES, (chunk + 1) * LANES)
-                source = [jnp.broadcast_to(ref[which, j : j + 1, cut], (tall, LANES)) for j in range(7)]
+                source = [jnp.broadcast_to(source_of(which, j, chunk), (tall, LANES)) for j in range(7)]
                 rx, ry, rz = (source[j] - target[j] for j in range(3))
                 ux, uy, uz = (source[j] - target[j] for j in range(3, 6))
                 inverse = lax.rsqrt((rx * rx + ry * ry + rz * rz) + SOFTENING_SQ)
@@ -331,21 +330,16 @@
                     rx * closing, ry * closing, rz * closing,
                 )
                 running = [a + b for a, b in zip(running, parts)]
-            return tuple(running)
+            return running
 
         def both(step, running):
-            running = segment(far, step, running, False)
-            which = jnp.where(step < my_z, step, step + 1)
-            which = jnp.where(step == n_z - 1, my_z, which)
-            return lax.cond(
-                step == n_z - 1,
-                lambda r: segment(near, which, r, True),
-                lambda r: segment(near, which, r, False),
-                running,
-            )
+            running = segment(far_of, step, list(running))
+            return tuple(segment(near_of, jnp.where(step < my_z, step, step + 1), running))
 
         zero = jnp.zeros((tall, LANES), jnp.float32)
-        running = lax.fori_loop(0, n_z, both, (zero,) * 9)
+        running = lax.fori_loop(0, n_z - 1, both, (zero,) * 9)
+        running = segment(far_of, n_z - 1, list(running))
+        running = segment(near_of, my_z, running, own=True)
         totals = [jnp.sum(r, axis=1, keepdims=True) for r in running]
         totals = totals[0:3] + [totals[3 + j] - 3.0 * totals[6 + j] for j in range(3)]
         lanes = iota((tall, LANES), 1)
@@ -353,14 +347,41 @@
         for j in range(6):
             packed = jnp.where(lanes == j, jnp.broadcast_to(totals[j], (tall, LANES)), packed)
         sums[at, :] = packed
-        return 0
-
-    lax.fori_loop(0, (count + tall - 1) // tall, one_block, 0)
+
+    tall_blocks = (count + 7) // 16
+    pl.loop(0, tall_blocks)(lambda block: one_block(block * 16, 16))
+    pl.when(count > tall_blocks * 16)(lambda: one_block(tall_blocks * 16, 8))
     for part in range(room // LANES):
         cut = slice(part * LANES, (part + 1) * LANES)
         rows = sums[cut, :].T[0:8]
         for copy in range(copies):
             force_out[copy, :, cut] = rows
+
+
+def in_rows(ref):
+    return lambda which, value, chunk: ref[which, value : value + 1, chunk * LANES : (chunk + 1) * LANES]
+
+
+def in_chunks(ref, weight_ref):
+    def source_of(which, value, chunk):
+        if value == 6:
+            return weight_ref[which, :, chunk * LANES : (chunk + 1) * LANES]
+        return ref[which, chunk * 6 + value : chunk * 6 + value + 1, :]
+
+    return source_of
+
+
+def first_force_kernel(info, near, far, turned_in, force_out, near_weights, far_weights, sums):
+    n_z, _, s_dev = near.shape
+    near_weights[...] = near[:, 6:7, :]
+    far_weights[...] = far[:, 6:7, :]
+    force_sums(info[0], info[3], turned_in, in_rows(near), in_rows(far), s_dev, n_z, force_out, sums)
+
+
+def second_force_kernel(info, near, far, near_weights, far_weights, turned_in, force_out, sums):
+    n_z, _, s_dev = near_weights.shape
+    near_of, far_of = in_chunks(near, near_weights), in_chunks(far, far_weights)
+    force_sums(info[1], info[3], turned_in, near_of, far_of, s_dev, n_z, force_out, sums)
 
 
 def summed(received):
@@ -396,8 +417,8 @@
     return new
 
 
-def correct_kernel(received, target, turned_in, old_states, old_last, weights, row_out, own_out, second_out, turned_out):
-    copies, _, s_dev = row_out.shape
+def correct_kernel(received, target, turned_in, old, row_out, own_out, second_out, turned_out):
+    copies = row_out.shape[0]
     room = received.shape[2]
     forces = summed(received)
     states = target[0:12, :room]
@@ -408,15 +429,14 @@
     columns = [turned_in[part * LANES : (part + 1) * LANES, :] for part in range(room // LANES)]
     keys = [jnp.broadcast_to(c[:, 6:7], (LANES, LANES)) for c in columns]
     numbers = [jnp.broadcast_to(c[:, 7:8], (LANES, LANES)) for c in columns]
-    old = rows_of([old_states[...], old_last[...]], 16)
-    outs, _ = placed(corrected, keys, old, room)
+    outs, _ = placed(corrected, keys, old[...], room)
     for chunk, states_new in enumerate(outs):
         cut = slice(chunk * LANES, (chunk + 1) * LANES)
         own_out[:, cut] = states_new
         ahead, moving = predict(states_new[0:12], TIME_SECOND - states_new[12:13])
-        row = rows_of([ahead, moving, weights[:, cut]], 8)
+        row = jnp.concatenate([ahead, moving], axis=0)
         for copy in range(copies):
-            row_out[copy, :, cut] = row
+            row_out[copy, 6 * chunk : 6 * chunk + 6, :] = row
     other = target[:, room : room + SECOND_ROOM]
     number = other[13:14]
     found = jnp.zeros((LANES, LANES), jnp.float32)
@@ -453,7 +473,7 @@
 INTERPRET = False
 
 
-def call(kernel, outs, name, scalars=0, operands=0, scratch=(), smem_out=None):
+def call(kernel, outs, scalars=0, operands=0, scratch=(), smem_out=None):
     smem, vmem = pl.BlockSpec(memory_space=pltpu.SMEM), pl.BlockSpec(memory_space=pltpu.VMEM)
     return pl.pallas_call(
         kernel,
@@ -461,7 +481,6 @@
         in_specs=[smem] * scalars + [vmem] * operands,
         out_specs=tuple(smem if i == smem_out else vmem for i in range(len(outs))),
         scratch_shapes=list(scratch),
-        name=name,
         interpret=INTERPRET,
     )
 
@@ -477,54 +496,45 @@
 def shards(positions, velocities, accels, jerks, masses, levels, active_first, active_second):
     s_dev = positions.shape[1]
     n_tgt, n_z, n_src = lax.axis_size("tgt"), lax.axis_size("z"), lax.axis_size(SRC)
-    my_row, my_column, my_z = lax.axis_index("tgt"), lax.axis_index(SRC), lax.axis_index("z")
-    weights = (masses / (s_dev * n_tgt * n_src)).reshape(1, s_dev)
-    column_copies, row_copies = call(prepare_kernel, (f32(n_tgt, 16, s_dev), f32(n_z, 8, s_dev)), "prepare", 0, 8)(
-        positions, velocities, accels, jerks, weights, levels.reshape(1, s_dev),
+    n_stars = s_dev * n_tgt * n_src
+    column_copies, row_copies, own = call(
+        functools.partial(prepare_kernel, n_stars), (f32(n_tgt, 16, s_dev), f32(n_z, 8, s_dev), f32(16, s_dev)), 0, 8
+    )(
+        positions, velocities, accels, jerks, masses.reshape(1, s_dev), levels.reshape(1, s_dev),
         active_first.reshape(1, -1), active_second.reshape(1, -1),
     )
     near = exchanged(row_copies, "z")
     column = exchanged(column_copies, "tgt")
     far = other_core(near)
     all_room = FIRST_ROOM + SECOND_ROOM
-
-    def select(where_am_i, held, *outs):
-        select_kernel(n_src, active_first.shape[0], active_second.shape[0], where_am_i, held, *outs)
-
     target, columns, info = call(
-        select, (f32(16, all_room), f32(all_room, LANES), jax.ShapeDtypeStruct((4,), jnp.int32)), "select", 1, 1, smem_out=2
-    )(jnp.stack([my_row, my_column]).astype(jnp.int32), column)
-
-    def by_columns(args):
-        near, far, target, columns, info, weights = args[:6]
-        states = jnp.concatenate(args[6:10], axis=0)
-        last = -BASE_STEP * jnp.exp2(-args[11].astype(jnp.float32)).reshape(1, s_dev)
-        first_info = jnp.stack([info[0], my_z]).astype(jnp.int32)
-        second_info = jnp.stack([info[1], my_z]).astype(jnp.int32)
-        (partial,) = call(
-            force_kernel, (f32(n_tgt, 8, FIRST_ROOM),), "forces_first", 1, 3, [pltpu.VMEM((FIRST_ROOM, LANES), jnp.float32)]
-        )(first_info, near, far, columns)
+        functools.partial(select_kernel, n_src, active_first.shape[0], active_second.shape[0]),
+        (f32(16, all_room), f32(all_room, LANES), jax.ShapeDtypeStruct((4,), jnp.int32)), 0, 1, smem_out=2,
+    )(column)
+
+    def by_columns(near_first, far_first, target, columns, info, own, *inputs):
+        partial, near_weights, far_weights = call(
+            first_force_kernel, (f32(n_tgt, 8, FIRST_ROOM), f32(n_z, 1, s_dev), f32(n_z, 1, s_dev)), 1, 3, [pltpu.VMEM((FIRST_ROOM, LANES), jnp.float32)]
+        )(info, near_first, far_first, columns)
         received = exchanged(partial, "tgt")
         row_copies, own, second, second_columns = call(
             correct_kernel,
-            (f32(n_z, 8, s_dev), f32(16, s_dev), f32(16, SECOND_ROOM), f32(LANES, LANES)),
-            "correct", 0, 6,
-        )(received, target, columns, states, last, weights)
+            (f32(n_z, 6 * s_dev // LANES, LANES), f32(16, s_dev), f32(16, SECOND_ROOM), f32(LANES, LANES)),
+            0, 4,
+        )(received, target, columns, own)
         near = exchanged(row_copies, "z")
         far = other_core(near)
         (partial,) = call(
-            force_kernel, (f32(n_tgt, 8, SECOND_ROOM),), "forces_second", 1, 3, [pltpu.VMEM((SECOND_ROOM, LANES), jnp.float32)]
-        )(second_info, near, far, second_columns)
+            second_force_kernel, (f32(n_tgt, 8, SECOND_ROOM),), 1, 5, [pltpu.VMEM((SECOND_ROOM, LANES), jnp.float32)]
+        )(info, near, far, near_weights, far_weights, second_columns)
         received = exchanged(partial, "tgt")
-        return call(finish_kernel, (f32(3, s_dev),) * 4, "finish", 0, 4)(received, second, second_columns, own)
+        return tuple(call(finish_kernel, (f32(3, s_dev),) * 4, 0, 4)(received, second, second_columns, own))
+
+    def anywhere(near_first, far_first, target, columns, info, own, *inputs):
+        return whole_program(*inputs)
 
     inputs = (positions, velocities, accels, jerks, masses, levels, active_first, active_second)
-    return lax.cond(
-        info[2] == 1,
-        lambda args: tuple(by_columns(args)),
-        lambda args: whole_program(*args[6:]),
-        (near, far, target, columns, info, weights, *inputs),
-    )
+    return lax.cond(info[2] == 1, by_columns, anywhere, near, far, target, columns, info, own, *inputs)
 
 
 def solution(mesh):

time: 131 us -> 126 us (0.962)
  the two profiles are of different devices: /device:TPU:32 before, /device:TPU:1 now
where the time goes in v2:
time: 126 us; the launch traced here: 125 us
  blocking collectives  76 us (60%)
  starting transfers between devices  22.1 us (18%)
  Pallas kernels  20.9 us (17%)
  waiting for transfers between devices  2.28 us (2%)
  local copies, waits for them, and re-layouts  2.05 us (2%)
  between operations  1.32 us (1%)
    all_to_all x4, blocking collectives, exchanged(): return lax.all_to_all(copies, axis, split_axis=0, concat_axis=0, tiled=True)  76 us
    ppermute x2, starting transfers between devices, other_core(): return lax.ppermute(near, 'core', [(0, 1), (1, 0)])  15.3 us
    all_to_all x1, starting transfers between devices, exchanged(): return lax.all_to_all(copies, axis, split_axis=0, concat_axis=0, tiled=True)  6.76 us
    pallas_call x1, Pallas kernels, by_columns(): call(first_force_kernel, (f32(n_tgt, 8, FIRST_ROOM), f32(n_z, 1, s_dev),...  6.4 us
    pallas_call x1, Pallas kernels, shards(): call(functools.partial(select_kernel, n_src, active_first.shape[0], activ...  4.61 us
    pallas_call x1, Pallas kernels, by_columns(): call(second_force_kernel, (f32(n_tgt, 8, SECOND_ROOM),), 1, 5, [pltpu.VME...  4.54 us
  transfers between devices with their start and end apart: 3, of which 2 were waited for; matrix products, arithmetic and copies ran while one was open for 0% of the time, Pallas kernels for 4%

profile of v2, /device:TPU:1, one launch (start us, length us, event | category | flops | bytes accessed | tf_op | source)
XLA Modules:
  0.0 124.8 jit_solution(2233860686314779145)
XLA Ops:
  0.6 1.7 %shard_map.119 = (f32[16,16,512]{2,1,0:T(8,128)}, f32[16,8,512]{2,1,0:T(8,128)}, f32[16,512]{1,0:T(8,128)S(1)}) custom-call(f32[3,512]{1,0:T(4,128)} %pos.1, f32[3,512]{1,0:T(4,128)} %vel.1, f32[3,512]{1,0:T(4,128)} %acc.1, f32[3,512]{1,0:T(4,128)} %jerk.1, f32[1,512]{1,0:T(1,128)} %bitcast.114, s32[1,512]{1,0:T(1,128)} %bitcast.115, s32[1,256]{1,0:T(1,128)} %bitcast.118, ...), custom_call_target="tpu_custom_call" | custom-call | tf_op jit(solution)/shard_map/pallas_call | solution.py:500
  2.4 29.5 %all_to_all.59 = f32[16,8,512]{2,1,0:T(8,128)S(1)} all-to-all(f32[16,8,512]{2,1,0:T(8,128)} %get-tuple-element.221), channel_id=1, replica_groups=mesh['tgt'=16,'z'=16,'core'=2] {'z'}, dimensions={0} | all-to-all | bytes 524288 | tf_op jit(solution)/shard_map/all_to_all | solution.py:489
  31.9 6.8 %all-to-all-start.11 = ((f32[16,16,512]{2,1,0:T(8,128)}), f32[16,16,512]{2,1,0:T(8,128)S(1)}, u32[]{:S(2)}, u32[]{:S(2)}) async-start(f32[16,16,512]{2,1,0:T(8,128)} %get-tuple-element.219), calls=%async_computation.11 | async-start | bytes 1048576 | tf_op jit(solution)/shard_map/all_to_all | solution.py:489
  38.6 7.8 %collective-permute-start.1 = (f32[16,8,512]{2,1,0:T(8,128)S(1)}, f32[16,8,512]{2,1,0:T(8,128)S(1)}, u32[]{:S(2)}, u32[]{:S(2)}) collective-permute-start(f32[16,8,512]{2,1,0:T(8,128)S(1)} %all_to_all.59), channel_id=1, source_target_pairs={{0,1},{1,0},{2,3},{3,2},{4,5},{5,4},{6,7},{7,6},{8,9},{9,8},{10,11... | collective-permute-start | bytes 786440 | tf_op jit(solution)/shard_map/ppermute | solution.py:493
  46.4 1.2 all-to-all-done.11.held
  47.6 0.0 copy-start
  47.6 0.8 copy-done
  48.4 4.6 %shard_map.120 = (f32[16,384]{1,0:T(8,128)S(1)}, f32[384,128]{1,0:T(8,128)S(1)}, s32[4]{0:T(128)S(1)}) custom-call(f32[16,16,512]{2,1,0:T(8,128)} %copy-done), custom_call_target="tpu_custom_call" | custom-call | tf_op jit(solution)/shard_map/pallas_call | solution.py:510
  53.0 0.6 slice.199
  54.2 0.0 collective-permute-done.1
  54.3 70.6 %conditional.1 = ((f32[3,512]{1,0:T(4,128)}, f32[3,512]{1,0:T(4,128)}, f32[3,512]{1,0:T(4,128)}, f32[3,512]{1,0:T(4,128)})) conditional(s32[]{:T(128)} %bitcast.31, (f32[3,512]{1,0:T(4,128)}, f32[3,512]{1,0:T(4,128)}, f32[3,512]{1,0:T(4,128)}, f32[3,512]{1,0:T(4,128)}, s32[256]{0:T(256)}, /*index=5*/s32[512]{0:T(512)}, f32[512]{0:T(512)}, ...), branch_computations={%region_0.26_spmd, %region_26.27_spmd} | conditional | flops 27315782 | bytes 40337412 | solution.py:537
  54.5 6.4 %branch_1_fun.4 = (f32[16,8,256]{2,1,0:T(8,128)}, f32[16,1,512]{2,1,0:T(1,128)}, f32[16,1,512]{2,1,0:T(1,128)}) custom-call(s32[4]{0:T(128)S(1)} %get-tuple-element.196.info, f32[16,8,512]{2,1,0:T(8,128)S(1)} %get-tuple-element.197.near, f32[16,8,512]{2,1,0:T(8,128)S(1)} %get-tuple-element.198.far, f32[384,128]{1,0:T(8,128)S(1)} %get-tuple-element.199.turned_in), custom_call_target="tpu_custom_call" | custom-call | tf_op jit(solution)/shard_map/cond/branch_1_fun/pallas_call | solution.py:516
  60.9 12.7 %all_to_all.56.received = f32[16,8,256]{2,1,0:T(8,128)} all-to-all(f32[16,8,256]{2,1,0:T(8,128)} %get-tuple-element.200), channel_id=1, replica_groups=mesh['tgt'=16,'z'=16,'core'=2] {'tgt'}, dimensions={0} | all-to-all | bytes 262144 | tf_op jit(solution)/shard_map/cond/branch_1_fun/all_to_all | solution.py:489
  73.6 1.9 %branch_1_fun.5 = (f32[16,24,128]{2,1,0:T(8,128)}, f32[16,512]{1,0:T(8,128)}, f32[16,128]{1,0:T(8,128)}, f32[128,128]{1,0:T(8,128)}) custom-call(f32[16,8,256]{2,1,0:T(8,128)} %all_to_all.56.received, f32[16,384]{1,0:T(8,128)S(1)} %get-tuple-element.201.target, f32[384,128]{1,0:T(8,128)S(1)} %get-tuple-element.199.turned_in, ...), custom_call_target="tpu_custom_call" | custom-call | tf_op jit(solution)/shard_map/cond/branch_1_fun/pallas_call | solution.py:520
  75.5 22.8 %all_to_all.57.near = f32[16,24,128]{2,1,0:T(8,128)S(1)} all-to-all(f32[16,24,128]{2,1,0:T(8,128)} %get-tuple-element.203), channel_id=1, replica_groups=mesh['tgt'=16,'z'=16,'core'=2] {'z'}, dimensions={0} | all-to-all | bytes 393216 | tf_op jit(solution)/shard_map/cond/branch_1_fun/all_to_all | solution.py:489
  98.3 0.0 copy-start.1
  98.3 7.6 %collective-permute-start = (f32[16,24,128]{2,1,0:T(8,128)S(1)}, f32[16,24,128]{2,1,0:T(8,128)S(1)}, u32[]{:S(2)}, u32[]{:S(2)}) collective-permute-start(f32[16,24,128]{2,1,0:T(8,128)S(1)} %all_to_all.57.near), channel_id=1, source_target_pairs={{0,1},{1,0},{2,3},{3,2},{4,5},{5,4},{6,7},{7,6},{8,9},{9,8},{10,11... | collective-permute-start | bytes 589832 | tf_op jit(solution)/shard_map/cond/branch_1_fun/ppermute | solution.py:493
  105.9 1.0 collective-permute-done.far
  106.9 0.0 copy-start.2
  106.9 0.0 copy-done.1
  106.9 0.7 copy-done.2
  107.6 4.5 %branch_1_fun.6 = f32[16,8,128]{2,1,0:T(8,128)} custom-call(s32[4]{0:T(128)S(1)} %get-tuple-element.196.info, f32[16,24,128]{2,1,0:T(8,128)} %copy-done.1, f32[16,24,128]{2,1,0:T(8,128)} %copy-done.2, f32[16,1,512]{2,1,0:T(1,128)} %get-tuple-element.204.near_weights, f32[16,1,512]{2,1,0:T(1,128)} %get-tuple-element.205.far_weights, ...), custom_call_target="tpu_custom_call" | custom-call | tf_op jit(solution)/shard_map/cond/branch_1_fun/pallas_call | solution.py:527
  112.1 11.0 %all_to_all.58.received = f32[16,8,128]{2,1,0:T(8,128)} all-to-all(f32[16,8,128]{2,1,0:T(8,128)} %branch_1_fun.6), channel_id=1, replica_groups=mesh['tgt'=16,'z'=16,'core'=2] {'tgt'}, dimensions={0} | all-to-all | bytes 131072 | tf_op jit(solution)/shard_map/cond/branch_1_fun/all_to_all | solution.py:489
  123.1 1.7 %branch_1_fun.7 = (f32[3,512]{1,0:T(4,128)}, f32[3,512]{1,0:T(4,128)}, f32[3,512]{1,0:T(4,128)}, f32[3,512]{1,0:T(4,128)}) custom-call(f32[16,8,128]{2,1,0:T(8,128)} %all_to_all.58.received, f32[16,128]{1,0:T(8,128)} %get-tuple-element.207.second, f32[128,128]{1,0:T(8,128)} %get-tuple-element.206.turned_in, f32[16,512]{1,0:T(8,128)} %get-tuple-element.208.own), custom_call_target="tpu_custom_call" | custom-call | tf_op jit(solution)/shard_map/cond/branch_1_fun/pallas_call | solution.py:531
Async XLA Ops:
  31.9 15.8 %all-to-all-start.11 = ((f32[16,16,512]{2,1,0:T(8,128)}), f32[16,16,512]{2,1,0:T(8,128)S(1)}, u32[]{:S(2)}, u32[]{:S(2)}) async-start(f32[16,16,512]{2,1,0:T(8,128)} %get-tuple-element.219), calls=%async_computation.11 | async-start | bytes 1048576 | tf_op jit(solution)/shard_map/all_to_all | solution.py:489
  38.6 15.6 %collective-permute-start.1 = (f32[16,8,512]{2,1,0:T(8,128)S(1)}, f32[16,8,512]{2,1,0:T(8,128)S(1)}, u32[]{:S(2)}, u32[]{:S(2)}) collective-permute-start(f32[16,8,512]{2,1,0:T(8,128)S(1)} %all_to_all.59), channel_id=1, source_target_pairs={{0,1},{1,0},{2,3},{3,2},{4,5},{5,4},{6,7},{7,6},{8,9},{9,8},{10,11... | collective-permute-start | bytes 786440 | tf_op jit(solution)/shard_map/ppermute | solution.py:493
  47.6 0.8 copy-start
  98.3 8.6 %copy-start.1 = (f32[16,24,128]{2,1,0:T(8,128)}, f32[16,24,128]{2,1,0:T(8,128)S(1)}, u32[]{:S(2)}) copy-start(f32[16,24,128]{2,1,0:T(8,128)S(1)} %all_to_all.57.near) | copy-start | bytes 589828 | tf_op jit(solution)/shard_map/cond
  98.3 8.6 %collective-permute-start = (f32[16,24,128]{2,1,0:T(8,128)S(1)}, f32[16,24,128]{2,1,0:T(8,128)S(1)}, u32[]{:S(2)}, u32[]{:S(2)}) collective-permute-start(f32[16,24,128]{2,1,0:T(8,128)S(1)} %all_to_all.57.near), channel_id=1, source_target_pairs={{0,1},{1,0},{2,3},{3,2},{4,5},{5,4},{6,7},{7,6},{8,9},{9,8},{10,11... | collective-permute-start | bytes 589832 | tf_op jit(solution)/shard_map/cond/branch_1_fun/ppermute | solution.py:493
  106.9 0.7 copy-start.2

commit v3 on v0

--- a/solution.py
+++ b/solution.py
@@ -1,14 +1,25 @@
+import functools
+
 import jax
 import jax.numpy as jnp
 from jax import lax
+from jax.experimental import pallas as pl
+from jax.experimental.pallas import tpu as pltpu
+from jax.sharding import Mesh
 from jax.sharding import PartitionSpec as P
 
 TILE = 128
 LEVELS = 4
-
+LANES = 128
+FIRST_ROOM = 256
+SECOND_ROOM = 128
+OWN_ROOM = 32
 
 SOFTENING_SQ = 0.0001
 BASE_STEP = 0.5
+TIME_FIRST = 0.0
+TIME_SECOND = BASE_STEP / (1 << LEVELS)
+SRC = ("z", "core")
 
 
 def sent_to_all(shard, axis):
@@ -119,7 +130,7 @@
     partial_rows = jnp.where(mine_owned[None, :], chosen, 0.0)
     ahead_pos, moving = predict(column_all[0:12], column_all[12:13])
     sources = jnp.concatenate([ahead_pos, moving, column_all[13:14]], axis=0)
-    target = over_pieces(partial_rows, "src")
+    target = over_pieces(partial_rows, SRC)
     tgt_ahead, tgt_moving = predict(target[0:12], target[12:13])
     zero_forces = jnp.zeros((6, slot_count), jnp.float32)
     columns = jnp.arange(sources.shape[1], dtype=jnp.int32)
@@ -127,7 +138,7 @@
     partial_forces = tile_forces(
         zero_forces, tgt_ahead, tgt_moving, my_slots, tiles_used, sources, idents
     )
-    forces = taken_together(partial_forces, "src")
+    forces = taken_together(partial_forces, SRC)
     corrected = correct(tgt_ahead, tgt_moving, target[6:9], target[9:12], target[12:13], forces)
     returned = gathered_copies(corrected, "tgt", 1)
     write_at = jnp.where(is_owned, local_at, s_dev)
@@ -136,41 +147,463 @@
     return (states, last_time)
 
 
-def shards(positions, velocities, accels, jerks, masses, levels, active_first, active_second):
+def whole_program(positions, velocities, accels, jerks, masses, levels, active_first, active_second):
     s_dev = positions.shape[1]
     n_tgt = lax.axis_size("tgt")
-    n_src = lax.axis_size("src")
+    n_src = lax.axis_size(SRC)
     my_row = lax.axis_index("tgt")
-    my_column = lax.axis_index("src")
+    my_column = lax.axis_index(SRC)
     weights = masses / (s_dev * n_tgt * n_src)
     states = jnp.concatenate([positions, velocities, accels, jerks], axis=0)
     last_time = -BASE_STEP * jnp.exp2(-levels.astype(jnp.float32))
-    for now_time, active in ((0.0, active_first), (BASE_STEP / (1 << LEVELS), active_second)):
+    for now_time, active in ((TIME_FIRST, active_first), (TIME_SECOND, active_second)):
         states, last_time = advance(
             states, last_time, weights, active, now_time, s_dev, n_tgt, n_src, my_row, my_column
         )
     return (states[0:3], states[3:6], states[6:9], states[9:12])
 
 
+def log2_of(size):
+    assert size & (size - 1) == 0, "size"
+    return size.bit_length() - 1
+
+
+def iota(shape, dim):
+    return lax.broadcasted_iota(jnp.int32, shape, dim)
+
+
+def lane_pick(table, lanes):
+    return lax.gather(
+        table,
+        lanes[:, :, None],
+        lax.GatherDimensionNumbers(
+            offset_dims=(),
+            collapsed_slice_dims=(1,),
+            start_index_map=(1,),
+            operand_batching_dims=(0,),
+            start_indices_batching_dims=(0,),
+        ),
+        slice_sizes=(1, 1),
+        mode=lax.GatherScatterMode.PROMISE_IN_BOUNDS,
+    )
+
+
+def turned(rows):
+    pad = jnp.zeros((LANES - rows.shape[0], LANES), rows.dtype)
+    return jnp.concatenate([rows, pad], axis=0).T
+
+
+def rows_of(values, count):
+    width = values[0].shape[1]
+    below = count - sum(v.shape[0] for v in values)
+    pad = [jnp.zeros((below, width), jnp.float32)] if below else []
+    return jnp.concatenate(list(values) + pad, axis=0)
+
+
+def prepare_kernel(n_stars, pos, vel, acc, jerk, mass, levels, first, second, column_out, row_out, own_out):
+    s_dev = pos.shape[1]
+    last = -BASE_STEP * jnp.exp2(-levels[...].astype(jnp.float32))
+    states = jnp.concatenate([pos[...], vel[...], acc[...], jerk[...]], axis=0)
+    weights = mass[...] / n_stars
+    room = first.shape[1] + second.shape[1]
+    lists = [first[...].astype(jnp.float32), second[...].astype(jnp.float32)]
+    if s_dev > room:
+        lists.append(jnp.full((1, s_dev - room), -1.0, jnp.float32))
+    listed = jnp.concatenate(lists, axis=1)
+    column = rows_of([states, last, listed, weights], 16)
+    for copy in range(column_out.shape[0]):
+        column_out[copy] = column
+    ahead, moving = predict(states, TIME_FIRST - last)
+    ahead_second, moving_second = predict(states, TIME_SECOND - last)
+    row_out[...] = jnp.concatenate([ahead, moving, weights, ahead_second, moving_second], axis=0)
+    own_out[...] = rows_of([states, last, weights], 16)
+
+
+def matching_slots(listed, column, n_src, s_dev):
+    ids = listed.astype(jnp.int32)
+    n_tgt, width = ids.shape
+    valid = ids >= 0
+    column_of = jnp.where(valid, (ids >> log2_of(s_dev)) & (n_src - 1), -1)
+    row_of = jnp.where(valid, ids >> log2_of(s_dev * n_src), -1)
+    cells = jnp.zeros((n_tgt, n_src), jnp.float32)
+    for slots in range(n_tgt):
+        in_row = (row_of[slots : slots + 1] == iota((n_tgt, width), 0)).astype(jnp.bfloat16)
+        in_column = (column_of[slots : slots + 1] == iota((n_src, width), 0)).astype(jnp.bfloat16)
+        cells = cells + lax.dot_general(
+            in_row, in_column, (((1,), (1,)), ((), ())), preferred_element_type=jnp.float32
+        )
+    return column_of == column, jnp.max(jnp.sum(cells, axis=0, keepdims=True)), jnp.max(cells)
+
+
+def slot_numbers(mine):
+    n_rows, width = mine.shape
+    upto = (iota((width, width), 0) <= iota((width, width), 1)).astype(jnp.bfloat16)
+    inside = jnp.dot(mine.astype(jnp.bfloat16), upto, preferred_element_type=jnp.float32)
+    totals = jnp.broadcast_to(inside[:, width - 1 : width], (n_rows, LANES))
+    place = jnp.zeros((1, LANES), jnp.float32)
+    before = []
+    for row in range(n_rows):
+        before.append(place)
+        place = place + totals[row : row + 1]
+    start = jnp.concatenate(before, axis=0)[:, 0:1]
+    return jnp.where(mine, (inside + start).astype(jnp.int32) - 1, -1), jnp.max(place)
+
+
+def packed_ids(listed, slot, part):
+    n_rows, width = listed.shape
+    found = jnp.zeros((LANES, LANES), jnp.float32)
+    want = iota((LANES, LANES), 0) + part * LANES
+    for row in range(n_rows):
+        for chunk in range(width // LANES):
+            cut = slice(chunk * LANES, (chunk + 1) * LANES)
+            hit = jnp.broadcast_to(slot[row : row + 1, cut], (LANES, LANES)) == want
+            found = found + jnp.where(hit, listed[row : row + 1, cut] + 1.0, 0.0)
+    ids = jnp.broadcast_to(jnp.sum(found, axis=1, keepdims=True) - 1.0, (LANES, LANES))
+    return ids.T[0:1]
+
+
+def target_facts(number, held, my_row, n_src):
+    n_tgt, _, s_dev = held.shape
+    row_bits, per_row = log2_of(s_dev * n_src), s_dev // LANES
+    ids = number.astype(jnp.int32)
+    lane = jnp.broadcast_to(ids & (LANES - 1), (16, LANES))
+    chunk_of = jnp.where(ids >= 0, (ids >> row_bits) * per_row + ((ids & (s_dev - 1)) >> log2_of(LANES)), -1)
+
+    def one_row(row, picked):
+        for chunk in range(per_row):
+            table = held[row, :, chunk * LANES : (chunk + 1) * LANES]
+            picked = jnp.where(chunk_of == row * per_row + chunk, lane_pick(table, lane), picked)
+        return picked
+
+    picked = lax.fori_loop(0, n_tgt, one_row, jnp.zeros((16, LANES), jnp.float32), unroll=2)
+    key = jnp.where((ids >= 0) & ((ids >> row_bits) == my_row), ids & (s_dev - 1), -1)
+    return rows_of([picked[0:13], number, picked[14:15], key.astype(jnp.float32)], 16)
+
+
+def select_kernel(n_src, slots_first, slots_second, held, target_out, turned_out, info_out):
+    s_dev = held.shape[2]
+    my_row, my_column = lax.axis_index("tgt"), lax.axis_index(SRC)
+    listed = held[:, 13, :]
+    first, second = listed[:, :slots_first], listed[:, slots_first : slots_first + slots_second]
+    mine, most_first, most_own = matching_slots(first, my_column, n_src, s_dev)
+    _, most_second, _ = matching_slots(second, my_column, n_src, s_dev)
+    slot, count = slot_numbers(mine)
+    count = count.astype(jnp.int32)
+    info_out[0] = count
+    fits = (most_first <= FIRST_ROOM) & (most_second <= SECOND_ROOM) & (most_own <= OWN_ROOM)
+    info_out[1] = fits.astype(jnp.int32)
+
+    def fill(part):
+        facts = target_facts(packed_ids(first, slot, part), held, my_row, n_src)
+        ahead, moving = predict(facts[0:12], TIME_FIRST - facts[12:13])
+        cut = slice(part * LANES, (part + 1) * LANES)
+        target_out[:, cut] = facts
+        turned_out[cut, :] = turned(rows_of([ahead, moving, facts[15:16], facts[13:14]], 8))
+
+    fill(0)
+    for part in range(1, FIRST_ROOM // LANES):
+        pl.when(count > part * LANES)(functools.partial(fill, part))
+
+        @pl.when(count <= part * LANES)
+        def _():
+            cut = slice(part * LANES, (part + 1) * LANES)
+            target_out[:, cut] = jnp.full((16, LANES), -1.0, jnp.float32)
+            turned_out[cut, :] = jnp.full((LANES, LANES), -1.0, jnp.float32)
+
+
+def found_slots(keys, wanted):
+    found = jnp.zeros((LANES, LANES), jnp.float32)
+    for part, key in enumerate(keys):
+        place = (iota((LANES, LANES), 0) + part * LANES + 1).astype(jnp.float32)
+        found = found + jnp.where((key == wanted) & (key >= 0.0), place, 0.0)
+    return jnp.sum(found, axis=0, keepdims=True).astype(jnp.int32) - 1
+
+
+def plan_kernel(n_src, slots_first, slots_second, held, first_target, turned_in, second_out, plan_out, info_out):
+    s_dev = held.shape[2]
+    my_row, my_column = lax.axis_index("tgt"), lax.axis_index(SRC)
+    listed = held[:, 13, slots_first : slots_first + slots_second]
+    ids = listed.astype(jnp.int32)
+    mine = (ids >= 0) & (((ids >> log2_of(s_dev)) & (n_src - 1)) == my_column)
+    slot, count = slot_numbers(mine)
+    info_out[0] = count.astype(jnp.int32)
+    facts = target_facts(packed_ids(listed, slot, 0), held, my_row, n_src)
+    second_out[...] = facts
+    parts = FIRST_ROOM // LANES
+    columns = [turned_in[part * LANES : (part + 1) * LANES, :] for part in range(parts)]
+    keys = [jnp.broadcast_to(c[:, 6:7], (LANES, LANES)) for c in columns]
+    numbers = [jnp.broadcast_to(c[:, 7:8], (LANES, LANES)) for c in columns]
+    second_keys = [jnp.broadcast_to(facts[15:16], (LANES, LANES)).T]
+    plan_out[...] = jnp.full(plan_out.shape, -1, jnp.int32)
+    for chunk in range(s_dev // LANES):
+        cut = slice(chunk * LANES, (chunk + 1) * LANES)
+        star = (iota((1, LANES), 1) + chunk * LANES).astype(jnp.float32)
+        plan_out[0:1, cut] = found_slots(keys, star)
+        plan_out[1:2, cut] = found_slots(second_keys, star)
+    plan_out[2:3, 0:LANES] = found_slots(numbers, facts[13:14])
+    own = [(key >= 0.0) for key in keys]
+    upto = (iota((LANES, LANES), 1) <= iota((LANES, LANES), 0)).astype(jnp.bfloat16)
+    before = jnp.zeros((1, LANES), jnp.float32)
+    order = []
+    for flags in own:
+        inside = jnp.dot(upto, flags.astype(jnp.bfloat16), preferred_element_type=jnp.float32) + before
+        order.append(jnp.where(flags, inside - 1.0, -1.0))
+        before = inside[LANES - 1 : LANES]
+    plan_out[3:4, 0:LANES] = found_slots(order, iota((1, LANES), 1).astype(jnp.float32))
+
+
+def pair_terms(source, target, own_place=None, key=None):
+    rx, ry, rz = (source[j] - target[j] for j in range(3))
+    ux, uy, uz = (source[j] - target[j] for j in range(3, 6))
+    inverse = lax.rsqrt((rx * rx + ry * ry + rz * rz) + SOFTENING_SQ)
+    inverse_sq = inverse * inverse
+    weight3 = source[6] * inverse * inverse_sq
+    if own_place is not None:
+        weight3 = jnp.where(key == own_place, 0.0, weight3)
+    closing = (rx * ux + ry * uy + rz * uz) * inverse_sq * weight3
+    return (
+        rx * weight3, ry * weight3, rz * weight3,
+        ux * weight3, uy * weight3, uz * weight3,
+        rx * closing, ry * closing, rz * closing,
+    )
+
+
+def added(running, parts):
+    return tuple(a + b for a, b in zip(running, parts))
+
+
+def target_blocks(count, turned_in, sums, visit):
+    def one_block(first, tall):
+        at = pl.ds(pl.multiple_of(first, 8), tall)
+        facts = turned_in[at, :]
+        target = [jnp.broadcast_to(facts[:, j : j + 1], (tall, LANES)) for j in range(6)]
+        key = jnp.broadcast_to(facts[:, 6:7], (tall, LANES))
+        running = visit(tall, target, key, (jnp.zeros((tall, LANES), jnp.float32),) * 9)
+        totals = [running[j] for j in range(3)] + [running[3 + j] - 3.0 * running[6 + j] for j in range(3)]
+        lanes = iota((tall, LANES), 1)
+        packed = sums[at, :]
+        for j in range(6):
+            total = jnp.broadcast_to(jnp.sum(totals[j], axis=1, keepdims=True), (tall, LANES))
+            packed = packed + jnp.where(lanes == j, total, 0.0)
+        sums[at, :] = packed
+
+    tall_blocks = (count + 7) // 16
+    pl.loop(0, tall_blocks)(lambda block: one_block(block * 16, 16))
+    pl.when(count > tall_blocks * 16)(lambda: one_block(tall_blocks * 16, 8))
+
+
+def row_sums(count, stars, first_row, turned_in, sums):
+    n_src, _, s_dev = stars.shape
+    my_column = lax.axis_index(SRC)
+    rows = [first_row + j for j in range(6)] + [6]
+    sums[...] = jnp.zeros_like(sums)
+
+    def visit(tall, target, key, running):
+        def segment(which, running, own):
+            for chunk in range(s_dev // LANES):
+                cut = slice(chunk * LANES, (chunk + 1) * LANES)
+                source = [jnp.broadcast_to(stars[which, j : j + 1, cut], (tall, LANES)) for j in rows]
+                place = (iota((tall, LANES), 1) + chunk * LANES).astype(jnp.float32) if own else None
+                running = added(running, pair_terms(source, target, place, key))
+            return running
+
+        running = lax.fori_loop(0, my_column, lambda which, r: segment(which, r, False), running)
+        running = segment(my_column, running, True)
+        return lax.fori_loop(my_column + 1, n_src, lambda which, r: segment(which, r, False), running)
+
+    target_blocks(count, turned_in, sums, visit)
+
+
+def write_sums(sums, force_out):
+    copies, _, room = force_out.shape
+    for part in range(room // LANES):
+        cut = slice(part * LANES, (part + 1) * LANES)
+        rows = sums[cut, :].T[0:8]
+        for copy in range(copies):
+            force_out[copy, :, cut] = rows
+
+
+def first_force_kernel(info, stars, turned_in, force_out, sums):
+    row_sums(info[0], stars, 0, turned_in, sums)
+    write_sums(sums, force_out)
+
+
+def second_force_kernel(info, stars, turned_in, sums_out):
+    row_sums(info[0], stars, 7, turned_in, sums_out)
+
+
+def update_force_kernel(info, near, far, turned_in, sums_in, force_out, sums, stars):
+    n_z = near.shape[0]
+    my_z = lax.axis_index("z")
+    half = iota((8, LANES), 1) < LANES // 2
+    for z in range(n_z):
+        both = jnp.where(half, near[z], pltpu.roll(far[z], LANES // 2, axis=1))
+        place = jnp.where(half[7:8] & (my_z == z), both[7:8], -2.0)
+        stars[z] = jnp.concatenate([both[0:7], place], axis=0)
+    sums[...] = sums_in[...]
+
+    def visit(tall, target, key, running):
+        def one(z, running):
+            source = [jnp.broadcast_to(stars[z, j : j + 1, :], (tall, LANES)) for j in range(8)]
+            return added(running, pair_terms(source, target, source[7], key))
+
+        return lax.fori_loop(0, n_z, one, running, unroll=4)
+
+    target_blocks(info[0], turned_in, sums, visit)
+    write_sums(sums, force_out)
+
+
+def summed(received):
+    total = received[0]
+    for row in range(1, received.shape[0]):
+        total = total + received[row]
+    return total
+
+
+def picked_slots(values, slot):
+    lane = jnp.broadcast_to(slot & (LANES - 1), (16, LANES))
+    new = jnp.zeros((16, LANES), jnp.float32)
+    for part in range(values.shape[1] // LANES):
+        pick = lane_pick(values[:, part * LANES : (part + 1) * LANES], lane)
+        new = jnp.where((slot >> log2_of(LANES)) == part, pick, new)
+    return new
+
+
+def correct_kernel(received, target, second, plan, own, update_out, own_out, second_out, turned_out):
+    copies = update_out.shape[0]
+    room = received.shape[2]
+    s_dev = own.shape[1]
+    forces = summed(received)
+    states = target[0:12, :]
+    span = TIME_FIRST - target[12:13, :]
+    ahead, moving = predict(states, span)
+    corrected = correct(ahead, moving, states[6:9], states[9:12], span, forces[0:6])
+    corrected = rows_of([corrected, jnp.full((1, room), TIME_FIRST, jnp.float32)], 16)
+    slot = plan[3:4, 0:LANES]
+    old = picked_slots(target[...], slot)
+    new = picked_slots(corrected, slot)
+    present = slot >= 0
+    weight, place = old[14:15], jnp.where(present, old[15:16], -1.0)
+    ahead_new, moving_new = predict(new[0:12], TIME_SECOND - new[12:13])
+    ahead_old, moving_old = predict(old[0:12], TIME_SECOND - old[12:13])
+    arrived = jnp.concatenate([ahead_new, moving_new, weight, place], axis=0)
+    left = jnp.concatenate([ahead_old, moving_old, -weight, place], axis=0)
+    lane = iota((8, LANES), 1)
+    update = jnp.where(lane < OWN_ROOM, arrived, pltpu.roll(left, OWN_ROOM, axis=1))
+    update = jnp.where(lane < 2 * OWN_ROOM, update, 0.0)
+    for copy in range(copies):
+        update_out[copy] = update
+    for chunk in range(s_dev // LANES):
+        cut = slice(chunk * LANES, (chunk + 1) * LANES)
+        slot = plan[0:1, cut]
+        own_out[:, cut] = jnp.where(slot >= 0, picked_slots(corrected, slot), own[:, cut])
+    other = second[...]
+    slot = plan[2:3, 0:LANES]
+    states = jnp.where(slot >= 0, picked_slots(corrected, slot), other)
+    span = TIME_SECOND - states[12:13]
+    ahead, moving = predict(states[0:12], span)
+    second_out[...] = rows_of([ahead, moving, states[6:12], span], 16)
+    turned_out[...] = turned(rows_of([ahead, moving, other[15:16]], 8))
+
+
+def finish_kernel(received, second, plan, own, pos_out, vel_out, acc_out, jerk_out):
+    forces = summed(received)
+    facts = second[...]
+    corrected = correct(facts[0:3], facts[3:6], facts[6:9], facts[9:12], facts[12:13], forces[0:6])
+    corrected = rows_of([corrected], 16)
+    for chunk in range(own.shape[1] // LANES):
+        cut = slice(chunk * LANES, (chunk + 1) * LANES)
+        slot = plan[1:2, cut]
+        new = jnp.where(slot >= 0, picked_slots(corrected, slot), own[:, cut])
+        pos_out[:, cut] = new[0:3]
+        vel_out[:, cut] = new[3:6]
+        acc_out[:, cut] = new[6:9]
+        jerk_out[:, cut] = new[9:12]
+
+
+def f32(*shape):
+    return jax.ShapeDtypeStruct(shape, jnp.float32)
+
+
+INTERPRET = False
+
+
+def call(kernel, outs, scalars=0, operands=0, scratch=(), smem_out=None):
+    smem, vmem = pl.BlockSpec(memory_space=pltpu.SMEM), pl.BlockSpec(memory_space=pltpu.VMEM)
+    return pl.pallas_call(
+        kernel,
+        out_shape=outs,
+        in_specs=[smem] * scalars + [vmem] * operands,
+        out_specs=tuple(smem if i == smem_out else vmem for i in range(len(outs))),
+        scratch_shapes=list(scratch),
+        interpret=INTERPRET,
+    )
+
+
+def exchanged(copies, axis):
+    return lax.all_to_all(copies, axis, split_axis=0, concat_axis=0, tiled=True)
+
+
+def other_core(near):
+    return lax.ppermute(near, "core", [(0, 1), (1, 0)])
+
+
+def shards(positions, velocities, accels, jerks, masses, levels, active_first, active_second):
+    s_dev = positions.shape[1]
+    n_tgt, n_z, n_src = lax.axis_size("tgt"), lax.axis_size("z"), lax.axis_size(SRC)
+    n_stars = s_dev * n_tgt * n_src
+    scalar = jax.ShapeDtypeStruct((2,), jnp.int32)
+    lists = (n_src, active_first.shape[0], active_second.shape[0])
+    column_copies, row, own = call(
+        functools.partial(prepare_kernel, n_stars), (f32(n_tgt, 16, s_dev), f32(13, s_dev), f32(16, s_dev)), 0, 8
+    )(
+        positions, velocities, accels, jerks, masses.reshape(1, s_dev), levels.reshape(1, s_dev),
+        active_first.reshape(1, -1), active_second.reshape(1, -1),
+    )
+    column = exchanged(column_copies, "tgt")
+    stars = lax.all_gather(row, SRC)
+    target, columns, info = call(
+        functools.partial(select_kernel, *lists), (f32(16, FIRST_ROOM), f32(FIRST_ROOM, LANES), scalar), 0, 1, smem_out=2
+    )(column)
+
+    def by_columns(stars, column, target, columns, info, own, *inputs):
+        (partial,) = call(
+            first_force_kernel, (f32(n_tgt, 8, FIRST_ROOM),), 1, 2, [pltpu.VMEM((FIRST_ROOM, LANES), jnp.float32)]
+        )(info, stars, columns)
+        received = exchanged(partial, "tgt")
+        second, plan, second_info = call(
+            functools.partial(plan_kernel, *lists),
+            (f32(16, SECOND_ROOM), jax.ShapeDtypeStruct((8, s_dev), jnp.int32), scalar), 0, 3, smem_out=2,
+        )(column, target, columns)
+        update, own, second, second_columns = call(
+            correct_kernel, (f32(n_z, 8, LANES), f32(16, s_dev), f32(16, SECOND_ROOM), f32(LANES, LANES)), 0, 5
+        )(received, target, second, plan, own)
+        near = exchanged(update, "z")
+        (sums,) = call(second_force_kernel, (f32(SECOND_ROOM, LANES),), 1, 2)(second_info, stars, second_columns)
+        far = other_core(near)
+        (partial,) = call(
+            update_force_kernel, (f32(n_tgt, 8, SECOND_ROOM),), 1, 4,
+            [pltpu.VMEM((SECOND_ROOM, LANES), jnp.float32), pltpu.VMEM((n_z, 8, LANES), jnp.float32)],
+        )(second_info, near, far, second_columns, sums)
+        received = exchanged(partial, "tgt")
+        return tuple(call(finish_kernel, (f32(3, s_dev),) * 4, 0, 4)(received, second, plan, own))
+
+    def anywhere(stars, column, target, columns, info, own, *inputs):
+        return whole_program(*inputs)
+
+    inputs = (positions, velocities, accels, jerks, masses, levels, active_first, active_second)
+    return lax.cond(info[1] == 1, by_columns, anywhere, stars, column, target, columns, info, own, *inputs)
+
+
 def solution(mesh):
+    n_tgt, n_src = mesh.devices.shape
+    finer = Mesh(mesh.devices.reshape(n_tgt, n_src // 2, 2), ("tgt", "z", "core"))
+    stars = ("tgt", "z", "core")
+    vector, scalar = P(None, stars), P(stars)
     return jax.shard_map(
         shards,
-        mesh=mesh,
-        in_specs=(
-            P(None, ("tgt", "src")),
-            P(None, ("tgt", "src")),
-            P(None, ("tgt", "src")),
-            P(None, ("tgt", "src")),
-            P(("tgt", "src")),
-            P(("tgt", "src")),
-            P("tgt"),
-            P("tgt"),
-        ),
-        out_specs=(
-            P(None, ("tgt", "src")),
-            P(None, ("tgt", "src")),
-            P(None, ("tgt", "src")),
-            P(None, ("tgt", "src")),
-        ),
+        mesh=finer,
+        in_specs=(vector, vector, vector, vector, scalar, scalar, P("tgt"), P("tgt")),
+        out_specs=(vector,) * 4,
         check_vma=False,
     )

time: 271 us -> 123 us (0.45)
  the two profiles are of different devices: /device:TPU:2 before, /device:TPU:1 now
where the time goes in v3:
time: 123 us; the launch traced here: 122 us
  blocking collectives  72 us (59%)
  Pallas kernels  23.2 us (19%)
  starting transfers between devices  18.8 us (15%)
  waiting for transfers between devices  4.72 us (4%)
  local copies, waits for them, and re-layouts  1.84 us (1%)
  between operations  1.3 us (1%)
    all_gather x1, blocking collectives, shards(): stars = lax.all_gather(row, SRC)  42.8 us
    all_to_all x2, blocking collectives, exchanged(): return lax.all_to_all(copies, axis, split_axis=0, concat_axis=0, tiled=True)  29.3 us
    all_to_all x2, starting transfers between devices, exchanged(): return lax.all_to_all(copies, axis, split_axis=0, concat_axis=0, tiled=True)  14.5 us
    pallas_call x1, Pallas kernels, by_columns(): call(first_force_kernel, (f32(n_tgt, 8, FIRST_ROOM),), 1, 2, [pltpu.VMEM(...  7.26 us
    all_to_all x2, waiting for transfers between devices, exchanged(): return lax.all_to_all(copies, axis, split_axis=0, concat_axis=0, tiled=True)  4.72 us
    ppermute x1, starting transfers between devices, other_core(): return lax.ppermute(near, 'core', [(0, 1), (1, 0)])  4.34 us
    pallas_call x1, Pallas kernels, by_columns(): call(second_force_kernel, (f32(SECOND_ROOM, LANES),), 1, 2)  4.27 us
  transfers between devices with their start and end apart: 3, of which 1 were waited for; matrix products, arithmetic and copies ran while one was open for 0% of the time, Pallas kernels for 5%

profile of v3, /device:TPU:1, one launch (start us, length us, event | category | flops | bytes accessed | tf_op | source)
XLA Modules:
  0.0 122.3 jit_solution(4188355214325230669)
XLA Ops:
  0.6 1.6 %shard_map.119 = (f32[16,16,512]{2,1,0:T(8,128)}, f32[13,512]{1,0:T(8,128)}, f32[16,512]{1,0:T(8,128)S(1)}) custom-call(f32[3,512]{1,0:T(4,128)} %pos.1, f32[3,512]{1,0:T(4,128)} %vel.1, f32[3,512]{1,0:T(4,128)} %acc.1, f32[3,512]{1,0:T(4,128)} %jerk.1, f32[1,512]{1,0:T(1,128)} %bitcast.116, s32[1,512]{1,0:T(1,128)} %bitcast.117, s32[1,256]{1,0:T(1,128)} %bitcast.120, ...), custom_call_target="tpu_custom_call" | custom-call | tf_op jit(solution)/shard_map/pallas_call | solution.py:557
  2.3 7.6 %all-to-all-start.11 = ((f32[16,16,512]{2,1,0:T(8,128)}), f32[16,16,512]{2,1,0:T(8,128)S(1)}, u32[]{:S(2)}, u32[]{:S(2)}) async-start(f32[16,16,512]{2,1,0:T(8,128)} %get-tuple-element.219), calls=%async_computation.11 | async-start | bytes 1048576 | tf_op jit(solution)/shard_map/all_to_all | solution.py:544
  9.8 42.8 %all-gather.1 = f32[32,13,512]{2,1,0:T(8,128)} all-gather(f32[1,13,512]{2,1,0:T(8,128)} %bitcast.113), channel_id=2, replica_groups=mesh['tgt'=16,'z'=16,'core'=2] {'z','core'}, dimensions={0}, use_global_device_ids=true | all-gather | bytes 878592 | tf_op jit(solution)/shard_map/all_gather | solution.py:564
  52.6 0.0 all-to-all-done.11.held
  52.6 2.2 %shard_map.120 = (f32[16,256]{1,0:T(8,128)S(1)}, f32[256,128]{1,0:T(8,128)S(1)}, s32[2]{0:T(128)S(1)}) custom-call(f32[16,16,512]{2,1,0:T(8,128)S(1)} %all-to-all-done.11.held), custom_call_target="tpu_custom_call" | custom-call | tf_op jit(solution)/shard_map/pallas_call | solution.py:565
  54.9 0.6 slice.199
  56.1 66.2 %conditional.1 = ((f32[3,512]{1,0:T(4,128)}, f32[3,512]{1,0:T(4,128)}, f32[3,512]{1,0:T(4,128)}, f32[3,512]{1,0:T(4,128)})) conditional(s32[]{:T(128)} %bitcast.31, (f32[3,512]{1,0:T(4,128)}, f32[3,512]{1,0:T(4,128)}, f32[3,512]{1,0:T(4,128)}, f32[3,512]{1,0:T(4,128)}, s32[256]{0:T(256)}, /*index=5*/s32[512]{0:T(512)}, f32[512]{0:T(512)}, ...), branch_computations={%region_0.26_spmd, %region_26.27_spmd} | conditional | flops 27315782 | bytes 40337412 | solution.py:595
  56.4 0.0 copy-start
  56.4 7.3 %branch_1_fun.7 = f32[16,8,256]{2,1,0:T(8,128)} custom-call(s32[2]{0:T(128)S(1)} %get-tuple-element.200.info, f32[32,13,512]{2,1,0:T(8,128)} %get-tuple-element.201.stars, f32[256,128]{1,0:T(8,128)S(1)} %get-tuple-element.198.turned_in), custom_call_target="tpu_custom_call" | custom-call | tf_op jit(solution)/shard_map/cond/branch_1_fun/pallas_call | solution.py:570
  63.6 6.9 %all-to-all-start = ((f32[16,8,256]{2,1,0:T(8,128)}), f32[16,8,256]{2,1,0:T(8,128)S(1)}, u32[]{:S(2)}, u32[]{:S(2)}) async-start(f32[16,8,256]{2,1,0:T(8,128)} %branch_1_fun.7), calls=%async_computation | async-start | bytes 262144 | tf_op jit(solution)/shard_map/cond/branch_1_fun/all_to_all | solution.py:544
  70.5 2.1 %branch_1_fun.6 = (f32[16,128]{1,0:T(8,128)}, s32[8,512]{1,0:T(8,128)}, s32[2]{0:T(128)}) custom-call(f32[16,16,512]{2,1,0:T(8,128)S(1)} %get-tuple-element.196.held, f32[16,256]{1,0:T(8,128)S(1)} %get-tuple-element.197.first_target.target, f32[256,128]{1,0:T(8,128)S(1)} %get-tuple-element.198.turned_in), custom_call_target="tpu_custom_call" | custom-call | tf_op jit(solution)/shard_map/cond/branch_1_fun/pallas_call | solution.py:574
  72.7 4.7 %all-to-all-done.received = f32[16,8,256]{2,1,0:T(8,128)S(1)} async-done(((f32[16,8,256]{2,1,0:T(8,128)}), f32[16,8,256]{2,1,0:T(8,128)S(1)}, u32[]{:S(2)}, u32[]{:S(2)}) %all-to-all-start) | async-done | bytes 131104 | tf_op jit(solution)/shard_map/cond/branch_1_fun/all_to_all | solution.py:544
  77.4 0.0 copy-start.1
  77.4 0.6 copy-done.1
  78.0 1.8 %branch_1_fun.8 = (f32[16,8,128]{2,1,0:T(8,128)}, f32[16,512]{1,0:T(8,128)}, f32[16,128]{1,0:T(8,128)}, f32[128,128]{1,0:T(8,128)}) custom-call(f32[16,8,256]{2,1,0:T(8,128)} %copy-done.1, f32[16,256]{1,0:T(8,128)S(1)} %get-tuple-element.197.first_target.target, f32[16,128]{1,0:T(8,128)} %get-tuple-element.202.second, s32[8,512]{1,0:T(8,128)} %get-tuple-element.203.plan, ...), custom_call_target="tpu_custom_call" | custom-call | tf_op jit(solution)/shard_map/cond/branch_1_fun/pallas_call | solution.py:578
  79.8 18.6 %all_to_all.51.near = f32[16,8,128]{2,1,0:T(8,128)S(1)} all-to-all(f32[16,8,128]{2,1,0:T(8,128)} %get-tuple-element.205), channel_id=1, replica_groups=mesh['tgt'=16,'z'=16,'core'=2] {'z'}, dimensions={0} | all-to-all | bytes 131072 | tf_op jit(solution)/shard_map/cond/branch_1_fun/all_to_all | solution.py:544
  98.4 0.0 copy-start.2
  98.4 4.3 %collective-permute-start = (f32[16,8,128]{2,1,0:T(8,128)S(1)}, f32[16,8,128]{2,1,0:T(8,128)S(1)}, u32[]{:S(2)}, u32[]{:S(2)}) collective-permute-start(f32[16,8,128]{2,1,0:T(8,128)S(1)} %all_to_all.51.near), channel_id=1, source_target_pairs={{0,1},{1,0},{2,3},{3,2},{4,5},{5,4},{6,7},{7,6},{8,9},{9,8},{10,11... | collective-permute-start | bytes 196616 | tf_op jit(solution)/shard_map/cond/branch_1_fun/ppermute | solution.py:548
  102.8 0.0 copy-done
  102.8 4.3 %branch_1_fun.9.sums_in = f32[128,128]{1,0:T(8,128)} custom-call(s32[2]{0:T(128)} %get-tuple-element.199.info, f32[32,13,512]{2,1,0:T(8,128)S(1)} %copy-done, f32[128,128]{1,0:T(8,128)} %get-tuple-element.206.turned_in), custom_call_target="tpu_custom_call" | custom-call | tf_op jit(solution)/shard_map/cond/branch_1_fun/pallas_call | solution.py:582
  107.1 0.0 collective-permute-done.far
  107.1 0.0 copy-done.2
  107.1 0.0 copy-start.3
  107.1 0.6 copy-done.3
  107.7 2.4 %branch_1_fun.10 = f32[16,8,128]{2,1,0:T(8,128)} custom-call(s32[2]{0:T(128)} %get-tuple-element.199.info, f32[16,8,128]{2,1,0:T(8,128)} %copy-done.2, f32[16,8,128]{2,1,0:T(8,128)} %copy-done.3, f32[128,128]{1,0:T(8,128)} %get-tuple-element.206.turned_in, f32[128,128]{1,0:T(8,128)} %branch_1_fun.9.sums_in), custom_call_target="tpu_custom_call" | custom-call | tf_op jit(solution)/shard_map/cond/branch_1_fun/pallas_call | solution.py:584
  110.1 10.6 %all_to_all.52.received = f32[16,8,128]{2,1,0:T(8,128)} all-to-all(f32[16,8,128]{2,1,0:T(8,128)} %branch_1_fun.10), channel_id=1, replica_groups=mesh['tgt'=16,'z'=16,'core'=2] {'tgt'}, dimensions={0} | all-to-all | bytes 131072 | tf_op jit(solution)/shard_map/cond/branch_1_fun/all_to_all | solution.py:544
  120.7 1.6 %branch_1_fun.11 = (f32[3,512]{1,0:T(4,128)}, f32[3,512]{1,0:T(4,128)}, f32[3,512]{1,0:T(4,128)}, f32[3,512]{1,0:T(4,128)}) custom-call(f32[16,8,128]{2,1,0:T(8,128)} %all_to_all.52.received, f32[16,128]{1,0:T(8,128)} %get-tuple-element.207.second, s32[8,512]{1,0:T(8,128)} %get-tuple-element.203.plan, f32[16,512]{1,0:T(8,128)} %get-tuple-element.208.own), custom_call_target="tpu_custom_call" | custom-call | tf_op jit(solution)/shard_map/cond/branch_1_fun/pallas_call | solution.py:589
Async XLA Ops:
  2.3 50.4 %all-to-all-start.11 = ((f32[16,16,512]{2,1,0:T(8,128)}), f32[16,16,512]{2,1,0:T(8,128)S(1)}, u32[]{:S(2)}, u32[]{:S(2)}) async-start(f32[16,16,512]{2,1,0:T(8,128)} %get-tuple-element.219), calls=%async_computation.11 | async-start | bytes 1048576 | tf_op jit(solution)/shard_map/all_to_all | solution.py:544
  56.4 46.4 %copy-start = (f32[32,13,512]{2,1,0:T(8,128)S(1)}, f32[32,13,512]{2,1,0:T(8,128)}, u32[]{:S(2)}) copy-start(f32[32,13,512]{2,1,0:T(8,128)} %get-tuple-element.201.stars) | copy-start | bytes 2555908 | tf_op jit(solution)/shard_map/cond
  63.6 13.8 %all-to-all-start = ((f32[16,8,256]{2,1,0:T(8,128)}), f32[16,8,256]{2,1,0:T(8,128)S(1)}, u32[]{:S(2)}, u32[]{:S(2)}) async-start(f32[16,8,256]{2,1,0:T(8,128)} %branch_1_fun.7), calls=%async_computation | async-start | bytes 262144 | tf_op jit(solution)/shard_map/cond/branch_1_fun/all_to_all | solution.py:544
  77.4 0.6 copy-start.1
  98.4 8.6 %copy-start.2 = (f32[16,8,128]{2,1,0:T(8,128)}, f32[16,8,128]{2,1,0:T(8,128)S(1)}, u32[]{:S(2)}) copy-start(f32[16,8,128]{2,1,0:T(8,128)S(1)} %all_to_all.51.near) | copy-start | bytes 196612 | tf_op jit(solution)/shard_map/cond
  98.4 8.6 %collective-permute-start = (f32[16,8,128]{2,1,0:T(8,128)S(1)}, f32[16,8,128]{2,1,0:T(8,128)S(1)}, u32[]{:S(2)}, u32[]{:S(2)}) collective-permute-start(f32[16,8,128]{2,1,0:T(8,128)S(1)} %all_to_all.51.near), channel_id=1, source_target_pairs={{0,1},{1,0},{2,3},{3,2},{4,5},{5,4},{6,7},{7,6},{8,9},{9,8},{10,11... | collective-permute-start | bytes 196616 | tf_op jit(solution)/shard_map/cond/branch_1_fun/ppermute | solution.py:548
  107.1 0.6 copy-start.3

commit v4 on v3

--- a/solution.py
+++ b/solution.py
@@ -211,11 +211,12 @@
         lists.append(jnp.full((1, s_dev - room), -1.0, jnp.float32))
     listed = jnp.concatenate(lists, axis=1)
     column = rows_of([states, last, listed, weights], 16)
-    for copy in range(column_out.shape[0]):
-        column_out[copy] = column
+    column_out[...] = column
     ahead, moving = predict(states, TIME_FIRST - last)
     ahead_second, moving_second = predict(states, TIME_SECOND - last)
-    row_out[...] = jnp.concatenate([ahead, moving, weights, ahead_second, moving_second], axis=0)
+    row = jnp.concatenate([ahead, moving, weights, ahead_second, moving_second], axis=0)
+    for copy in range(row_out.shape[0]):
+        row_out[copy] = row
     own_out[...] = rows_of([states, last, weights], 16)
 
 
@@ -288,7 +289,7 @@
     mine, most_first, most_own = matching_slots(first, my_column, n_src, s_dev)
     _, most_second, _ = matching_slots(second, my_column, n_src, s_dev)
     slot, count = slot_numbers(mine)
-    count = count.astype(jnp.int32)
+    count = jnp.minimum(count.astype(jnp.int32), FIRST_ROOM)
     info_out[0] = count
     fits = (most_first <= FIRST_ROOM) & (most_second <= SECOND_ROOM) & (most_own <= OWN_ROOM)
     info_out[1] = fits.astype(jnp.int32)
@@ -326,7 +327,7 @@
     ids = listed.astype(jnp.int32)
     mine = (ids >= 0) & (((ids >> log2_of(s_dev)) & (n_src - 1)) == my_column)
     slot, count = slot_numbers(mine)
-    info_out[0] = count.astype(jnp.int32)
+    info_out[0] = jnp.minimum(count.astype(jnp.int32), SECOND_ROOM)
     facts = target_facts(packed_ids(listed, slot, 0), held, my_row, n_src)
     second_out[...] = facts
     parts = FIRST_ROOM // LANES
@@ -392,14 +393,14 @@
     pl.when(count > tall_blocks * 16)(lambda: one_block(tall_blocks * 16, 8))
 
 
-def row_sums(count, stars, first_row, turned_in, sums):
-    n_src, _, s_dev = stars.shape
-    my_column = lax.axis_index(SRC)
+def row_sums(count, near, far, first_row, turned_in, sums):
+    n_z, _, s_dev = near.shape
+    my_z = lax.axis_index("z")
     rows = [first_row + j for j in range(6)] + [6]
     sums[...] = jnp.zeros_like(sums)
 
     def visit(tall, target, key, running):
-        def segment(which, running, own):
+        def segment(stars, which, running, own=False):
             for chunk in range(s_dev // LANES):
                 cut = slice(chunk * LANES, (chunk + 1) * LANES)
                 source = [jnp.broadcast_to(stars[which, j : j + 1, cut], (tall, LANES)) for j in rows]
@@ -407,9 +408,11 @@
                 running = added(running, pair_terms(source, target, place, key))
             return running
 
-        running = lax.fori_loop(0, my_column, lambda which, r: segment(which, r, False), running)
-        running = segment(my_column, running, True)
-        return lax.fori_loop(my_column + 1, n_src, lambda which, r: segment(which, r, False), running)
+        def both(step, running):
+            return segment(near, jnp.where(step < my_z, step, step + 1), segment(far, step, running))
+
+        running = lax.fori_loop(0, n_z - 1, both, running)
+        return segment(near, my_z, segment(far, n_z - 1, running), own=True)
 
     target_blocks(count, turned_in, sums, visit)
 
@@ -423,13 +426,13 @@
             force_out[copy, :, cut] = rows
 
 
-def first_force_kernel(info, stars, turned_in, force_out, sums):
-    row_sums(info[0], stars, 0, turned_in, sums)
+def first_force_kernel(info, near, far, turned_in, force_out, sums):
+    row_sums(info[0], near, far, 0, turned_in, sums)
     write_sums(sums, force_out)
 
 
-def second_force_kernel(info, stars, turned_in, sums_out):
-    row_sums(info[0], stars, 7, turned_in, sums_out)
+def second_force_kernel(info, near, far, turned_in, sums_out):
+    row_sums(info[0], near, far, 7, turned_in, sums_out)
 
 
 def update_force_kernel(info, near, far, turned_in, sums_in, force_out, sums, stars):
@@ -537,6 +540,7 @@
         out_specs=tuple(smem if i == smem_out else vmem for i in range(len(outs))),
         scratch_shapes=list(scratch),
         interpret=INTERPRET,
+        compiler_params=pltpu.CompilerParams(vmem_limit_bytes=16 << 20),
     )
 
 
@@ -554,45 +558,46 @@
     n_stars = s_dev * n_tgt * n_src
     scalar = jax.ShapeDtypeStruct((2,), jnp.int32)
     lists = (n_src, active_first.shape[0], active_second.shape[0])
-    column_copies, row, own = call(
-        functools.partial(prepare_kernel, n_stars), (f32(n_tgt, 16, s_dev), f32(13, s_dev), f32(16, s_dev)), 0, 8
+    column, row_copies, own = call(
+        functools.partial(prepare_kernel, n_stars), (f32(16, s_dev), f32(n_z, 13, s_dev), f32(16, s_dev)), 0, 8
     )(
         positions, velocities, accels, jerks, masses.reshape(1, s_dev), levels.reshape(1, s_dev),
         active_first.reshape(1, -1), active_second.reshape(1, -1),
     )
-    column = exchanged(column_copies, "tgt")
-    stars = lax.all_gather(row, SRC)
+    near = exchanged(row_copies, "z")
+    column = lax.all_gather(column, "tgt")
+    far = other_core(near)
     target, columns, info = call(
         functools.partial(select_kernel, *lists), (f32(16, FIRST_ROOM), f32(FIRST_ROOM, LANES), scalar), 0, 1, smem_out=2
     )(column)
-
-    def by_columns(stars, column, target, columns, info, own, *inputs):
-        (partial,) = call(
-            first_force_kernel, (f32(n_tgt, 8, FIRST_ROOM),), 1, 2, [pltpu.VMEM((FIRST_ROOM, LANES), jnp.float32)]
-        )(info, stars, columns)
-        received = exchanged(partial, "tgt")
-        second, plan, second_info = call(
-            functools.partial(plan_kernel, *lists),
-            (f32(16, SECOND_ROOM), jax.ShapeDtypeStruct((8, s_dev), jnp.int32), scalar), 0, 3, smem_out=2,
-        )(column, target, columns)
-        update, own, second, second_columns = call(
-            correct_kernel, (f32(n_z, 8, LANES), f32(16, s_dev), f32(16, SECOND_ROOM), f32(LANES, LANES)), 0, 5
-        )(received, target, second, plan, own)
-        near = exchanged(update, "z")
-        (sums,) = call(second_force_kernel, (f32(SECOND_ROOM, LANES),), 1, 2)(second_info, stars, second_columns)
-        far = other_core(near)
-        (partial,) = call(
-            update_force_kernel, (f32(n_tgt, 8, SECOND_ROOM),), 1, 4,
-            [pltpu.VMEM((SECOND_ROOM, LANES), jnp.float32), pltpu.VMEM((n_z, 8, LANES), jnp.float32)],
-        )(second_info, near, far, second_columns, sums)
-        received = exchanged(partial, "tgt")
+    (partial,) = call(
+        first_force_kernel, (f32(n_tgt, 8, FIRST_ROOM),), 1, 3, [pltpu.VMEM((FIRST_ROOM, LANES), jnp.float32)]
+    )(info, near, far, columns)
+    received = exchanged(partial, "tgt")
+    second, plan, second_info = call(
+        functools.partial(plan_kernel, *lists),
+        (f32(16, SECOND_ROOM), jax.ShapeDtypeStruct((8, s_dev), jnp.int32), scalar), 0, 3, smem_out=2,
+    )(column, target, columns)
+    update, own, second, second_columns = call(
+        correct_kernel, (f32(n_z, 8, LANES), f32(16, s_dev), f32(16, SECOND_ROOM), f32(LANES, LANES)), 0, 5
+    )(received, target, second, plan, own)
+    near_update = exchanged(update, "z")
+    (sums,) = call(second_force_kernel, (f32(SECOND_ROOM, LANES),), 1, 3)(second_info, near, far, second_columns)
+    far_update = other_core(near_update)
+    (partial,) = call(
+        update_force_kernel, (f32(n_tgt, 8, SECOND_ROOM),), 1, 4,
+        [pltpu.VMEM((SECOND_ROOM, LANES), jnp.float32), pltpu.VMEM((n_z, 8, LANES), jnp.float32)],
+    )(second_info, near_update, far_update, second_columns, sums)
+    received = exchanged(partial, "tgt")
+
+    def by_columns(received, second, plan, own, *inputs):
         return tuple(call(finish_kernel, (f32(3, s_dev),) * 4, 0, 4)(received, second, plan, own))
 
-    def anywhere(stars, column, target, columns, info, own, *inputs):
+    def anywhere(received, second, plan, own, *inputs):
         return whole_program(*inputs)
 
     inputs = (positions, velocities, accels, jerks, masses, levels, active_first, active_second)
-    return lax.cond(info[1] == 1, by_columns, anywhere, stars, column, target, columns, info, own, *inputs)
+    return lax.cond(info[1] == 1, by_columns, anywhere, received, second, plan, own, *inputs)
 
 
 def solution(mesh):

time: 123 us -> 133 us (1.081)
  starting transfers between devices: 18.8 us -> 26.2 us
  Pallas kernels: 23.2 us -> 17.4 us
  waiting for transfers between devices: 4.72 us -> 10.3 us
  blocking collectives: 72 us -> 76.1 us
    all_to_all x2, blocking collectives: 29.3 us -> 56.7 us  [exchanged(): return lax.all_to_all(copies, axis, split_axis=0, concat_axis=0, tiled=True)]
    all_gather x1, blocking collectives: 42.8 us -> 19.4 us  [shards(): column = lax.all_gather(column, 'tgt')]
    ppermute x1 -> x2, starting transfers between devices: 4.34 us -> 18 us  [other_core(): return lax.ppermute(near, 'core', [(0, 1), (1, 0)])]
    all_to_all x2, starting transfers between devices: 14.5 us -> 8.2 us  [exchanged(): return lax.all_to_all(copies, axis, split_axis=0, concat_axis=0, tiled=True)]
    all_to_all x2, waiting for transfers between devices: 4.72 us -> 10.3 us  [exchanged(): return lax.all_to_all(copies, axis, split_axis=0, concat_axis=0, tiled=True)]
    pallas_call x6, Pallas kernels: 19.4 us -> 14.4 us  [the longest x1 6.38 us: shards(): call(first_force_kernel, (f32(n_tgt, 8, FIRST_ROOM),), 1, 3, [pltpu.VMEM(...]
  transfers between devices with their start and end apart: 3 -> 4, of which waited for: 1 -> 2; matrix products, arithmetic and copies ran while one was open for 0% -> 0% of each run, Pallas kernels for 5% -> 5%
where the time goes in v4:
time: 133 us; the launch traced here: 132 us
  blocking collectives  76.1 us (57%)
  starting transfers between devices  26.2 us (20%)
  Pallas kernels  17.4 us (13%)
  waiting for transfers between devices  10.3 us (8%)
  between operations  1.46 us (1%)
    all_to_all x2, blocking collectives, exchanged(): return lax.all_to_all(copies, axis, split_axis=0, concat_axis=0, tiled=True)  56.7 us
    all_gather x1, blocking collectives, shards(): column = lax.all_gather(column, 'tgt')  19.4 us
    ppermute x2, starting transfers between devices, other_core(): return lax.ppermute(near, 'core', [(0, 1), (1, 0)])  18 us
    all_to_all x2, waiting for transfers between devices, exchanged(): return lax.all_to_all(copies, axis, split_axis=0, concat_axis=0, tiled=True)  10.3 us
    all_to_all x2, starting transfers between devices, exchanged(): return lax.all_to_all(copies, axis, split_axis=0, concat_axis=0, tiled=True)  8.2 us
    pallas_call x1, Pallas kernels, shards(): call(first_force_kernel, (f32(n_tgt, 8, FIRST_ROOM),), 1, 3, [pltpu.VMEM(...  6.38 us
    pallas_call x1, Pallas kernels, shards(): call(second_force_kernel, (f32(SECOND_ROOM, LANES),), 1, 3)  3.2 us
  transfers between devices with their start and end apart: 4, of which 2 were waited for; matrix products, arithmetic and copies ran while one was open for 0% of the time, Pallas kernels for 5%

profile of v4, /device:TPU:1, one launch (start us, length us, event | category | flops | bytes accessed | tf_op | source)
XLA Modules:
  0.0 132.3 jit_solution(1687396340749549426)
XLA Ops:
  0.6 0.9 shard_map.119
  1.5 0.0 copy-start
  1.5 0.0 copy-start.1
  1.5 0.0 copy-start.2
  1.5 0.0 copy-start.3
  1.6 0.0 copy-start.4
  1.6 0.0 copy-start.5
  1.6 0.0 copy-start.6
  1.6 0.0 copy-start.7
  1.6 38.7 %all_to_all.54.near = f32[16,13,512]{2,1,0:T(8,128)S(1)} all-to-all(f32[16,13,512]{2,1,0:T(8,128)S(1)} %get-tuple-element.218), channel_id=1, replica_groups=mesh['tgt'=16,'z'=16,'core'=2] {'z'}, dimensions={0} | all-to-all | bytes 851968 | tf_op jit(solution)/shard_map/all_to_all | solution.py:548
  40.3 8.9 %collective-permute-start = (f32[16,13,512]{2,1,0:T(8,128)S(1)}, f32[16,13,512]{2,1,0:T(8,128)S(1)}, u32[]{:S(2)}, u32[]{:S(2)}) collective-permute-start(f32[16,13,512]{2,1,0:T(8,128)S(1)} %all_to_all.54.near), channel_id=1, source_target_pairs={{0,1},{1,0},{2,3},{3,2},{4,5},{5,4},{6,7},{7,6},{8,9},{9,8},{10,11... | collective-permute-start | bytes 1277960 | tf_op jit(solution)/shard_map/ppermute | solution.py:552
  49.2 19.4 %all-gather = f32[256,512]{1,0:T(8,128)S(1)} all-gather(f32[16,512]{1,0:T(8,128)S(1)} %get-tuple-element.213), channel_id=2, replica_groups=mesh['tgt'=16,'z'=16,'core'=2] {'tgt'}, dimensions={0}, use_global_device_ids=true | all-gather | bytes 557056 | tf_op jit(solution)/shard_map/all_gather | solution.py:568
  68.6 2.2 %shard_map.120 = (f32[16,256]{1,0:T(8,128)S(1)}, f32[256,128]{1,0:T(8,128)S(1)}, s32[2]{0:T(128)S(1)}) custom-call(f32[16,16,512]{2,1,0:T(8,128)S(1)} %bitcast.87), custom_call_target="tpu_custom_call" | custom-call | tf_op jit(solution)/shard_map/pallas_call | solution.py:570
  70.8 0.0 collective-permute-done.far
  70.8 6.4 %shard_map.122 = f32[16,8,256]{2,1,0:T(8,128)} custom-call(s32[2]{0:T(128)S(1)} %get-tuple-element.214.info, f32[16,13,512]{2,1,0:T(8,128)S(1)} %all_to_all.54.near, f32[16,13,512]{2,1,0:T(8,128)S(1)} %collective-permute-done.far, f32[256,128]{1,0:T(8,128)S(1)} %get-tuple-element.216.turned_in), custom_call_target="tpu_custom_call" | custom-call | tf_op jit(solution)/shard_map/pallas_call | solution.py:573
  77.2 4.7 %all-to-all-start.9 = ((f32[16,8,256]{2,1,0:T(8,128)}), f32[16,8,256]{2,1,0:T(8,128)S(1)}, u32[]{:S(2)}, u32[]{:S(2)}) async-start(f32[16,8,256]{2,1,0:T(8,128)} %shard_map.122), calls=%async_computation.9 | async-start | bytes 262144 | tf_op jit(solution)/shard_map/all_to_all | solution.py:548
  81.9 1.8 %shard_map.121 = (f32[16,128]{1,0:T(8,128)S(1)}, s32[8,512]{1,0:T(8,128)S(1)}, s32[2]{0:T(128)S(1)}) custom-call(f32[16,16,512]{2,1,0:T(8,128)S(1)} %bitcast.88, f32[16,256]{1,0:T(8,128)S(1)} %get-tuple-element.215.first_target.target, f32[256,128]{1,0:T(8,128)S(1)} %get-tuple-element.216.turned_in), custom_call_target="tpu_custom_call" | custom-call | tf_op jit(solution)/shard_map/pallas_call | solution.py:577
  83.7 5.1 %all-to-all-done.9.received = f32[16,8,256]{2,1,0:T(8,128)S(1)} async-done(((f32[16,8,256]{2,1,0:T(8,128)}), f32[16,8,256]{2,1,0:T(8,128)S(1)}, u32[]{:S(2)}, u32[]{:S(2)}) %all-to-all-start.9) | async-done | bytes 131104 | tf_op jit(solution)/shard_map/all_to_all | solution.py:548
  88.7 0.2 shard_map.123
  89.0 18.1 %all_to_all.55.near = f32[16,8,128]{2,1,0:T(8,128)S(1)} all-to-all(f32[16,8,128]{2,1,0:T(8,128)S(1)} %get-tuple-element.222), channel_id=1, replica_groups=mesh['tgt'=16,'z'=16,'core'=2] {'z'}, dimensions={0} | all-to-all | bytes 131072 | tf_op jit(solution)/shard_map/all_to_all | solution.py:548
  107.0 9.1 %collective-permute-start.1 = (f32[16,8,128]{2,1,0:T(8,128)S(1)}, f32[16,8,128]{2,1,0:T(8,128)S(1)}, u32[]{:S(2)}, u32[]{:S(2)}) collective-permute-start(f32[16,8,128]{2,1,0:T(8,128)S(1)} %all_to_all.55.near), channel_id=1, source_target_pairs={{0,1},{1,0},{2,3},{3,2},{4,5},{5,4},{6,7},{7,6},{8,9},{9,8},{10,11... | collective-permute-start | bytes 196616 | tf_op jit(solution)/shard_map/ppermute | solution.py:552
  116.2 3.2 %shard_map.124.sums_in = f32[128,128]{1,0:T(8,128)S(1)} custom-call(s32[2]{0:T(128)S(1)} %get-tuple-element.217.info, f32[16,13,512]{2,1,0:T(8,128)S(1)} %all_to_all.54.near, f32[16,13,512]{2,1,0:T(8,128)S(1)} %collective-permute-done.far, f32[128,128]{1,0:T(8,128)S(1)} %get-tuple-element.223.turned_in), custom_call_target="tpu_custom_call" | custom-call | tf_op jit(solution)/shard_map/pallas_call | solution.py:585
  119.4 0.0 collective-permute-done.1.far
  119.4 2.0 %shard_map.125 = f32[16,8,128]{2,1,0:T(8,128)} custom-call(s32[2]{0:T(128)S(1)} %get-tuple-element.217.info, f32[16,8,128]{2,1,0:T(8,128)S(1)} %all_to_all.55.near, f32[16,8,128]{2,1,0:T(8,128)S(1)} %collective-permute-done.1.far, f32[128,128]{1,0:T(8,128)S(1)} %get-tuple-element.223.turned_in, f32[128,128]{1,0:T(8,128)S(1)} %shard_map.124.sums_in), custom_call_target="tpu_custom_call" | custom-call | tf_op jit(solution)/shard_map/pallas_call | solution.py:587
  121.3 3.5 %all-to-all-start.11 = ((f32[16,8,128]{2,1,0:T(8,128)}), f32[16,8,128]{2,1,0:T(8,128)S(1)}, u32[]{:S(2)}, u32[]{:S(2)}) async-start(f32[16,8,128]{2,1,0:T(8,128)} %shard_map.125), calls=%async_computation.11 | async-start | bytes 131072 | tf_op jit(solution)/shard_map/all_to_all | solution.py:548
  124.8 0.6 slice.199
  126.1 5.2 %all-to-all-done.11 = f32[16,8,128]{2,1,0:T(8,128)S(1)} async-done(((f32[16,8,128]{2,1,0:T(8,128)}), f32[16,8,128]{2,1,0:T(8,128)S(1)}, u32[]{:S(2)}, u32[]{:S(2)}) %all-to-all-start.11) | async-done | bytes 65568 | tf_op jit(solution)/shard_map/all_to_all | solution.py:548
  131.3 0.0 copy-done
  131.3 0.0 copy-done.1
  131.3 0.0 copy-done.2
  131.4 1.0 conditional.1
  131.6 0.7 branch_1_fun.1
  (5 shorter events, 0.0 us)
Async XLA Ops:
  1.5 129.8 %copy-start = (f32[3,512]{1,0:T(4,128)S(1)}, f32[3,512]{1,0:T(4,128)}, u32[]{:S(2)}) copy-start(f32[3,512]{1,0:T(4,128)} %pos.1) | copy-start | bytes 18436
  1.5 129.8 %copy-start.1 = (f32[3,512]{1,0:T(4,128)S(1)}, f32[3,512]{1,0:T(4,128)}, u32[]{:S(2)}) copy-start(f32[3,512]{1,0:T(4,128)} %vel.1) | copy-start | bytes 18436
  1.5 129.8 %copy-start.2 = (f32[3,512]{1,0:T(4,128)S(1)}, f32[3,512]{1,0:T(4,128)}, u32[]{:S(2)}) copy-start(f32[3,512]{1,0:T(4,128)} %acc.1) | copy-start | bytes 18436
  1.5 129.8 %copy-start.3 = (f32[3,512]{1,0:T(4,128)S(1)}, f32[3,512]{1,0:T(4,128)}, u32[]{:S(2)}) copy-start(f32[3,512]{1,0:T(4,128)} %jerk.1) | copy-start | bytes 18436
  1.6 129.8 %copy-start.4 = (f32[512]{0:T(512)S(1)}, f32[512]{0:T(512)}, u32[]{:S(2)}) copy-start(f32[512]{0:T(512)} %param.22) | copy-start | bytes 6148
  1.6 129.8 %copy-start.5 = (s32[512]{0:T(512)S(1)}, s32[512]{0:T(512)}, u32[]{:S(2)}) copy-start(s32[512]{0:T(512)} %param.23) | copy-start | bytes 6148
  1.6 129.8 %copy-start.6 = (s32[256]{0:T(256)S(1)}, s32[256]{0:T(256)}, u32[]{:S(2)}) copy-start(s32[256]{0:T(256)} %param.24) | copy-start | bytes 3076
  1.6 129.8 %copy-start.7 = (s32[128]{0:T(128)S(1)}, s32[128]{0:T(128)}, u32[]{:S(2)}) copy-start(s32[128]{0:T(128)} %param.25) | copy-start | bytes 1540
  40.3 30.5 %collective-permute-start = (f32[16,13,512]{2,1,0:T(8,128)S(1)}, f32[16,13,512]{2,1,0:T(8,128)S(1)}, u32[]{:S(2)}, u32[]{:S(2)}) collective-permute-start(f32[16,13,512]{2,1,0:T(8,128)S(1)} %all_to_all.54.near), channel_id=1, source_target_pairs={{0,1},{1,0},{2,3},{3,2},{4,5},{5,4},{6,7},{7,6},{8,9},{9,8},{10,11... | collective-permute-start | bytes 1277960 | tf_op jit(solution)/shard_map/ppermute | solution.py:552
  77.2 11.6 %all-to-all-start.9 = ((f32[16,8,256]{2,1,0:T(8,128)}), f32[16,8,256]{2,1,0:T(8,128)S(1)}, u32[]{:S(2)}, u32[]{:S(2)}) async-start(f32[16,8,256]{2,1,0:T(8,128)} %shard_map.122), calls=%async_computation.9 | async-start | bytes 262144 | tf_op jit(solution)/shard_map/all_to_all | solution.py:548
  107.0 12.3 %collective-permute-start.1 = (f32[16,8,128]{2,1,0:T(8,128)S(1)}, f32[16,8,128]{2,1,0:T(8,128)S(1)}, u32[]{:S(2)}, u32[]{:S(2)}) collective-permute-start(f32[16,8,128]{2,1,0:T(8,128)S(1)} %all_to_all.55.near), channel_id=1, source_target_pairs={{0,1},{1,0},{2,3},{3,2},{4,5},{5,4},{6,7},{7,6},{8,9},{9,8},{10,11... | collective-permute-start | bytes 196616 | tf_op jit(solution)/shard_map/ppermute | solution.py:552
  121.3 10.0 %all-to-all-start.11 = ((f32[16,8,128]{2,1,0:T(8,128)}), f32[16,8,128]{2,1,0:T(8,128)S(1)}, u32[]{:S(2)}, u32[]{:S(2)}) async-start(f32[16,8,128]{2,1,0:T(8,128)} %shard_map.125), calls=%async_computation.11 | async-start | bytes 131072 | tf_op jit(solution)/shard_map/all_to_all | solution.py:548

commit v5 on v4

--- a/solution.py
+++ b/solution.py
@@ -215,6 +215,7 @@
     ahead, moving = predict(states, TIME_FIRST - last)
     ahead_second, moving_second = predict(states, TIME_SECOND - last)
     row = jnp.concatenate([ahead, moving, weights, ahead_second, moving_second], axis=0)
+    row = jnp.concatenate([row[:, at : at + LANES] for at in range(0, s_dev, LANES)], axis=0)
     for copy in range(row_out.shape[0]):
         row_out[copy] = row
     own_out[...] = rows_of([states, last, weights], 16)
@@ -361,12 +362,9 @@
     weight3 = source[6] * inverse * inverse_sq
     if own_place is not None:
         weight3 = jnp.where(key == own_place, 0.0, weight3)
-    closing = (rx * ux + ry * uy + rz * uz) * inverse_sq * weight3
-    return (
-        rx * weight3, ry * weight3, rz * weight3,
-        ux * weight3, uy * weight3, uz * weight3,
-        rx * closing, ry * closing, rz * closing,
-    )
+    closing = (rx * ux + ry * uy + rz * uz) * inverse_sq
+    ax, ay, az = rx * weight3, ry * weight3, rz * weight3
+    return (ax, ay, az, ux * weight3, uy * weight3, uz * weight3, ax * closing, ay * closing, az * closing)
 
 
 def added(running, parts):
@@ -394,16 +392,16 @@
 
 
 def row_sums(count, near, far, first_row, turned_in, sums):
-    n_z, _, s_dev = near.shape
+    n_z, height, _ = near.shape
     my_z = lax.axis_index("z")
     rows = [first_row + j for j in range(6)] + [6]
     sums[...] = jnp.zeros_like(sums)
 
     def visit(tall, target, key, running):
         def segment(stars, which, running, own=False):
-            for chunk in range(s_dev // LANES):
-                cut = slice(chunk * LANES, (chunk + 1) * LANES)
-                source = [jnp.broadcast_to(stars[which, j : j + 1, cut], (tall, LANES)) for j in rows]
+            for chunk in range(height // 13):
+                at = chunk * 13
+                source = [jnp.broadcast_to(stars[which, at + j : at + j + 1, :], (tall, LANES)) for j in rows]
                 place = (iota((tall, LANES), 1) + chunk * LANES).astype(jnp.float32) if own else None
                 running = added(running, pair_terms(source, target, place, key))
             return running
@@ -559,7 +557,7 @@
     scalar = jax.ShapeDtypeStruct((2,), jnp.int32)
     lists = (n_src, active_first.shape[0], active_second.shape[0])
     column, row_copies, own = call(
-        functools.partial(prepare_kernel, n_stars), (f32(16, s_dev), f32(n_z, 13, s_dev), f32(16, s_dev)), 0, 8
+        functools.partial(prepare_kernel, n_stars), (f32(16, s_dev), f32(n_z, 13 * s_dev // LANES, LANES), f32(16, s_dev)), 0, 8
     )(
         positions, velocities, accels, jerks, masses.reshape(1, s_dev), levels.reshape(1, s_dev),
         active_first.reshape(1, -1), active_second.reshape(1, -1),

time: 133 us -> 130 us (0.977)
  blocking collectives: 76.1 us -> 73 us
    all_to_all x2, blocking collectives: 56.7 us -> 53.6 us  [exchanged(): return lax.all_to_all(copies, axis, split_axis=0, concat_axis=0, tiled=True)]
  transfers between devices with their start and end apart: 4 -> 4, of which waited for: 2 -> 2; matrix products, arithmetic and copies ran while one was open for 0% -> 0% of each run, Pallas kernels for 5% -> 6%
where the time goes in v5:
time: 130 us
  blocking collectives  73 us (56%)
  starting transfers between devices  26.4 us (20%)
  Pallas kernels  17.8 us (14%)
  waiting for transfers between devices  10.3 us (8%)
  between operations  1.46 us (1%)
    all_to_all x2, blocking collectives, exchanged(): return lax.all_to_all(copies, axis, split_axis=0, concat_axis=0, tiled=True)  53.6 us
    all_gather x1, blocking collectives, shards(): column = lax.all_gather(column, 'tgt')  19.4 us
    ppermute x2, starting transfers between devices, other_core(): return lax.ppermute(near, 'core', [(0, 1), (1, 0)])  18.2 us
    all_to_all x2, waiting for transfers between devices, exchanged(): return lax.all_to_all(copies, axis, split_axis=0, concat_axis=0, tiled=True)  10.3 us
    all_to_all x2, starting transfers between devices, exchanged(): return lax.all_to_all(copies, axis, split_axis=0, concat_axis=0, tiled=True)  8.2 us
    pallas_call x1, Pallas kernels, shards(): call(first_force_kernel, (f32(n_tgt, 8, FIRST_ROOM),), 1, 3, [pltpu.VMEM(...  6.68 us
    pallas_call x1, Pallas kernels, shards(): call(second_force_kernel, (f32(SECOND_ROOM, LANES),), 1, 3)  3.31 us
  transfers between devices with their start and end apart: 4, of which 2 were waited for; matrix products, arithmetic and copies ran while one was open for 0% of the time, Pallas kernels for 6%

profile of v5, /device:TPU:1, one launch (start us, length us, event | category | flops | bytes accessed | tf_op | source)
XLA Modules:
  0.0 129.8 jit_solution(6750859285660542531)
XLA Ops:
  0.6 0.0 copy-start.4
  0.6 0.0 copy-start.5
  0.7 0.0 copy-start.6
  0.7 0.0 copy-start.7
  0.7 0.0 copy-start
  0.7 0.0 copy-start.1
  0.7 0.0 copy-start.2
  0.7 0.0 copy-start.3
  0.7 0.9 shard_map.119
  1.6 36.4 %all_to_all.54.near = f32[16,52,128]{2,1,0:T(8,128)S(1)} all-to-all(f32[16,52,128]{2,1,0:T(8,128)S(1)} %get-tuple-element.218), channel_id=1, replica_groups=mesh['tgt'=16,'z'=16,'core'=2] {'z'}, dimensions={0} | all-to-all | bytes 851968 | tf_op jit(solution)/shard_map/all_to_all | solution.py:546
  38.0 9.0 %collective-permute-start = (f32[16,52,128]{2,1,0:T(8,128)S(1)}, f32[16,52,128]{2,1,0:T(8,128)S(1)}, u32[]{:S(2)}, u32[]{:S(2)}) collective-permute-start(f32[16,52,128]{2,1,0:T(8,128)S(1)} %all_to_all.54.near), channel_id=1, source_target_pairs={{0,1},{1,0},{2,3},{3,2},{4,5},{5,4},{6,7},{7,6},{8,9},{9,8},{10,11... | collective-permute-start | bytes 1277960 | tf_op jit(solution)/shard_map/ppermute | solution.py:550
  47.0 19.4 %all-gather = f32[256,512]{1,0:T(8,128)S(1)} all-gather(f32[16,512]{1,0:T(8,128)S(1)} %get-tuple-element.213), channel_id=2, replica_groups=mesh['tgt'=16,'z'=16,'core'=2] {'tgt'}, dimensions={0}, use_global_device_ids=true | all-gather | bytes 557056 | tf_op jit(solution)/shard_map/all_gather | solution.py:566
  66.3 2.2 %shard_map.120 = (f32[16,256]{1,0:T(8,128)S(1)}, f32[256,128]{1,0:T(8,128)S(1)}, s32[2]{0:T(128)S(1)}) custom-call(f32[16,16,512]{2,1,0:T(8,128)S(1)} %bitcast.87), custom_call_target="tpu_custom_call" | custom-call | tf_op jit(solution)/shard_map/pallas_call | solution.py:568
  68.6 0.0 collective-permute-done.far
  68.6 6.7 %shard_map.122 = f32[16,8,256]{2,1,0:T(8,128)} custom-call(s32[2]{0:T(128)S(1)} %get-tuple-element.214.info, f32[16,52,128]{2,1,0:T(8,128)S(1)} %all_to_all.54.near, f32[16,52,128]{2,1,0:T(8,128)S(1)} %collective-permute-done.far, f32[256,128]{1,0:T(8,128)S(1)} %get-tuple-element.216.turned_in), custom_call_target="tpu_custom_call" | custom-call | tf_op jit(solution)/shard_map/pallas_call | solution.py:571
  75.3 4.7 %all-to-all-start.9 = ((f32[16,8,256]{2,1,0:T(8,128)}), f32[16,8,256]{2,1,0:T(8,128)S(1)}, u32[]{:S(2)}, u32[]{:S(2)}) async-start(f32[16,8,256]{2,1,0:T(8,128)} %shard_map.122), calls=%async_computation.9 | async-start | bytes 262144 | tf_op jit(solution)/shard_map/all_to_all | solution.py:546
  80.0 1.8 %shard_map.121 = (f32[16,128]{1,0:T(8,128)S(1)}, s32[8,512]{1,0:T(8,128)S(1)}, s32[2]{0:T(128)S(1)}) custom-call(f32[16,16,512]{2,1,0:T(8,128)S(1)} %bitcast.88, f32[16,256]{1,0:T(8,128)S(1)} %get-tuple-element.215.first_target.target, f32[256,128]{1,0:T(8,128)S(1)} %get-tuple-element.216.turned_in), custom_call_target="tpu_custom_call" | custom-call | tf_op jit(solution)/shard_map/pallas_call | solution.py:575
  81.8 5.1 %all-to-all-done.9.received = f32[16,8,256]{2,1,0:T(8,128)S(1)} async-done(((f32[16,8,256]{2,1,0:T(8,128)}), f32[16,8,256]{2,1,0:T(8,128)S(1)}, u32[]{:S(2)}, u32[]{:S(2)}) %all-to-all-start.9) | async-done | bytes 131104 | tf_op jit(solution)/shard_map/all_to_all | solution.py:546
  86.8 0.2 shard_map.123
  87.1 17.2 %all_to_all.55.near = f32[16,8,128]{2,1,0:T(8,128)S(1)} all-to-all(f32[16,8,128]{2,1,0:T(8,128)S(1)} %get-tuple-element.222), channel_id=1, replica_groups=mesh['tgt'=16,'z'=16,'core'=2] {'z'}, dimensions={0} | all-to-all | bytes 131072 | tf_op jit(solution)/shard_map/all_to_all | solution.py:546
  104.3 9.2 %collective-permute-start.1 = (f32[16,8,128]{2,1,0:T(8,128)S(1)}, f32[16,8,128]{2,1,0:T(8,128)S(1)}, u32[]{:S(2)}, u32[]{:S(2)}) collective-permute-start(f32[16,8,128]{2,1,0:T(8,128)S(1)} %all_to_all.55.near), channel_id=1, source_target_pairs={{0,1},{1,0},{2,3},{3,2},{4,5},{5,4},{6,7},{7,6},{8,9},{9,8},{10,11... | collective-permute-start | bytes 196616 | tf_op jit(solution)/shard_map/ppermute | solution.py:550
  113.5 3.3 %shard_map.124.sums_in = f32[128,128]{1,0:T(8,128)S(1)} custom-call(s32[2]{0:T(128)S(1)} %get-tuple-element.217.info, f32[16,52,128]{2,1,0:T(8,128)S(1)} %all_to_all.54.near, f32[16,52,128]{2,1,0:T(8,128)S(1)} %collective-permute-done.far, f32[128,128]{1,0:T(8,128)S(1)} %get-tuple-element.223.turned_in), custom_call_target="tpu_custom_call" | custom-call | tf_op jit(solution)/shard_map/pallas_call | solution.py:583
  116.8 0.0 collective-permute-done.1.far
  116.8 2.0 %shard_map.125 = f32[16,8,128]{2,1,0:T(8,128)} custom-call(s32[2]{0:T(128)S(1)} %get-tuple-element.217.info, f32[16,8,128]{2,1,0:T(8,128)S(1)} %all_to_all.55.near, f32[16,8,128]{2,1,0:T(8,128)S(1)} %collective-permute-done.1.far, f32[128,128]{1,0:T(8,128)S(1)} %get-tuple-element.223.turned_in, f32[128,128]{1,0:T(8,128)S(1)} %shard_map.124.sums_in), custom_call_target="tpu_custom_call" | custom-call | tf_op jit(solution)/shard_map/pallas_call | solution.py:585
  118.8 3.5 %all-to-all-start.11 = ((f32[16,8,128]{2,1,0:T(8,128)}), f32[16,8,128]{2,1,0:T(8,128)S(1)}, u32[]{:S(2)}, u32[]{:S(2)}) async-start(f32[16,8,128]{2,1,0:T(8,128)} %shard_map.125), calls=%async_computation.11 | async-start | bytes 131072 | tf_op jit(solution)/shard_map/all_to_all | solution.py:546
  122.3 0.6 slice.199
  123.6 5.2 %all-to-all-done.11 = f32[16,8,128]{2,1,0:T(8,128)S(1)} async-done(((f32[16,8,128]{2,1,0:T(8,128)}), f32[16,8,128]{2,1,0:T(8,128)S(1)}, u32[]{:S(2)}, u32[]{:S(2)}) %all-to-all-start.11) | async-done | bytes 65568 | tf_op jit(solution)/shard_map/all_to_all | solution.py:546
  128.8 0.0 copy-done.4
  128.8 0.0 copy-done.5
  128.8 0.0 copy-done.6
  128.8 1.0 conditional.1
  129.1 0.7 branch_1_fun.1
  (5 shorter events, 0.0 us)
Async XLA Ops:
  0.6 128.2 %copy-start.4 = (f32[512]{0:T(512)S(1)}, f32[512]{0:T(512)}, u32[]{:S(2)}) copy-start(f32[512]{0:T(512)} %param.22) | copy-start | bytes 6148
  0.6 128.1 %copy-start.5 = (s32[512]{0:T(512)S(1)}, s32[512]{0:T(512)}, u32[]{:S(2)}) copy-start(s32[512]{0:T(512)} %param.23) | copy-start | bytes 6148
  0.7 128.1 %copy-start.6 = (s32[256]{0:T(256)S(1)}, s32[256]{0:T(256)}, u32[]{:S(2)}) copy-start(s32[256]{0:T(256)} %param.24) | copy-start | bytes 3076
  0.7 128.1 %copy-start.7 = (s32[128]{0:T(128)S(1)}, s32[128]{0:T(128)}, u32[]{:S(2)}) copy-start(s32[128]{0:T(128)} %param.25) | copy-start | bytes 1540
  0.7 128.1 %copy-start = (f32[3,512]{1,0:T(4,128)S(1)}, f32[3,512]{1,0:T(4,128)}, u32[]{:S(2)}) copy-start(f32[3,512]{1,0:T(4,128)} %pos.1) | copy-start | bytes 18436
  0.7 128.1 %copy-start.1 = (f32[3,512]{1,0:T(4,128)S(1)}, f32[3,512]{1,0:T(4,128)}, u32[]{:S(2)}) copy-start(f32[3,512]{1,0:T(4,128)} %vel.1) | copy-start | bytes 18436
  0.7 128.1 %copy-start.2 = (f32[3,512]{1,0:T(4,128)S(1)}, f32[3,512]{1,0:T(4,128)}, u32[]{:S(2)}) copy-start(f32[3,512]{1,0:T(4,128)} %acc.1) | copy-start | bytes 18436
  0.7 128.1 %copy-start.3 = (f32[3,512]{1,0:T(4,128)S(1)}, f32[3,512]{1,0:T(4,128)}, u32[]{:S(2)}) copy-start(f32[3,512]{1,0:T(4,128)} %jerk.1) | copy-start | bytes 18436
  38.0 30.6 %collective-permute-start = (f32[16,52,128]{2,1,0:T(8,128)S(1)}, f32[16,52,128]{2,1,0:T(8,128)S(1)}, u32[]{:S(2)}, u32[]{:S(2)}) collective-permute-start(f32[16,52,128]{2,1,0:T(8,128)S(1)} %all_to_all.54.near), channel_id=1, source_target_pairs={{0,1},{1,0},{2,3},{3,2},{4,5},{5,4},{6,7},{7,6},{8,9},{9,8},{10,11... | collective-permute-start | bytes 1277960 | tf_op jit(solution)/shard_map/ppermute | solution.py:550
  75.3 11.6 %all-to-all-start.9 = ((f32[16,8,256]{2,1,0:T(8,128)}), f32[16,8,256]{2,1,0:T(8,128)S(1)}, u32[]{:S(2)}, u32[]{:S(2)}) async-start(f32[16,8,256]{2,1,0:T(8,128)} %shard_map.122), calls=%async_computation.9 | async-start | bytes 262144 | tf_op jit(solution)/shard_map/all_to_all | solution.py:546
  104.3 12.5 %collective-permute-start.1 = (f32[16,8,128]{2,1,0:T(8,128)S(1)}, f32[16,8,128]{2,1,0:T(8,128)S(1)}, u32[]{:S(2)}, u32[]{:S(2)}) collective-permute-start(f32[16,8,128]{2,1,0:T(8,128)S(1)} %all_to_all.55.near), channel_id=1, source_target_pairs={{0,1},{1,0},{2,3},{3,2},{4,5},{5,4},{6,7},{7,6},{8,9},{9,8},{10,11... | collective-permute-start | bytes 196616 | tf_op jit(solution)/shard_map/ppermute | solution.py:550
  118.8 10.0 %all-to-all-start.11 = ((f32[16,8,128]{2,1,0:T(8,128)}), f32[16,8,128]{2,1,0:T(8,128)S(1)}, u32[]{:S(2)}, u32[]{:S(2)}) async-start(f32[16,8,128]{2,1,0:T(8,128)} %shard_map.125), calls=%async_computation.11 | async-start | bytes 131072 | tf_op jit(solution)/shard_map/all_to_all | solution.py:546

commit v6 on v5

--- a/solution.py
+++ b/solution.py
@@ -14,6 +14,7 @@
 FIRST_ROOM = 256
 SECOND_ROOM = 128
 OWN_ROOM = 32
+CHUNK_ROWS = 14
 
 SOFTENING_SQ = 0.0001
 BASE_STEP = 0.5
@@ -214,7 +215,7 @@
     column_out[...] = column
     ahead, moving = predict(states, TIME_FIRST - last)
     ahead_second, moving_second = predict(states, TIME_SECOND - last)
-    row = jnp.concatenate([ahead, moving, weights, ahead_second, moving_second], axis=0)
+    row = rows_of([ahead, moving, weights, ahead_second, moving_second], CHUNK_ROWS)
     row = jnp.concatenate([row[:, at : at + LANES] for at in range(0, s_dev, LANES)], axis=0)
     for copy in range(row_out.shape[0]):
         row_out[copy] = row
@@ -391,26 +392,26 @@
     pl.when(count > tall_blocks * 16)(lambda: one_block(tall_blocks * 16, 8))
 
 
-def row_sums(count, near, far, first_row, turned_in, sums):
-    n_z, height, _ = near.shape
-    my_z = lax.axis_index("z")
+def row_sums(count, stars, first_row, turned_in, sums):
+    _, n_z, height, _ = stars.shape
+    my_z, my_core = lax.axis_index("z"), lax.axis_index("core")
     rows = [first_row + j for j in range(6)] + [6]
     sums[...] = jnp.zeros_like(sums)
 
     def visit(tall, target, key, running):
-        def segment(stars, which, running, own=False):
-            for chunk in range(height // 13):
-                at = chunk * 13
-                source = [jnp.broadcast_to(stars[which, at + j : at + j + 1, :], (tall, LANES)) for j in rows]
+        def segment(core, which, running, own=False):
+            for chunk in range(height // CHUNK_ROWS):
+                at = chunk * CHUNK_ROWS
+                source = [jnp.broadcast_to(stars[core, which, at + j : at + j + 1, :], (tall, LANES)) for j in rows]
                 place = (iota((tall, LANES), 1) + chunk * LANES).astype(jnp.float32) if own else None
                 running = added(running, pair_terms(source, target, place, key))
             return running
 
         def both(step, running):
-            return segment(near, jnp.where(step < my_z, step, step + 1), segment(far, step, running))
+            return segment(my_core, jnp.where(step < my_z, step, step + 1), segment(1 - my_core, step, running))
 
         running = lax.fori_loop(0, n_z - 1, both, running)
-        return segment(near, my_z, segment(far, n_z - 1, running), own=True)
+        return segment(my_core, my_z, segment(1 - my_core, n_z - 1, running), own=True)
 
     target_blocks(count, turned_in, sums, visit)
 
@@ -424,22 +425,23 @@
             force_out[copy, :, cut] = rows
 
 
-def first_force_kernel(info, near, far, turned_in, force_out, sums):
-    row_sums(info[0], near, far, 0, turned_in, sums)
+def first_force_kernel(info, stars, turned_in, force_out, sums):
+    row_sums(info[0], stars, 0, turned_in, sums)
     write_sums(sums, force_out)
 
 
-def second_force_kernel(info, near, far, turned_in, sums_out):
-    row_sums(info[0], near, far, 7, turned_in, sums_out)
-
-
-def update_force_kernel(info, near, far, turned_in, sums_in, force_out, sums, stars):
-    n_z = near.shape[0]
-    my_z = lax.axis_index("z")
+def second_force_kernel(info, stars, turned_in, sums_out):
+    row_sums(info[0], stars, 7, turned_in, sums_out)
+
+
+def update_force_kernel(info, updates, turned_in, sums_in, force_out, sums, stars):
+    n_z = updates.shape[1]
+    my_z, my_core = lax.axis_index("z"), lax.axis_index("core")
     half = iota((8, LANES), 1) < LANES // 2
+    own_half = half[7:8] == (my_core == 0)
     for z in range(n_z):
-        both = jnp.where(half, near[z], pltpu.roll(far[z], LANES // 2, axis=1))
-        place = jnp.where(half[7:8] & (my_z == z), both[7:8], -2.0)
+        both = jnp.where(half, updates[0, z], pltpu.roll(updates[1, z], LANES // 2, axis=1))
+        place = jnp.where(own_half & (my_z == z), both[7:8], -2.0)
         stars[z] = jnp.concatenate([both[0:7], place], axis=0)
     sums[...] = sums_in[...]
 
@@ -546,8 +548,8 @@
     return lax.all_to_all(copies, axis, split_axis=0, concat_axis=0, tiled=True)
 
 
-def other_core(near):
-    return lax.ppermute(near, "core", [(0, 1), (1, 0)])
+def both_cores(near):
+    return lax.all_gather(near, "core")
 
 
 def shards(positions, velocities, accels, jerks, masses, levels, active_first, active_second):
@@ -557,20 +559,20 @@
     scalar = jax.ShapeDtypeStruct((2,), jnp.int32)
     lists = (n_src, active_first.shape[0], active_second.shape[0])
     column, row_copies, own = call(
-        functools.partial(prepare_kernel, n_stars), (f32(16, s_dev), f32(n_z, 13 * s_dev // LANES, LANES), f32(16, s_dev)), 0, 8
+        functools.partial(prepare_kernel, n_stars), (f32(16, s_dev), f32(n_z, CHUNK_ROWS * s_dev // LANES, LANES), f32(16, s_dev)), 0, 8
     )(
         positions, velocities, accels, jerks, masses.reshape(1, s_dev), levels.reshape(1, s_dev),
         active_first.reshape(1, -1), active_second.reshape(1, -1),
     )
     near = exchanged(row_copies, "z")
     column = lax.all_gather(column, "tgt")
-    far = other_core(near)
+    stars = both_cores(near)
     target, columns, info = call(
         functools.partial(select_kernel, *lists), (f32(16, FIRST_ROOM), f32(FIRST_ROOM, LANES), scalar), 0, 1, smem_out=2
     )(column)
     (partial,) = call(
-        first_force_kernel, (f32(n_tgt, 8, FIRST_ROOM),), 1, 3, [pltpu.VMEM((FIRST_ROOM, LANES), jnp.float32)]
-    )(info, near, far, columns)
+        first_force_kernel, (f32(n_tgt, 8, FIRST_ROOM),), 1, 2, [pltpu.VMEM((FIRST_ROOM, LANES), jnp.float32)]
+    )(info, stars, columns)
     received = exchanged(partial, "tgt")
     second, plan, second_info = call(
         functools.partial(plan_kernel, *lists),
@@ -580,12 +582,12 @@
         correct_kernel, (f32(n_z, 8, LANES), f32(16, s_dev), f32(16, SECOND_ROOM), f32(LANES, LANES)), 0, 5
     )(received, target, second, plan, own)
     near_update = exchanged(update, "z")
-    (sums,) = call(second_force_kernel, (f32(SECOND_ROOM, LANES),), 1, 3)(second_info, near, far, second_columns)
-    far_update = other_core(near_update)
+    (sums,) = call(second_force_kernel, (f32(SECOND_ROOM, LANES),), 1, 2)(second_info, stars, second_columns)
+    updates = both_cores(near_update)
     (partial,) = call(
-        update_force_kernel, (f32(n_tgt, 8, SECOND_ROOM),), 1, 4,
+        update_force_kernel, (f32(n_tgt, 8, SECOND_ROOM),), 1, 3,
         [pltpu.VMEM((SECOND_ROOM, LANES), jnp.float32), pltpu.VMEM((n_z, 8, LANES), jnp.float32)],
-    )(second_info, near_update, far_update, second_columns, sums)
+    )(second_info, updates, second_columns, sums)
     received = exchanged(partial, "tgt")
 
     def by_columns(received, second, plan, own, *inputs):

time: 130 us -> 108 us (0.83)
  blocking collectives: 73 us -> 32.5 us
  starting transfers between devices: 26.4 us -> 35.3 us
  waiting for transfers between devices: 10.3 us -> 18.6 us
  Pallas kernels: 17.8 us -> 19.1 us
    all_to_all x2 -> x0, blocking collectives: 53.6 us -> none  [exchanged(): return lax.all_to_all(copies, axis, split_axis=0, concat_axis=0, tiled=True)]
    all_to_all x2 -> x4, starting transfers between devices: 8.2 us -> 35.3 us  [exchanged(): return lax.all_to_all(copies, axis, split_axis=0, concat_axis=0, tiled=True)]
    ppermute x2 -> x0, starting transfers between devices: 18.2 us -> none  [other_core(): return lax.ppermute(near, 'core', [(0, 1), (1, 0)])]
    all_gather x0 -> x2, blocking collectives: none -> 12.3 us  [both_cores(): return lax.all_gather(near, 'core')]
    all_to_all x2 -> x4, waiting for transfers between devices: 10.3 us -> 18.6 us  [exchanged(): return lax.all_to_all(copies, axis, split_axis=0, concat_axis=0, tiled=True)]
  transfers between devices with their start and end apart: 4 -> 4, of which waited for: 2 -> 3; matrix products, arithmetic and copies ran while one was open for 0% -> 1% of each run, Pallas kernels for 6% -> 7%
where the time goes in v6:
time: 108 us
  starting transfers between devices  35.3 us (33%)
  blocking collectives  32.5 us (30%)
  Pallas kernels  19.1 us (18%)
  waiting for transfers between devices  18.6 us (17%)
  between operations  1.45 us (1%)
    all_to_all x4, starting transfers between devices, exchanged(): return lax.all_to_all(copies, axis, split_axis=0, concat_axis=0, tiled=True)  35.3 us
    all_gather x1, blocking collectives, shards(): column = lax.all_gather(column, 'tgt')  20.2 us
    all_to_all x4, waiting for transfers between devices, exchanged(): return lax.all_to_all(copies, axis, split_axis=0, concat_axis=0, tiled=True)  18.6 us
    all_gather x2, blocking collectives, both_cores(): return lax.all_gather(near, 'core')  12.3 us
    pallas_call x1, Pallas kernels, shards(): call(first_force_kernel, (f32(n_tgt, 8, FIRST_ROOM),), 1, 2, [pltpu.VMEM(...  6.68 us
    pallas_call x1, Pallas kernels, shards(): call(second_force_kernel, (f32(SECOND_ROOM, LANES),), 1, 2)  3.32 us
    pallas_call x1, Pallas kernels, shards(): call(functools.partial(select_kernel, *lists), (f32(16, FIRST_ROOM), f32(...  2.23 us
  transfers between devices with their start and end apart: 4, of which 3 were waited for; matrix products, arithmetic and copies ran while one was open for 1% of the time, Pallas kernels for 7%

profile of v6, /device:TPU:1, one launch (start us, length us, event | category | flops | bytes accessed | tf_op | source)
XLA Modules:
  0.0 107.9 jit_solution(9402531248852354304)
XLA Ops:
  0.6 1.6 %shard_map.119 = (f32[16,512]{1,0:T(8,128)S(1)}, f32[16,56,128]{2,1,0:T(8,128)}, f32[16,512]{1,0:T(8,128)S(1)}) custom-call(f32[3,512]{1,0:T(4,128)} %pos.1, f32[3,512]{1,0:T(4,128)} %vel.1, f32[3,512]{1,0:T(4,128)} %acc.1, f32[3,512]{1,0:T(4,128)} %jerk.1, f32[1,512]{1,0:T(1,128)} %bitcast.122, s32[1,512]{1,0:T(1,128)} %bitcast.123, s32[1,256]{1,0:T(1,128)} %bitcast.126, ...), custom_call_target="tpu_custom_call" | custom-call | tf_op jit(solution)/shard_map/pallas_call | solution.py:561
  2.2 15.7 %all-to-all-start.8 = ((f32[16,56,128]{2,1,0:T(8,128)}), f32[16,56,128]{2,1,0:T(8,128)S(1)}, u32[]{:S(2)}, u32[]{:S(2)}) async-start(f32[16,56,128]{2,1,0:T(8,128)} %get-tuple-element.218), calls=%async_computation.8 | async-start | bytes 917504 | tf_op jit(solution)/shard_map/all_to_all | solution.py:548
  18.0 20.2 %all-gather = f32[256,512]{1,0:T(8,128)S(1)} all-gather(f32[16,512]{1,0:T(8,128)S(1)} %get-tuple-element.213), channel_id=2, replica_groups=mesh['tgt'=16,'z'=16,'core'=2] {'tgt'}, dimensions={0}, use_global_device_ids=true | all-gather | bytes 557056 | tf_op jit(solution)/shard_map/all_gather | solution.py:568
  38.1 0.0 copy-start.1
  38.2 0.0 copy-start.2
  38.2 0.0 copy-start.3
  38.2 0.0 copy-start.4
  38.2 0.0 copy-start.5
  38.2 0.0 copy-start.6
  38.2 0.0 copy-start.7
  38.2 2.2 %shard_map.120 = (f32[16,256]{1,0:T(8,128)S(1)}, f32[256,128]{1,0:T(8,128)S(1)}, s32[2]{0:T(128)S(1)}) custom-call(f32[16,16,512]{2,1,0:T(8,128)S(1)} %bitcast.91), custom_call_target="tpu_custom_call" | custom-call | tf_op jit(solution)/shard_map/pallas_call | solution.py:570
  40.5 0.0 all-to-all-done.8
  40.5 7.5 %all-gather.1 = f32[32,56,128]{2,1,0:T(8,128)S(1)} all-gather(f32[16,56,128]{2,1,0:T(8,128)S(1)} %all-to-all-done.8), channel_id=3, replica_groups=mesh['tgt'=16,'z'=16,'core'=2] {'core'}, dimensions={0}, use_global_device_ids=true | all-gather | bytes 1376256 | tf_op jit(solution)/shard_map/all_gather | solution.py:552
  48.0 6.7 %shard_map.122 = f32[16,8,256]{2,1,0:T(8,128)} custom-call(s32[2]{0:T(128)S(1)} %get-tuple-element.214.info, f32[2,16,56,128]{3,2,1,0:T(8,128)S(1)} %bitcast.89, f32[256,128]{1,0:T(8,128)S(1)} %get-tuple-element.216.turned_in), custom_call_target="tpu_custom_call" | custom-call | tf_op jit(solution)/shard_map/pallas_call | solution.py:573
  54.7 6.8 %all-to-all-start.9 = ((f32[16,8,256]{2,1,0:T(8,128)}), f32[16,8,256]{2,1,0:T(8,128)S(1)}, u32[]{:S(2)}, u32[]{:S(2)}) async-start(f32[16,8,256]{2,1,0:T(8,128)} %shard_map.122), calls=%async_computation.9 | async-start | bytes 262144 | tf_op jit(solution)/shard_map/all_to_all | solution.py:548
  61.5 1.8 %shard_map.121 = (f32[16,128]{1,0:T(8,128)S(1)}, s32[8,512]{1,0:T(8,128)S(1)}, s32[2]{0:T(128)S(1)}) custom-call(f32[16,16,512]{2,1,0:T(8,128)S(1)} %bitcast.92, f32[16,256]{1,0:T(8,128)S(1)} %get-tuple-element.215.first_target.target, f32[256,128]{1,0:T(8,128)S(1)} %get-tuple-element.216.turned_in), custom_call_target="tpu_custom_call" | custom-call | tf_op jit(solution)/shard_map/pallas_call | solution.py:577
  63.2 5.1 %all-to-all-done.9.received = f32[16,8,256]{2,1,0:T(8,128)S(1)} async-done(((f32[16,8,256]{2,1,0:T(8,128)}), f32[16,8,256]{2,1,0:T(8,128)S(1)}, u32[]{:S(2)}, u32[]{:S(2)}) %all-to-all-start.9) | async-done | bytes 131104 | tf_op jit(solution)/shard_map/all_to_all | solution.py:548
  68.3 0.8 shard_map.123
  69.1 9.3 %all-to-all-start.10 = ((f32[16,8,128]{2,1,0:T(8,128)}), f32[16,8,128]{2,1,0:T(8,128)S(1)}, u32[]{:S(2)}, u32[]{:S(2)}) async-start(f32[16,8,128]{2,1,0:T(8,128)} %get-tuple-element.222), calls=%async_computation.10 | async-start | bytes 131072 | tf_op jit(solution)/shard_map/all_to_all | solution.py:548
  78.5 3.3 %shard_map.124.sums_in = f32[128,128]{1,0:T(8,128)S(1)} custom-call(s32[2]{0:T(128)S(1)} %get-tuple-element.217.info, f32[2,16,56,128]{3,2,1,0:T(8,128)S(1)} %bitcast.90, f32[128,128]{1,0:T(8,128)S(1)} %get-tuple-element.223.turned_in), custom_call_target="tpu_custom_call" | custom-call | tf_op jit(solution)/shard_map/pallas_call | solution.py:585
  81.8 8.3 %all-to-all-done.10 = f32[16,8,128]{2,1,0:T(8,128)S(1)} async-done(((f32[16,8,128]{2,1,0:T(8,128)}), f32[16,8,128]{2,1,0:T(8,128)S(1)}, u32[]{:S(2)}, u32[]{:S(2)}) %all-to-all-start.10) | async-done | bytes 65568 | tf_op jit(solution)/shard_map/all_to_all | solution.py:548
  90.0 4.8 %all-gather.2 = f32[32,8,128]{2,1,0:T(8,128)S(1)} all-gather(f32[16,8,128]{2,1,0:T(8,128)S(1)} %all-to-all-done.10), channel_id=4, replica_groups=mesh['tgt'=16,'z'=16,'core'=2] {'core'}, dimensions={0}, use_global_device_ids=true | all-gather | bytes 196608 | tf_op jit(solution)/shard_map/all_gather | solution.py:552
  94.8 2.0 %shard_map.125 = f32[16,8,128]{2,1,0:T(8,128)} custom-call(s32[2]{0:T(128)S(1)} %get-tuple-element.217.info, f32[2,16,8,128]{3,2,1,0:T(8,128)S(1)} %bitcast.93, f32[128,128]{1,0:T(8,128)S(1)} %get-tuple-element.223.turned_in, f32[128,128]{1,0:T(8,128)S(1)} %shard_map.124.sums_in), custom_call_target="tpu_custom_call" | custom-call | tf_op jit(solution)/shard_map/pallas_call | solution.py:587
  96.8 3.5 %all-to-all-start.11 = ((f32[16,8,128]{2,1,0:T(8,128)}), f32[16,8,128]{2,1,0:T(8,128)S(1)}, u32[]{:S(2)}, u32[]{:S(2)}) async-start(f32[16,8,128]{2,1,0:T(8,128)} %shard_map.125), calls=%async_computation.11 | async-start | bytes 131072 | tf_op jit(solution)/shard_map/all_to_all | solution.py:548
  100.3 0.6 slice.199
  101.5 5.3 %all-to-all-done.11 = f32[16,8,128]{2,1,0:T(8,128)S(1)} async-done(((f32[16,8,128]{2,1,0:T(8,128)}), f32[16,8,128]{2,1,0:T(8,128)S(1)}, u32[]{:S(2)}, u32[]{:S(2)}) %all-to-all-start.11) | async-done | bytes 65568 | tf_op jit(solution)/shard_map/all_to_all | solution.py:548
  106.9 0.0 copy-done.2
  106.9 0.0 copy-done.3
  106.9 0.0 copy-done.4
  106.9 0.0 copy-done.5
  106.9 1.0 conditional.1
  107.2 0.7 branch_1_fun.1
  (5 shorter events, 0.0 us)
Async XLA Ops:
  2.2 38.2 %all-to-all-start.8 = ((f32[16,56,128]{2,1,0:T(8,128)}), f32[16,56,128]{2,1,0:T(8,128)S(1)}, u32[]{:S(2)}, u32[]{:S(2)}) async-start(f32[16,56,128]{2,1,0:T(8,128)} %get-tuple-element.218), calls=%async_computation.8 | async-start | bytes 917504 | tf_op jit(solution)/shard_map/all_to_all | solution.py:548
  38.1 68.7 %copy-start = (f32[3,512]{1,0:T(4,128)S(1)}, f32[3,512]{1,0:T(4,128)}, u32[]{:S(2)}) copy-start(f32[3,512]{1,0:T(4,128)} %pos.1) | copy-start | bytes 18436
  38.1 68.7 %copy-start.1 = (f32[3,512]{1,0:T(4,128)S(1)}, f32[3,512]{1,0:T(4,128)}, u32[]{:S(2)}) copy-start(f32[3,512]{1,0:T(4,128)} %vel.1) | copy-start | bytes 18436
  38.2 68.7 %copy-start.2 = (f32[3,512]{1,0:T(4,128)S(1)}, f32[3,512]{1,0:T(4,128)}, u32[]{:S(2)}) copy-start(f32[3,512]{1,0:T(4,128)} %acc.1) | copy-start | bytes 18436
  38.2 68.7 %copy-start.3 = (f32[3,512]{1,0:T(4,128)S(1)}, f32[3,512]{1,0:T(4,128)}, u32[]{:S(2)}) copy-start(f32[3,512]{1,0:T(4,128)} %jerk.1) | copy-start | bytes 18436
  38.2 68.7 %copy-start.4 = (f32[512]{0:T(512)S(1)}, f32[512]{0:T(512)}, u32[]{:S(2)}) copy-start(f32[512]{0:T(512)} %param.22) | copy-start | bytes 6148
  38.2 68.7 %copy-start.5 = (s32[512]{0:T(512)S(1)}, s32[512]{0:T(512)}, u32[]{:S(2)}) copy-start(s32[512]{0:T(512)} %param.23) | copy-start | bytes 6148
  38.2 68.7 %copy-start.6 = (s32[256]{0:T(256)S(1)}, s32[256]{0:T(256)}, u32[]{:S(2)}) copy-start(s32[256]{0:T(256)} %param.24) | copy-start | bytes 3076
  38.2 68.7 %copy-start.7 = (s32[128]{0:T(128)S(1)}, s32[128]{0:T(128)}, u32[]{:S(2)}) copy-start(s32[128]{0:T(128)} %param.25) | copy-start | bytes 1540
  54.7 13.6 %all-to-all-start.9 = ((f32[16,8,256]{2,1,0:T(8,128)}), f32[16,8,256]{2,1,0:T(8,128)S(1)}, u32[]{:S(2)}, u32[]{:S(2)}) async-start(f32[16,8,256]{2,1,0:T(8,128)} %shard_map.122), calls=%async_computation.9 | async-start | bytes 262144 | tf_op jit(solution)/shard_map/all_to_all | solution.py:548
  69.1 20.9 %all-to-all-start.10 = ((f32[16,8,128]{2,1,0:T(8,128)}), f32[16,8,128]{2,1,0:T(8,128)S(1)}, u32[]{:S(2)}, u32[]{:S(2)}) async-start(f32[16,8,128]{2,1,0:T(8,128)} %get-tuple-element.222), calls=%async_computation.10 | async-start | bytes 131072 | tf_op jit(solution)/shard_map/all_to_all | solution.py:548
  96.8 10.1 %all-to-all-start.11 = ((f32[16,8,128]{2,1,0:T(8,128)}), f32[16,8,128]{2,1,0:T(8,128)S(1)}, u32[]{:S(2)}, u32[]{:S(2)}) async-start(f32[16,8,128]{2,1,0:T(8,128)} %shard_map.125), calls=%async_computation.11 | async-start | bytes 131072 | tf_op jit(solution)/shard_map/all_to_all | solution.py:548

commit v7 on v6

--- a/solution.py
+++ b/solution.py
@@ -222,7 +222,12 @@
     own_out[...] = rows_of([states, last, weights], 16)
 
 
-def matching_slots(listed, column, n_src, s_dev):
+def in_column(listed, column, n_src, s_dev):
+    ids = listed.astype(jnp.int32)
+    return (ids >= 0) & (((ids >> log2_of(s_dev)) & (n_src - 1)) == column)
+
+
+def most_listed(listed, n_src, s_dev):
     ids = listed.astype(jnp.int32)
     n_tgt, width = ids.shape
     valid = ids >= 0
@@ -231,11 +236,11 @@
     cells = jnp.zeros((n_tgt, n_src), jnp.float32)
     for slots in range(n_tgt):
         in_row = (row_of[slots : slots + 1] == iota((n_tgt, width), 0)).astype(jnp.bfloat16)
-        in_column = (column_of[slots : slots + 1] == iota((n_src, width), 0)).astype(jnp.bfloat16)
+        in_col = (column_of[slots : slots + 1] == iota((n_src, width), 0)).astype(jnp.bfloat16)
         cells = cells + lax.dot_general(
-            in_row, in_column, (((1,), (1,)), ((), ())), preferred_element_type=jnp.float32
+            in_row, in_col, (((1,), (1,)), ((), ())), preferred_element_type=jnp.float32
         )
-    return column_of == column, jnp.max(jnp.sum(cells, axis=0, keepdims=True)), jnp.max(cells)
+    return jnp.max(jnp.sum(cells, axis=0, keepdims=True)), jnp.max(cells)
 
 
 def slot_numbers(mine):
@@ -287,14 +292,11 @@
     s_dev = held.shape[2]
     my_row, my_column = lax.axis_index("tgt"), lax.axis_index(SRC)
     listed = held[:, 13, :]
-    first, second = listed[:, :slots_first], listed[:, slots_first : slots_first + slots_second]
-    mine, most_first, most_own = matching_slots(first, my_column, n_src, s_dev)
-    _, most_second, _ = matching_slots(second, my_column, n_src, s_dev)
-    slot, count = slot_numbers(mine)
+    first = listed[:, :slots_first]
+    slot, count = slot_numbers(in_column(first, my_column, n_src, s_dev))
     count = jnp.minimum(count.astype(jnp.int32), FIRST_ROOM)
     info_out[0] = count
-    fits = (most_first <= FIRST_ROOM) & (most_second <= SECOND_ROOM) & (most_own <= OWN_ROOM)
-    info_out[1] = fits.astype(jnp.int32)
+    info_out[1] = 0
 
     def fill(part):
         facts = target_facts(packed_ids(first, slot, part), held, my_row, n_src)
@@ -325,10 +327,13 @@
 def plan_kernel(n_src, slots_first, slots_second, held, first_target, turned_in, second_out, plan_out, info_out):
     s_dev = held.shape[2]
     my_row, my_column = lax.axis_index("tgt"), lax.axis_index(SRC)
-    listed = held[:, 13, slots_first : slots_first + slots_second]
-    ids = listed.astype(jnp.int32)
-    mine = (ids >= 0) & (((ids >> log2_of(s_dev)) & (n_src - 1)) == my_column)
-    slot, count = slot_numbers(mine)
+    lists = held[:, 13, :]
+    first, listed = lists[:, :slots_first], lists[:, slots_first : slots_first + slots_second]
+    most_first, most_own = most_listed(first, n_src, s_dev)
+    most_second, _ = most_listed(listed, n_src, s_dev)
+    fits = (most_first <= FIRST_ROOM) & (most_second <= SECOND_ROOM) & (most_own <= OWN_ROOM)
+    info_out[1] = fits.astype(jnp.int32)
+    slot, count = slot_numbers(in_column(listed, my_column, n_src, s_dev))
     info_out[0] = jnp.minimum(count.astype(jnp.int32), SECOND_ROOM)
     facts = target_facts(packed_ids(listed, slot, 0), held, my_row, n_src)
     second_out[...] = facts
@@ -597,7 +602,7 @@
         return whole_program(*inputs)
 
     inputs = (positions, velocities, accels, jerks, masses, levels, active_first, active_second)
-    return lax.cond(info[1] == 1, by_columns, anywhere, received, second, plan, own, *inputs)
+    return lax.cond(second_info[1] == 1, by_columns, anywhere, received, second, plan, own, *inputs)
 
 
 def solution(mesh):

time: 108 us -> 108 us (level)
  no operation moved by 1% of the time
where the time goes in v7:
time: 108 us
  starting transfers between devices  35.2 us (33%)
  blocking collectives  32.6 us (30%)
  Pallas kernels  19.1 us (18%)
  waiting for transfers between devices  18.5 us (17%)
  between operations  1.45 us (1%)
    all_to_all x4, starting transfers between devices, exchanged(): return lax.all_to_all(copies, axis, split_axis=0, concat_axis=0, tiled=True)  35.2 us
    all_gather x1, blocking collectives, shards(): column = lax.all_gather(column, 'tgt')  20.2 us
    all_to_all x4, waiting for transfers between devices, exchanged(): return lax.all_to_all(copies, axis, split_axis=0, concat_axis=0, tiled=True)  18.5 us
    all_gather x2, blocking collectives, both_cores(): return lax.all_gather(near, 'core')  12.4 us
    pallas_call x1, Pallas kernels, shards(): call(first_force_kernel, (f32(n_tgt, 8, FIRST_ROOM),), 1, 2, [pltpu.VMEM(...  6.68 us
    pallas_call x1, Pallas kernels, shards(): call(second_force_kernel, (f32(SECOND_ROOM, LANES),), 1, 2)  3.32 us
  transfers between devices with their start and end apart: 4, of which 3 were waited for; matrix products, arithmetic and copies ran while one was open for 1% of the time, Pallas kernels for 7%

profile of v7, /device:TPU:1, one launch (start us, length us, event | category | flops | bytes accessed | tf_op | source)
XLA Modules:
  0.0 107.8 jit_solution(14955901368334500663)
XLA Ops:
  0.6 1.6 %shard_map.119 = (f32[16,512]{1,0:T(8,128)S(1)}, f32[16,56,128]{2,1,0:T(8,128)}, f32[16,512]{1,0:T(8,128)S(1)}) custom-call(f32[3,512]{1,0:T(4,128)} %pos.1, f32[3,512]{1,0:T(4,128)} %vel.1, f32[3,512]{1,0:T(4,128)} %acc.1, f32[3,512]{1,0:T(4,128)} %jerk.1, f32[1,512]{1,0:T(1,128)} %bitcast.122, s32[1,512]{1,0:T(1,128)} %bitcast.123, s32[1,256]{1,0:T(1,128)} %bitcast.126, ...), custom_call_target="tpu_custom_call" | custom-call | tf_op jit(solution)/shard_map/pallas_call | solution.py:566
  2.2 15.7 %all-to-all-start.8 = ((f32[16,56,128]{2,1,0:T(8,128)}), f32[16,56,128]{2,1,0:T(8,128)S(1)}, u32[]{:S(2)}, u32[]{:S(2)}) async-start(f32[16,56,128]{2,1,0:T(8,128)} %get-tuple-element.218), calls=%async_computation.8 | async-start | bytes 917504 | tf_op jit(solution)/shard_map/all_to_all | solution.py:553
  18.0 20.2 %all-gather = f32[256,512]{1,0:T(8,128)S(1)} all-gather(f32[16,512]{1,0:T(8,128)S(1)} %get-tuple-element.213), channel_id=2, replica_groups=mesh['tgt'=16,'z'=16,'core'=2] {'tgt'}, dimensions={0}, use_global_device_ids=true | all-gather | bytes 557056 | tf_op jit(solution)/shard_map/all_gather | solution.py:573
  38.1 0.0 copy-start.1
  38.2 0.0 copy-start.2
  38.2 0.0 copy-start.3
  38.2 0.0 copy-start.4
  38.2 0.0 copy-start.5
  38.2 0.0 copy-start.6
  38.2 0.0 copy-start.7
  38.2 2.1 %shard_map.120 = (f32[16,256]{1,0:T(8,128)S(1)}, f32[256,128]{1,0:T(8,128)S(1)}, s32[2]{0:T(128)S(1)}) custom-call(f32[16,16,512]{2,1,0:T(8,128)S(1)} %bitcast.91), custom_call_target="tpu_custom_call" | custom-call | tf_op jit(solution)/shard_map/pallas_call | solution.py:575
  40.4 0.0 all-to-all-done.8
  40.4 7.6 %all-gather.1 = f32[32,56,128]{2,1,0:T(8,128)S(1)} all-gather(f32[16,56,128]{2,1,0:T(8,128)S(1)} %all-to-all-done.8), channel_id=3, replica_groups=mesh['tgt'=16,'z'=16,'core'=2] {'core'}, dimensions={0}, use_global_device_ids=true | all-gather | bytes 1376256 | tf_op jit(solution)/shard_map/all_gather | solution.py:557
  48.0 6.7 %shard_map.122 = f32[16,8,256]{2,1,0:T(8,128)} custom-call(s32[2]{0:T(128)S(1)} %get-tuple-element.217.info, f32[2,16,56,128]{3,2,1,0:T(8,128)S(1)} %bitcast.89, f32[256,128]{1,0:T(8,128)S(1)} %get-tuple-element.215.turned_in), custom_call_target="tpu_custom_call" | custom-call | tf_op jit(solution)/shard_map/pallas_call | solution.py:578
  54.7 6.8 %all-to-all-start.9 = ((f32[16,8,256]{2,1,0:T(8,128)}), f32[16,8,256]{2,1,0:T(8,128)S(1)}, u32[]{:S(2)}, u32[]{:S(2)}) async-start(f32[16,8,256]{2,1,0:T(8,128)} %shard_map.122), calls=%async_computation.9 | async-start | bytes 262144 | tf_op jit(solution)/shard_map/all_to_all | solution.py:553
  61.5 1.9 %shard_map.121 = (f32[16,128]{1,0:T(8,128)S(1)}, s32[8,512]{1,0:T(8,128)S(1)}, s32[2]{0:T(128)S(1)}) custom-call(f32[16,16,512]{2,1,0:T(8,128)S(1)} %bitcast.92, f32[16,256]{1,0:T(8,128)S(1)} %get-tuple-element.214.first_target.target, f32[256,128]{1,0:T(8,128)S(1)} %get-tuple-element.215.turned_in), custom_call_target="tpu_custom_call" | custom-call | tf_op jit(solution)/shard_map/pallas_call | solution.py:582
  63.3 5.0 %all-to-all-done.9.received = f32[16,8,256]{2,1,0:T(8,128)S(1)} async-done(((f32[16,8,256]{2,1,0:T(8,128)}), f32[16,8,256]{2,1,0:T(8,128)S(1)}, u32[]{:S(2)}, u32[]{:S(2)}) %all-to-all-start.9) | async-done | bytes 131104 | tf_op jit(solution)/shard_map/all_to_all | solution.py:553
  68.3 0.8 shard_map.123
  69.1 9.2 %all-to-all-start.10 = ((f32[16,8,128]{2,1,0:T(8,128)}), f32[16,8,128]{2,1,0:T(8,128)S(1)}, u32[]{:S(2)}, u32[]{:S(2)}) async-start(f32[16,8,128]{2,1,0:T(8,128)} %get-tuple-element.222), calls=%async_computation.10 | async-start | bytes 131072 | tf_op jit(solution)/shard_map/all_to_all | solution.py:553
  78.3 3.3 %shard_map.124.sums_in = f32[128,128]{1,0:T(8,128)S(1)} custom-call(s32[2]{0:T(128)S(1)} %get-tuple-element.216.info, f32[2,16,56,128]{3,2,1,0:T(8,128)S(1)} %bitcast.90, f32[128,128]{1,0:T(8,128)S(1)} %get-tuple-element.223.turned_in), custom_call_target="tpu_custom_call" | custom-call | tf_op jit(solution)/shard_map/pallas_call | solution.py:590
  81.7 8.3 %all-to-all-done.10 = f32[16,8,128]{2,1,0:T(8,128)S(1)} async-done(((f32[16,8,128]{2,1,0:T(8,128)}), f32[16,8,128]{2,1,0:T(8,128)S(1)}, u32[]{:S(2)}, u32[]{:S(2)}) %all-to-all-start.10) | async-done | bytes 65568 | tf_op jit(solution)/shard_map/all_to_all | solution.py:553
  89.9 4.8 %all-gather.2 = f32[32,8,128]{2,1,0:T(8,128)S(1)} all-gather(f32[16,8,128]{2,1,0:T(8,128)S(1)} %all-to-all-done.10), channel_id=4, replica_groups=mesh['tgt'=16,'z'=16,'core'=2] {'core'}, dimensions={0}, use_global_device_ids=true | all-gather | bytes 196608 | tf_op jit(solution)/shard_map/all_gather | solution.py:557
  94.7 2.0 %shard_map.125 = f32[16,8,128]{2,1,0:T(8,128)} custom-call(s32[2]{0:T(128)S(1)} %get-tuple-element.216.info, f32[2,16,8,128]{3,2,1,0:T(8,128)S(1)} %bitcast.93, f32[128,128]{1,0:T(8,128)S(1)} %get-tuple-element.223.turned_in, f32[128,128]{1,0:T(8,128)S(1)} %shard_map.124.sums_in), custom_call_target="tpu_custom_call" | custom-call | tf_op jit(solution)/shard_map/pallas_call | solution.py:592
  96.7 3.5 %all-to-all-start.11 = ((f32[16,8,128]{2,1,0:T(8,128)}), f32[16,8,128]{2,1,0:T(8,128)S(1)}, u32[]{:S(2)}, u32[]{:S(2)}) async-start(f32[16,8,128]{2,1,0:T(8,128)} %shard_map.125), calls=%async_computation.11 | async-start | bytes 131072 | tf_op jit(solution)/shard_map/all_to_all | solution.py:553
  100.2 0.6 slice.199
  101.4 5.3 %all-to-all-done.11 = f32[16,8,128]{2,1,0:T(8,128)S(1)} async-done(((f32[16,8,128]{2,1,0:T(8,128)}), f32[16,8,128]{2,1,0:T(8,128)S(1)}, u32[]{:S(2)}, u32[]{:S(2)}) %all-to-all-start.11) | async-done | bytes 65568 | tf_op jit(solution)/shard_map/all_to_all | solution.py:553
  106.7 0.0 copy-done
  106.7 0.0 copy-done.1
  106.7 0.0 copy-done.2
  106.8 0.0 copy-done.3
  106.8 1.0 conditional.1
  107.0 0.7 branch_1_fun.1
  (5 shorter events, 0.0 us)
Async XLA Ops:
  2.2 38.1 %all-to-all-start.8 = ((f32[16,56,128]{2,1,0:T(8,128)}), f32[16,56,128]{2,1,0:T(8,128)S(1)}, u32[]{:S(2)}, u32[]{:S(2)}) async-start(f32[16,56,128]{2,1,0:T(8,128)} %get-tuple-element.218), calls=%async_computation.8 | async-start | bytes 917504 | tf_op jit(solution)/shard_map/all_to_all | solution.py:553
  38.1 68.6 %copy-start = (f32[3,512]{1,0:T(4,128)S(1)}, f32[3,512]{1,0:T(4,128)}, u32[]{:S(2)}) copy-start(f32[3,512]{1,0:T(4,128)} %pos.1) | copy-start | bytes 18436
  38.1 68.6 %copy-start.1 = (f32[3,512]{1,0:T(4,128)S(1)}, f32[3,512]{1,0:T(4,128)}, u32[]{:S(2)}) copy-start(f32[3,512]{1,0:T(4,128)} %vel.1) | copy-start | bytes 18436
  38.2 68.6 %copy-start.2 = (f32[3,512]{1,0:T(4,128)S(1)}, f32[3,512]{1,0:T(4,128)}, u32[]{:S(2)}) copy-start(f32[3,512]{1,0:T(4,128)} %acc.1) | copy-start | bytes 18436
  38.2 68.6 %copy-start.3 = (f32[3,512]{1,0:T(4,128)S(1)}, f32[3,512]{1,0:T(4,128)}, u32[]{:S(2)}) copy-start(f32[3,512]{1,0:T(4,128)} %jerk.1) | copy-start | bytes 18436
  38.2 68.6 %copy-start.4 = (f32[512]{0:T(512)S(1)}, f32[512]{0:T(512)}, u32[]{:S(2)}) copy-start(f32[512]{0:T(512)} %param.22) | copy-start | bytes 6148
  38.2 68.6 %copy-start.5 = (s32[512]{0:T(512)S(1)}, s32[512]{0:T(512)}, u32[]{:S(2)}) copy-start(s32[512]{0:T(512)} %param.23) | copy-start | bytes 6148
  38.2 68.6 %copy-start.6 = (s32[256]{0:T(256)S(1)}, s32[256]{0:T(256)}, u32[]{:S(2)}) copy-start(s32[256]{0:T(256)} %param.24) | copy-start | bytes 3076
  38.2 68.6 %copy-start.7 = (s32[128]{0:T(128)S(1)}, s32[128]{0:T(128)}, u32[]{:S(2)}) copy-start(s32[128]{0:T(128)} %param.25) | copy-start | bytes 1540
  54.7 13.6 %all-to-all-start.9 = ((f32[16,8,256]{2,1,0:T(8,128)}), f32[16,8,256]{2,1,0:T(8,128)S(1)}, u32[]{:S(2)}, u32[]{:S(2)}) async-start(f32[16,8,256]{2,1,0:T(8,128)} %shard_map.122), calls=%async_computation.9 | async-start | bytes 262144 | tf_op jit(solution)/shard_map/all_to_all | solution.py:553
  69.1 20.8 %all-to-all-start.10 = ((f32[16,8,128]{2,1,0:T(8,128)}), f32[16,8,128]{2,1,0:T(8,128)S(1)}, u32[]{:S(2)}, u32[]{:S(2)}) async-start(f32[16,8,128]{2,1,0:T(8,128)} %get-tuple-element.222), calls=%async_computation.10 | async-start | bytes 131072 | tf_op jit(solution)/shard_map/all_to_all | solution.py:553
  96.7 10.1 %all-to-all-start.11 = ((f32[16,8,128]{2,1,0:T(8,128)}), f32[16,8,128]{2,1,0:T(8,128)S(1)}, u32[]{:S(2)}, u32[]{:S(2)}) async-start(f32[16,8,128]{2,1,0:T(8,128)} %shard_map.125), calls=%async_computation.11 | async-start | bytes 131072 | tf_op jit(solution)/shard_map/all_to_all | solution.py:553

commit v8 on v7

--- a/solution.py
+++ b/solution.py
@@ -445,7 +445,7 @@
     half = iota((8, LANES), 1) < LANES // 2
     own_half = half[7:8] == (my_core == 0)
     for z in range(n_z):
-        both = jnp.where(half, updates[0, z], pltpu.roll(updates[1, z], LANES // 2, axis=1))
+        both = updates[0, z] + updates[1, z]
         place = jnp.where(own_half & (my_z == z), both[7:8], -2.0)
         stars[z] = jnp.concatenate([both[0:7], place], axis=0)
     sums[...] = sums_in[...]
@@ -455,7 +455,7 @@
             source = [jnp.broadcast_to(stars[z, j : j + 1, :], (tall, LANES)) for j in range(8)]
             return added(running, pair_terms(source, target, source[7], key))
 
-        return lax.fori_loop(0, n_z, one, running, unroll=4)
+        return lax.fori_loop(0, n_z, one, running, unroll=8 if n_z % 8 == 0 else 1)
 
     target_blocks(info[0], turned_in, sums, visit)
     write_sums(sums, force_out)
@@ -499,6 +499,7 @@
     lane = iota((8, LANES), 1)
     update = jnp.where(lane < OWN_ROOM, arrived, pltpu.roll(left, OWN_ROOM, axis=1))
     update = jnp.where(lane < 2 * OWN_ROOM, update, 0.0)
+    update = jnp.where(lax.axis_index("core") == 0, update, pltpu.roll(update, LANES // 2, axis=1))
     for copy in range(copies):
         update_out[copy] = update
     for chunk in range(s_dev // LANES):

time: 108 us -> 108 us (level)
  no operation moved by 1% of the time
where the time goes in v8:
time: 108 us
  starting transfers between devices  35.2 us (33%)
  blocking collectives  32.6 us (30%)
  Pallas kernels  19.1 us (18%)
  waiting for transfers between devices  18.5 us (17%)
  between operations  1.45 us (1%)
    all_to_all x4, starting transfers between devices, exchanged(): return lax.all_to_all(copies, axis, split_axis=0, concat_axis=0, tiled=True)  35.2 us
    all_gather x1, blocking collectives, shards(): column = lax.all_gather(column, 'tgt')  20.2 us
    all_to_all x4, waiting for transfers between devices, exchanged(): return lax.all_to_all(copies, axis, split_axis=0, concat_axis=0, tiled=True)  18.5 us
    all_gather x2, blocking collectives, both_cores(): return lax.all_gather(near, 'core')  12.4 us
    pallas_call x1, Pallas kernels, shards(): call(first_force_kernel, (f32(n_tgt, 8, FIRST_ROOM),), 1, 2, [pltpu.VMEM(...  6.68 us
    pallas_call x1, Pallas kernels, shards(): call(second_force_kernel, (f32(SECOND_ROOM, LANES),), 1, 2)  3.32 us
  transfers between devices with their start and end apart: 4, of which 3 were waited for; matrix products, arithmetic and copies ran while one was open for 1% of the time, Pallas kernels for 7%

profile of v8, /device:TPU:1, one launch (start us, length us, event | category | flops | bytes accessed | tf_op | source)
XLA Modules:
  0.0 107.7 jit_solution(10230448695383438064)
XLA Ops:
  0.6 1.6 %shard_map.119 = (f32[16,512]{1,0:T(8,128)S(1)}, f32[16,56,128]{2,1,0:T(8,128)}, f32[16,512]{1,0:T(8,128)S(1)}) custom-call(f32[3,512]{1,0:T(4,128)} %pos.1, f32[3,512]{1,0:T(4,128)} %vel.1, f32[3,512]{1,0:T(4,128)} %acc.1, f32[3,512]{1,0:T(4,128)} %jerk.1, f32[1,512]{1,0:T(1,128)} %bitcast.122, s32[1,512]{1,0:T(1,128)} %bitcast.123, s32[1,256]{1,0:T(1,128)} %bitcast.126, ...), custom_call_target="tpu_custom_call" | custom-call | tf_op jit(solution)/shard_map/pallas_call | solution.py:567
  2.2 15.7 %all-to-all-start.8 = ((f32[16,56,128]{2,1,0:T(8,128)}), f32[16,56,128]{2,1,0:T(8,128)S(1)}, u32[]{:S(2)}, u32[]{:S(2)}) async-start(f32[16,56,128]{2,1,0:T(8,128)} %get-tuple-element.218), calls=%async_computation.8 | async-start | bytes 917504 | tf_op jit(solution)/shard_map/all_to_all | solution.py:554
  18.0 20.2 %all-gather = f32[256,512]{1,0:T(8,128)S(1)} all-gather(f32[16,512]{1,0:T(8,128)S(1)} %get-tuple-element.213), channel_id=2, replica_groups=mesh['tgt'=16,'z'=16,'core'=2] {'tgt'}, dimensions={0}, use_global_device_ids=true | all-gather | bytes 557056 | tf_op jit(solution)/shard_map/all_gather | solution.py:574
  38.1 0.0 copy-start.1
  38.2 0.0 copy-start.2
  38.2 0.0 copy-start.3
  38.2 0.0 copy-start.4
  38.2 0.0 copy-start.5
  38.2 0.0 copy-start.6
  38.2 0.0 copy-start.7
  38.2 2.1 %shard_map.120 = (f32[16,256]{1,0:T(8,128)S(1)}, f32[256,128]{1,0:T(8,128)S(1)}, s32[2]{0:T(128)S(1)}) custom-call(f32[16,16,512]{2,1,0:T(8,128)S(1)} %bitcast.91), custom_call_target="tpu_custom_call" | custom-call | tf_op jit(solution)/shard_map/pallas_call | solution.py:576
  40.4 0.0 all-to-all-done.8
  40.4 7.6 %all-gather.1 = f32[32,56,128]{2,1,0:T(8,128)S(1)} all-gather(f32[16,56,128]{2,1,0:T(8,128)S(1)} %all-to-all-done.8), channel_id=3, replica_groups=mesh['tgt'=16,'z'=16,'core'=2] {'core'}, dimensions={0}, use_global_device_ids=true | all-gather | bytes 1376256 | tf_op jit(solution)/shard_map/all_gather | solution.py:558
  48.0 6.7 %shard_map.122 = f32[16,8,256]{2,1,0:T(8,128)} custom-call(s32[2]{0:T(128)S(1)} %get-tuple-element.217.info, f32[2,16,56,128]{3,2,1,0:T(8,128)S(1)} %bitcast.89, f32[256,128]{1,0:T(8,128)S(1)} %get-tuple-element.215.turned_in), custom_call_target="tpu_custom_call" | custom-call | tf_op jit(solution)/shard_map/pallas_call | solution.py:579
  54.7 6.8 %all-to-all-start.9 = ((f32[16,8,256]{2,1,0:T(8,128)}), f32[16,8,256]{2,1,0:T(8,128)S(1)}, u32[]{:S(2)}, u32[]{:S(2)}) async-start(f32[16,8,256]{2,1,0:T(8,128)} %shard_map.122), calls=%async_computation.9 | async-start | bytes 262144 | tf_op jit(solution)/shard_map/all_to_all | solution.py:554
  61.5 1.9 %shard_map.121 = (f32[16,128]{1,0:T(8,128)S(1)}, s32[8,512]{1,0:T(8,128)S(1)}, s32[2]{0:T(128)S(1)}) custom-call(f32[16,16,512]{2,1,0:T(8,128)S(1)} %bitcast.92, f32[16,256]{1,0:T(8,128)S(1)} %get-tuple-element.214.first_target.target, f32[256,128]{1,0:T(8,128)S(1)} %get-tuple-element.215.turned_in), custom_call_target="tpu_custom_call" | custom-call | tf_op jit(solution)/shard_map/pallas_call | solution.py:583
  63.3 5.0 %all-to-all-done.9.received = f32[16,8,256]{2,1,0:T(8,128)S(1)} async-done(((f32[16,8,256]{2,1,0:T(8,128)}), f32[16,8,256]{2,1,0:T(8,128)S(1)}, u32[]{:S(2)}, u32[]{:S(2)}) %all-to-all-start.9) | async-done | bytes 131104 | tf_op jit(solution)/shard_map/all_to_all | solution.py:554
  68.3 0.8 shard_map.123
  69.1 9.2 %all-to-all-start.10 = ((f32[16,8,128]{2,1,0:T(8,128)}), f32[16,8,128]{2,1,0:T(8,128)S(1)}, u32[]{:S(2)}, u32[]{:S(2)}) async-start(f32[16,8,128]{2,1,0:T(8,128)} %get-tuple-element.222), calls=%async_computation.10 | async-start | bytes 131072 | tf_op jit(solution)/shard_map/all_to_all | solution.py:554
  78.4 3.3 %shard_map.124.sums_in = f32[128,128]{1,0:T(8,128)S(1)} custom-call(s32[2]{0:T(128)S(1)} %get-tuple-element.216.info, f32[2,16,56,128]{3,2,1,0:T(8,128)S(1)} %bitcast.90, f32[128,128]{1,0:T(8,128)S(1)} %get-tuple-element.223.turned_in), custom_call_target="tpu_custom_call" | custom-call | tf_op jit(solution)/shard_map/pallas_call | solution.py:591
  81.7 8.3 %all-to-all-done.10 = f32[16,8,128]{2,1,0:T(8,128)S(1)} async-done(((f32[16,8,128]{2,1,0:T(8,128)}), f32[16,8,128]{2,1,0:T(8,128)S(1)}, u32[]{:S(2)}, u32[]{:S(2)}) %all-to-all-start.10) | async-done | bytes 65568 | tf_op jit(solution)/shard_map/all_to_all | solution.py:554
  89.9 4.8 %all-gather.2 = f32[32,8,128]{2,1,0:T(8,128)S(1)} all-gather(f32[16,8,128]{2,1,0:T(8,128)S(1)} %all-to-all-done.10), channel_id=4, replica_groups=mesh['tgt'=16,'z'=16,'core'=2] {'core'}, dimensions={0}, use_global_device_ids=true | all-gather | bytes 196608 | tf_op jit(solution)/shard_map/all_gather | solution.py:558
  94.7 1.9 %shard_map.125 = f32[16,8,128]{2,1,0:T(8,128)} custom-call(s32[2]{0:T(128)S(1)} %get-tuple-element.216.info, f32[2,16,8,128]{3,2,1,0:T(8,128)S(1)} %bitcast.93, f32[128,128]{1,0:T(8,128)S(1)} %get-tuple-element.223.turned_in, f32[128,128]{1,0:T(8,128)S(1)} %shard_map.124.sums_in), custom_call_target="tpu_custom_call" | custom-call | tf_op jit(solution)/shard_map/pallas_call | solution.py:593
  96.6 3.5 %all-to-all-start.11 = ((f32[16,8,128]{2,1,0:T(8,128)}), f32[16,8,128]{2,1,0:T(8,128)S(1)}, u32[]{:S(2)}, u32[]{:S(2)}) async-start(f32[16,8,128]{2,1,0:T(8,128)} %shard_map.125), calls=%async_computation.11 | async-start | bytes 131072 | tf_op jit(solution)/shard_map/all_to_all | solution.py:554
  100.1 0.6 slice.199
  101.4 5.3 %all-to-all-done.11 = f32[16,8,128]{2,1,0:T(8,128)S(1)} async-done(((f32[16,8,128]{2,1,0:T(8,128)}), f32[16,8,128]{2,1,0:T(8,128)S(1)}, u32[]{:S(2)}, u32[]{:S(2)}) %all-to-all-start.11) | async-done | bytes 65568 | tf_op jit(solution)/shard_map/all_to_all | solution.py:554
  106.7 0.0 copy-done.2
  106.7 0.0 copy-done.3
  106.7 0.0 copy-done.4
  106.7 0.0 copy-done.5
  106.7 1.0 conditional.1
  107.0 0.7 branch_1_fun.1
  (5 shorter events, 0.0 us)
Async XLA Ops:
  2.2 38.1 %all-to-all-start.8 = ((f32[16,56,128]{2,1,0:T(8,128)}), f32[16,56,128]{2,1,0:T(8,128)S(1)}, u32[]{:S(2)}, u32[]{:S(2)}) async-start(f32[16,56,128]{2,1,0:T(8,128)} %get-tuple-element.218), calls=%async_computation.8 | async-start | bytes 917504 | tf_op jit(solution)/shard_map/all_to_all | solution.py:554
  38.1 68.5 %copy-start = (f32[3,512]{1,0:T(4,128)S(1)}, f32[3,512]{1,0:T(4,128)}, u32[]{:S(2)}) copy-start(f32[3,512]{1,0:T(4,128)} %pos.1) | copy-start | bytes 18436
  38.1 68.5 %copy-start.1 = (f32[3,512]{1,0:T(4,128)S(1)}, f32[3,512]{1,0:T(4,128)}, u32[]{:S(2)}) copy-start(f32[3,512]{1,0:T(4,128)} %vel.1) | copy-start | bytes 18436
  38.2 68.5 %copy-start.2 = (f32[3,512]{1,0:T(4,128)S(1)}, f32[3,512]{1,0:T(4,128)}, u32[]{:S(2)}) copy-start(f32[3,512]{1,0:T(4,128)} %acc.1) | copy-start | bytes 18436
  38.2 68.5 %copy-start.3 = (f32[3,512]{1,0:T(4,128)S(1)}, f32[3,512]{1,0:T(4,128)}, u32[]{:S(2)}) copy-start(f32[3,512]{1,0:T(4,128)} %jerk.1) | copy-start | bytes 18436
  38.2 68.5 %copy-start.4 = (f32[512]{0:T(512)S(1)}, f32[512]{0:T(512)}, u32[]{:S(2)}) copy-start(f32[512]{0:T(512)} %param.22) | copy-start | bytes 6148
  38.2 68.5 %copy-start.5 = (s32[512]{0:T(512)S(1)}, s32[512]{0:T(512)}, u32[]{:S(2)}) copy-start(s32[512]{0:T(512)} %param.23) | copy-start | bytes 6148
  38.2 68.5 %copy-start.6 = (s32[256]{0:T(256)S(1)}, s32[256]{0:T(256)}, u32[]{:S(2)}) copy-start(s32[256]{0:T(256)} %param.24) | copy-start | bytes 3076
  38.2 68.5 %copy-start.7 = (s32[128]{0:T(128)S(1)}, s32[128]{0:T(128)}, u32[]{:S(2)}) copy-start(s32[128]{0:T(128)} %param.25) | copy-start | bytes 1540
  54.7 13.6 %all-to-all-start.9 = ((f32[16,8,256]{2,1,0:T(8,128)}), f32[16,8,256]{2,1,0:T(8,128)S(1)}, u32[]{:S(2)}, u32[]{:S(2)}) async-start(f32[16,8,256]{2,1,0:T(8,128)} %shard_map.122), calls=%async_computation.9 | async-start | bytes 262144 | tf_op jit(solution)/shard_map/all_to_all | solution.py:554
  69.1 20.8 %all-to-all-start.10 = ((f32[16,8,128]{2,1,0:T(8,128)}), f32[16,8,128]{2,1,0:T(8,128)S(1)}, u32[]{:S(2)}, u32[]{:S(2)}) async-start(f32[16,8,128]{2,1,0:T(8,128)} %get-tuple-element.222), calls=%async_computation.10 | async-start | bytes 131072 | tf_op jit(solution)/shard_map/all_to_all | solution.py:554
  96.6 10.1 %all-to-all-start.11 = ((f32[16,8,128]{2,1,0:T(8,128)}), f32[16,8,128]{2,1,0:T(8,128)S(1)}, u32[]{:S(2)}, u32[]{:S(2)}) async-start(f32[16,8,128]{2,1,0:T(8,128)} %shard_map.125), calls=%async_computation.11 | async-start | bytes 131072 | tf_op jit(solution)/shard_map/all_to_all | solution.py:554
